TPU v7x, 8 devices: a whole 2x2x1 slice. The times are simulated.
8 devices in a mesh: rep: 2 (over y, z), dp: 4 (over x, core).
Axes of the slice: x: 2, y: 2, z: 1, core: 2. Of those that a mesh axis runs over, the one named last changes fastest.
Arguments:
- x: bfloat16 [8, 2048, 1536], P(('rep', 'dp')), parts along dimension 0
- dy: bfloat16 [8, 2048, 1536], P(('rep', 'dp')), parts along dimension 0
- w_gate: bfloat16 [2, 1536, 3584], P(None, 'dp')
- w_up: bfloat16 [2, 1536, 3584], P(None, 'dp')
- w_down: bfloat16 [2, 3584, 1536], P(None, 'dp')
- m_w_gate: float32 [2, 1536, 3584], P(None, 'dp')
- m_w_up: float32 [2, 1536, 3584], P(None, 'dp')
- m_w_down: float32 [2, 3584, 1536], P(None, 'dp')
- v_w_gate: float32 [2, 1536, 3584], P(None, 'dp')
- v_w_up: float32 [2, 1536, 3584], P(None, 'dp')
- v_w_down: float32 [2, 3584, 1536], P(None, 'dp')
Outputs:
- output 1: bfloat16 [4, 1536, 3584], P('rep', 'dp'), parts along dimension 0
- output 2: bfloat16 [4, 1536, 3584], P('rep', 'dp'), parts along dimension 0
- output 3: bfloat16 [4, 3584, 1536], P('rep', 'dp'), parts along dimension 0
- output 4: float32 [4, 1536, 3584], P('rep', 'dp'), parts along dimension 0
- output 5: float32 [4, 1536, 3584], P('rep', 'dp'), parts along dimension 0
- output 6: float32 [4, 3584, 1536], P('rep', 'dp'), parts along dimension 0
- output 7: float32 [4, 1536, 3584], P('rep', 'dp'), parts along dimension 0
- output 8: float32 [4, 1536, 3584], P('rep', 'dp'), parts along dimension 0
- output 9: float32 [4, 3584, 1536], P('rep', 'dp'), parts along dimension 0
There are 2 independent parts. A program takes and returns all parts, laid end to end along the dimension named above; an argument that names none is the same for every part.
All inputs are finite; a program needn't handle non-finite values.
Results may differ from a plain program's by a relative error of at most 0.022.
Values are sent between devices in bfloat16 or wider.
A program may use at most 2 GiB of HBM per device.

v0:
```python
import jax
import jax.numpy as jnp
from jax import lax
from jax.sharding import PartitionSpec as P

NAMES = ("w_gate", "w_up", "w_down")


def matmul(a, w):
    return jnp.dot(a, w, preferred_element_type=jnp.float32).astype(jnp.bfloat16)


def normed(h):
    wide = h.astype(jnp.float32)
    scale = lax.rsqrt(jnp.mean(wide**2, -1, keepdims=True) + 1e-6)
    return (wide * scale).astype(jnp.bfloat16)


def layer(h, w):
    a = normed(h)
    gate = jnp.dot(a, w["w_gate"], preferred_element_type=jnp.float32)
    up = jnp.dot(a, w["w_up"], preferred_element_type=jnp.float32)
    return h + matmul((jax.nn.silu(gate) * up).astype(jnp.bfloat16), w["w_down"])


def adamw(w, m, v, g):
    m = 0.9 * m + 0.1 * g
    v = 0.95 * v + 0.05 * g * g
    step = m * lax.rsqrt(v + 1e-8) + 0.1 * w
    return (w - 0.02 * step).astype(jnp.bfloat16), m, v


def clipped(gradients, sum_of_squares, count):
    factor = jnp.minimum(1.0, 0.5 * lax.rsqrt(sum_of_squares / count + 1e-30))
    return [g * factor for g in gradients]


def solution(mesh):
    def fetched(weights, number):
        return {name: lax.all_gather(w[number], "dp", axis=0, tiled=True) for name, w in zip(NAMES, weights, strict=True)}

    def step(x, dy, *arrays):
        weights, m, v = (arrays[i : i + 3] for i in (0, 3, 6))
        layers = weights[0].shape[0]
        h, kept = x[0], []
        for number in range(layers):
            kept.append(h)
            h = layer(h, fetched(weights, number))
        by_h, mine = dy[0], [None] * layers
        for number in reversed(range(layers)):
            _, back = jax.vjp(lambda w, h: layer(h, w), fetched(weights, number), kept[number])
            by_w, by_h = back(by_h)
            mine[number] = [lax.psum_scatter(by_w[name], "dp", scatter_dimension=0, tiled=True) for name in NAMES]
        gradients = [jnp.stack([mine[number][i] for number in range(layers)]).astype(jnp.float32) for i in range(3)]
        squares = lax.psum(sum(jnp.sum(g * g) for g in gradients), "dp")
        gradients = clipped(gradients, squares, lax.psum(1, "dp") * sum(g.size for g in gradients))
        new = [adamw(w.astype(jnp.float32), m, v, g) for w, m, v, g in zip(weights, m, v, gradients, strict=True)]
        return tuple(one[which] for which in range(3) for one in new)

    states, cut = P(("rep", "dp"), None, None), P(None, "dp", None)
    return jax.shard_map(
        step,
        mesh=mesh,
        in_specs=(states, states) + (cut,) * 9,
        out_specs=(P("rep", "dp", None),) * 9,
        check_vma=False,
    )
```

profile of v0, /device:TPU:0, one launch (start us, length us, event | category | flops | bytes accessed | tf_op | source)
XLA Modules:
  0.0 1189.5 jit_solution(7525896813173820642)
XLA Ops:
  46.8 39.7 %all-gather.13.cloned.1.call-done = bf16[1,1536,3584]{2,1,0:T(8,128)(2,1)} async-done(((bf16[1,384,3584]{2,1,0:T(8,128)(2,1)}), bf16[1,1536,3584]{2,1,0:T(8,128)(2,1)}) %all-gather.13.cloned.1.call-update) | async-done | bytes 11010064 | tf_op jit(solution)/shard_map/all_gather | solution.py:40
  86.5 31.4 %fusion.60 = f32[2048,3584]{1,0:T(8,128)} fusion(bf16[1,1536,3584]{2,1,0:T(8,128)(2,1)} %all-gather.13.cloned.1.call-done, bf16[1,2048,1536]{1,2,0:T(8,128)(2,1)} %copy.20, f32[2048]{0:T(1024)S(1)} %add_rsqrt_fusion), kind=kOutput, calls=%fused_computation.94 | convolution fusion | flops 22558015488 | bytes 46669824 | tf_op jit(solution)/shard_map/dot_general | solution.py:21
  117.9 41.6 %all-gather.15.cloned.1.call-done = bf16[1,1536,3584]{2,1,0:T(8,128)(2,1)} async-done(((bf16[1,384,3584]{2,1,0:T(8,128)(2,1)}), bf16[1,1536,3584]{2,1,0:T(8,128)(2,1)}) %all-gather.15.cloned.1.call-update) | async-done | bytes 11010064 | tf_op jit(solution)/shard_map/all_gather | solution.py:40
  159.5 39.6 %multiply_convert_fusion.1 = (bf16[2048,3584]{1,0:T(8,128)(2,1)}, f32[2048,3584]{1,0:T(8,128)}) fusion(f32[2048,3584]{1,0:T(8,128)} %fusion.60, bf16[1,1536,3584]{2,1,0:T(8,128)(2,1)} %all-gather.15.cloned.1.call-done, bf16[1,2048,1536]{1,2,0:T(8,128)(2,1)} %copy.20, f32[2048]{0:T(1024)S(1)} %add_rsqrt_fusion), kind=kOutput, calls=%fused_computation.17 | convolution fusion | flops 22602055680 | bytes 90710016 | tf_op jit(solution)/shard_map/dot_general | solution.py:22
  199.1 33.4 %all-gather.17.cloned.1.call-done = bf16[1,3584,1536]{2,1,0:T(8,128)(2,1)} async-done(((bf16[1,896,1536]{2,1,0:T(8,128)(2,1)}), bf16[1,3584,1536]{2,1,0:T(8,128)(2,1)}) %all-gather.17.cloned.1.call-update) | async-done | bytes 11010064 | tf_op jit(solution)/shard_map/all_gather | solution.py:40
  232.5 32.0 %fusion.26 = (f32[2048]{0:T(1024)S(1)}, bf16[2048,1536]{0,1:T(8,128)(2,1)}) fusion(bf16[2048,3584]{1,0:T(8,128)(2,1)} %get-tuple-element.24, bf16[1,3584,1536]{2,1,0:T(8,128)(2,1)} %all-gather.17.cloned.1.call-done, bf16[1,2048,1536]{1,2,0:T(8,128)(2,1)} %copy.20), kind=kOutput, calls=%fused_computation.60 | convolution fusion | flops 22564304896 | bytes 38281216 | tf_op jit(solution)/shard_map/dot_general | solution.py:10
  264.5 40.8 %all-gather.21.cloned.1.call-done = bf16[1,3584,1536]{2,1,0:T(8,128)(2,1)} async-done(((bf16[1,896,1536]{2,1,0:T(8,128)(2,1)}), bf16[1,3584,1536]{2,1,0:T(8,128)(2,1)}) %all-gather.21.cloned.1.call-update) | async-done | bytes 11010064 | tf_op jit(solution)/shard_map/all_gather | solution.py:40
  335.3 42.9 %all-gather.23.cloned.1.call-done = bf16[1,1536,3584]{2,1,0:T(8,128)(2,1)} async-done(((bf16[1,384,3584]{2,1,0:T(8,128)(2,1)}), bf16[1,1536,3584]{2,1,0:T(8,128)(2,1)}) %all-gather.23.cloned.1.call-update) | async-done | bytes 11010064 | tf_op jit(solution)/shard_map/all_gather | solution.py:40
  378.2 31.6 %fusion.47 = f32[2048,3584]{1,0:T(8,128)} fusion(bf16[1,1536,3584]{2,1,0:T(8,128)(2,1)} %all-gather.23.cloned.1.call-done, bf16[2048,1536]{0,1:T(8,128)(2,1)} %get-tuple-element.27, f32[2048]{0:T(1024)S(1)} %fusion.88), kind=kOutput, calls=%fused_computation.81 | convolution fusion | flops 22558015488 | bytes 46669824 | tf_op jit(solution)/shard_map/jvp()/dot_general | solution.py:22
  409.8 41.3 %all-gather.19.cloned.1.call-done = bf16[1,1536,3584]{2,1,0:T(8,128)(2,1)} async-done(((bf16[1,384,3584]{2,1,0:T(8,128)(2,1)}), bf16[1,1536,3584]{2,1,0:T(8,128)(2,1)}) %all-gather.19.cloned.1.call-update) | async-done | bytes 11010064 | tf_op jit(solution)/shard_map/all_gather | solution.py:40
  451.1 47.9 %fusion.2 = (bf16[2048,3584]{1,0:T(8,128)(2,1)}, f32[2048,3584]{1,0:T(8,128)}) fusion(f32[2048,3584]{1,0:T(8,128)} %fusion.47, bf16[2048,3584]{1,0:T(8,128)(2,1)} %convolution_convert_fusion.4, bf16[1,1536,3584]{2,1,0:T(8,128)(2,1)} %all-gather.19.cloned.1.call-done, bf16[2048,1536]{0,1:T(8,128)(2,1)} %get-tuple-element.27, f32[2048]{0:T(1024)S(1)} %fusion.88), kind=kOutput, calls=%fused_computation.8 | convolution fusion | flops 22646095872 | bytes 105390080 | tf_op jit(solution)/shard_map/jvp()/dot_general | solution.py:21
  499.0 30.3 %fusion.65 = bf16[2048,1536]{0,1:T(8,128)(2,1)} fusion(bf16[2048,3584]{1,0:T(8,128)(2,1)} %get-tuple-element.28, bf16[1,1536,3584]{2,1,0:T(8,128)(2,1)} %all-gather.19.cloned.1.call-done), kind=kOutput, calls=%fused_computation.97 | convolution fusion | flops 22548578304 | bytes 31981568 | tf_op jit(solution)/shard_map/transpose(jvp())/dot_general | solution.py:21
  529.3 37.8 %fusion.28 = (f32[2048]{0:T(1024)S(1)}, bf16[2048,1536]{0,1:T(8,128)(2,1)}) fusion(bf16[2048,1536]{0,1:T(8,128)(2,1)} %get-tuple-element.27, bf16[2048,1536]{0,1:T(8,128)(2,1)} %fusion.65, bf16[1,1536,3584]{2,1,0:T(8,128)(2,1)} %all-gather.23.cloned.1.call-done, bf16[2048,3584]{1,0:T(8,128)(2,1)} %convolution_convert_fusion.4, ...), kind=kOutput, calls=%fused_computation.62 | convolution fusion | flops 22611490816 | bytes 73932800 | tf_op jit(solution)/shard_map/transpose(jvp())/dot_general | solution.py:22
  606.2 33.6 %convolution_convert_fusion.1 = bf16[3584,1536]{1,0:T(8,128)(2,1)} fusion(f32[2048,3584]{1,0:T(8,128)} %fusion.47, bf16[1,2048,1536]{2,1,0:T(8,128)(2,1)} %param.12, f32[2048,3584]{1,0:T(8,128)} %get-tuple-element.29), kind=kOutput, calls=%fused_computation.34 | convolution fusion | flops 22598123520 | bytes 76021760 | tf_op jit(solution)/shard_map/transpose(jvp())/dot_general | solution.py:10
  639.9 30.2 %convolution_convert_fusion.3 = bf16[2048,3584]{1,0:T(8,128)(2,1)} fusion(bf16[2048,1536]{0,1:T(8,128)(2,1)} %copy-done.1, bf16[1,3584,1536]{2,1,0:T(8,128)(2,1)} %all-gather.17.cloned.1.call-done), kind=kOutput, calls=%fused_computation.38 | convolution fusion | flops 22555918336 | bytes 31981568 | tf_op jit(solution)/shard_map/transpose(jvp())/dot_general | solution.py:10
  670.1 35.2 %fusion.17 = bf16[1536,3584]{1,0:T(8,128)(2,1)} fusion(bf16[2048,3584]{1,0:T(8,128)(2,1)} %convolution_convert_fusion.3, f32[2048,3584]{1,0:T(8,128)} %fusion.60, bf16[1,2048,1536]{1,2,0:T(8,128)(2,1)} %copy.20, f32[2048]{0:T(1024)S(1)} %copy-done.7), kind=kOutput, calls=%fused_computation.37 | convolution fusion | flops 22607560704 | bytes 61349888 | tf_op jit(solution)/shard_map/transpose(jvp())/dot_general | solution.py:22
  706.0 35.2 %fusion.16 = bf16[1536,3584]{1,0:T(8,128)(2,1)} fusion(bf16[2048,3584]{1,0:T(8,128)(2,1)} %convolution_convert_fusion.4, bf16[2048,1536]{0,1:T(8,128)(2,1)} %get-tuple-element.27, f32[2048]{0:T(1024)S(1)} %copy-done.3, f32[2048,3584]{1,0:T(8,128)} %get-tuple-element.29), kind=kOutput, calls=%fused_computation.36 | convolution fusion | flops 22607560704 | bytes 61349888 | tf_op jit(solution)/shard_map/transpose(jvp())/dot_general | solution.py:22
  741.2 39.5 %fusion.13 = bf16[1536,3584]{1,0:T(8,128)(2,1)} fusion(f32[2048,3584]{1,0:T(8,128)} %fusion.60, f32[2048,3584]{1,0:T(8,128)} %get-tuple-element.25, bf16[2048,3584]{1,0:T(8,128)(2,1)} %convolution_convert_fusion.3, bf16[1,2048,1536]{1,2,0:T(8,128)(2,1)} %copy.20, f32[2048]{0:T(1024)S(1)} %copy-done.7), kind=kOutput, calls=%fused_computation.32 | convolution fusion | flops 22644260864 | bytes 90710016 | tf_op jit(solution)/shard_map/transpose(jvp())/dot_general | solution.py:21
  780.8 30.9 %convolution_convert_fusion = bf16[1536,3584]{1,0:T(8,128)(2,1)} fusion(bf16[2048,3584]{1,0:T(8,128)(2,1)} %get-tuple-element.28, bf16[2048,1536]{0,1:T(8,128)(2,1)} %get-tuple-element.27, f32[2048]{0:T(1024)S(1)} %copy-done.3), kind=kOutput, calls=%fused_computation.33 | convolution fusion | flops 22558015488 | bytes 31989760 | tf_op jit(solution)/shard_map/transpose(jvp())/dot_general | solution.py:21
  817.9 37.9 %reduce-scatter.11.cloned.1.call-done = bf16[384,3584]{1,0:T(8,128)(2,1)} async-done(((bf16[1536,3584]{1,0:T(8,128)(2,1)}), bf16[384,3584]{1,0:T(8,128)(2,1)}) %reduce-scatter.11.cloned.1.call-update) | async-done | bytes 2752528 | tf_op jit(solution)/shard_map/reduce_scatter | solution.py:53
  855.8 84.1 %reduce-scatter.13.cloned.1.call-done = bf16[384,3584]{1,0:T(8,128)(2,1)} async-done(((bf16[1536,3584]{1,0:T(8,128)(2,1)}), bf16[384,3584]{1,0:T(8,128)(2,1)}) %reduce-scatter.13.cloned.1.call-update) | async-done | bytes 2752528 | tf_op jit(solution)/shard_map/reduce_scatter | solution.py:53
  945.9 78.2 %reduce-scatter.7.cloned.1.call-done = bf16[384,3584]{1,0:T(8,128)(2,1)} async-done(((bf16[1536,3584]{1,0:T(8,128)(2,1)}), bf16[384,3584]{1,0:T(8,128)(2,1)}) %reduce-scatter.7.cloned.1.call-update) | async-done | bytes 2752528 | tf_op jit(solution)/shard_map/reduce_scatter | solution.py:53
  1024.1 84.1 %reduce-scatter.9.cloned.1.call-done = bf16[384,3584]{1,0:T(8,128)(2,1)} async-done(((bf16[1536,3584]{1,0:T(8,128)(2,1)}), bf16[384,3584]{1,0:T(8,128)(2,1)}) %reduce-scatter.9.cloned.1.call-update) | async-done | bytes 2752528 | tf_op jit(solution)/shard_map/reduce_scatter | solution.py:53
  1145.5 37.0 %fusion.34 = (bf16[2,384,3584]{2,1,0:T(8,128)(2,1)}, f32[2,384,3584]{2,1,0:T(8,128)}, f32[2,384,3584]{2,1,0:T(8,128)}, bf16[2,384,3584]{2,1,0:T(8,128)(2,1)}, f3...) fusion(bf16[2,384,3584]{2,1,0:T(8,128)(2,1)} %param.13, f32[]{:T(128)S(6)} %min_shard_map.3, ...), kind=kLoop, calls=%fused_computation.68 | loop fusion | flops 110100480 | bytes 121110528 | tf_op jit(solution)/shard_map/convert_element_type | solution.py:30
  (59 shorter events, 156.3 us)
Async XLA Ops:
  7.2 79.3 %all-gather.13.cloned.1.call-start = ((), (), s32[]{:S(2)}) async-start(), calls=%async_computation.12 | async-start | bytes 13762560 | tf_op jit(solution)/shard_map/all_gather | solution.py:40
  12.7 146.9 %all-gather.15.cloned.1.call-start = ((), (), s32[]{:S(2)}) async-start(), calls=%async_computation.13 | async-start | bytes 13762560 | tf_op jit(solution)/shard_map/all_gather | solution.py:40
  18.1 214.4 %all-gather.17.cloned.1.call-start = ((), (), s32[]{:S(2)}) async-start(), calls=%async_computation.14 | async-start | bytes 13762560 | tf_op jit(solution)/shard_map/all_gather | solution.py:40
  23.6 281.7 %all-gather.21.cloned.1.call-start = ((), (), s32[]{:S(2)}) async-start(), calls=%async_computation.16 | async-start | bytes 13762560 | tf_op jit(solution)/shard_map/all_gather | solution.py:40
  24.2 354.0 %all-gather.23.cloned.1.call-start = ((), (), s32[]{:S(2)}) async-start(), calls=%async_computation.17 | async-start | bytes 13762560 | tf_op jit(solution)/shard_map/all_gather | solution.py:40
  24.8 426.3 %all-gather.19.cloned.1.call-start = ((), (), s32[]{:S(2)}) async-start(), calls=%async_computation.15 | async-start | bytes 13762560 | tf_op jit(solution)/shard_map/all_gather | solution.py:40
  25.4 786.4 %reduce-scatter.15.cloned.1.call-start = ((), (), s32[]{:S(2)}) async-start(), calls=%async_computation.10 | async-start | bytes 13762560 | tf_op jit(solution)/shard_map/reduce_scatter | solution.py:53
  38.1 121.4 %copy-start.6 = (f32[2048]{0:T(1024)}, f32[2048]{0:T(1024)S(1)}, u32[]{:S(2)}) copy-start(f32[2048]{0:T(1024)S(1)} %add_rsqrt_fusion) | copy-start | bytes 24580
  264.5 70.8 %copy-start.4 = (f32[2048]{0:T(1024)}, f32[2048]{0:T(1024)S(1)}, u32[]{:S(2)}) copy-start(f32[2048]{0:T(1024)S(1)} %get-tuple-element.26) | copy-start | bytes 24580
  264.5 302.6 %copy-start.2 = (f32[2048]{0:T(1024)}, f32[2048]{0:T(1024)S(1)}, u32[]{:S(2)}) copy-start(f32[2048]{0:T(1024)S(1)} %fusion.88) | copy-start | bytes 24580
  529.3 37.8 %copy-start.5 = (f32[2048]{0:T(1024)S(1)}, f32[2048]{0:T(1024)}, u32[]{:S(2)}) copy-start(f32[2048]{0:T(1024)} %copy-done.4) | copy-start | bytes 24580
  575.9 2.7 copy-start.1
  606.2 205.6 %reduce-scatter.17.cloned.1.call-start = ((), (), s32[]{:S(2)}) async-start(), calls=%async_computation.11 | async-start | bytes 13762560 | tf_op jit(solution)/shard_map/reduce_scatter | solution.py:53
  639.9 30.2 %copy-start.7 = (f32[2048]{0:T(1024)S(1)}, f32[2048]{0:T(1024)}, u32[]{:S(2)}) copy-start(f32[2048]{0:T(1024)} %copy-done.6) | copy-start | bytes 24580
  639.9 215.9 %reduce-scatter.11.cloned.1.call-start = ((), (), s32[]{:S(2)}) async-start(), calls=%async_computation.8 | async-start | bytes 13762560 | tf_op jit(solution)/shard_map/reduce_scatter | solution.py:53
  705.3 0.7 copy-start.3
  705.3 234.6 %reduce-scatter.13.cloned.1.call-start = ((), (), s32[]{:S(2)}) async-start(), calls=%async_computation.9 | async-start | bytes 13762560 | tf_op jit(solution)/shard_map/reduce_scatter | solution.py:53
  741.2 282.9 %reduce-scatter.7.cloned.1.call-start = ((), (), s32[]{:S(2)}) async-start(), calls=%async_computation.6 | async-start | bytes 13762560 | tf_op jit(solution)/shard_map/reduce_scatter | solution.py:53
  780.8 327.4 %reduce-scatter.9.cloned.1.call-start = ((), (), s32[]{:S(2)}) async-start(), calls=%async_computation.7 | async-start | bytes 13762560 | tf_op jit(solution)/shard_map/reduce_scatter | solution.py:53
  1123.3 22.2 %copy-start = (bf16[384,3584]{1,0:T(8,128)(2,1)S(1)}, bf16[384,3584]{1,0:T(8,128)(2,1)}, u32[]{:S(2)}) copy-start(bf16[384,3584]{1,0:T(8,128)(2,1)} %reduce-scatter.11.cloned.1.call-done) | copy-start | bytes 8257540
Sparse Core Ops, SparseCore 0:
  12.8 73.6 all-gather.12
  88.6 70.8 all-gather.14
  161.6 70.8 all-gather.16
  234.5 70.8 all-gather.20
  307.3 70.8 all-gather.22
  380.2 70.8 all-gather.18
  606.3 81.0 reduce-scatter.14
  690.5 81.0 reduce-scatter.16
  774.7 81.0 reduce-scatter.10
  858.8 81.0 reduce-scatter.12
  943.0 81.0 reduce-scatter.6
  1027.1 81.0 reduce-scatter.8
where the time goes:
time: 1200 us; the launch traced here: 1190 us
  waiting for transfers between devices  526 us (44%)
  matrix products  513 us (43%)
  other arithmetic  90.2 us (8%)
  local copies, waits for them, and re-layouts  36.8 us (3%)
  between operations  17.1 us (1%)
    reduce_scatter x6, waiting for transfers between devices, step(): lax.psum_scatter(by_w[name], 'dp', scatter_dimension=0, tiled=True)  284 us
    all_gather x6, waiting for transfers between devices, fetched(): lax.all_gather(w[number], 'dp', axis=0, tiled=True)  240 us
    dot_general x5, matrix products, layer(): gate = jnp.dot(a, w['w_gate'], preferred_element_type=jnp.float32)  180 us
    dot_general x5, matrix products, layer(): up = jnp.dot(a, w['w_up'], preferred_element_type=jnp.float32)  179 us
    dot_general x5, matrix products, matmul(): jnp.dot(a, w, preferred_element_type=jnp.float32).astype(jnp.bfloat16)  153 us
    convert_element_type x2, other arithmetic, adamw(): return ((w - 0.02 * step).astype(jnp.bfloat16), m, v)  59.2 us
  transfers between devices with their start and end apart: 12, of which 10 were waited for; matrix products, arithmetic and copies ran while one was open for 35% of the time, Pallas kernels for 0%

commit v1 on v0

v1 whole, which is shorter than its diff:
```python
import functools

import jax
import jax.numpy as jnp
from jax import lax
from jax.experimental import pallas as pl
from jax.experimental.pallas import tpu as pltpu
from jax.sharding import PartitionSpec as P


F32, BF16 = jnp.float32, jnp.bfloat16
OVER_X = [(0, 2), (2, 0), (1, 3), (3, 1)]
OVER_CORE = [(0, 1), (1, 0), (2, 3), (3, 2)]
OVER_Y = [(0, 1), (1, 0)]


def normed(h):
    wide = h.astype(F32)
    scale = lax.rsqrt(jnp.mean(wide**2, -1, keepdims=True) + 1e-6)
    return (wide * scale).astype(BF16)


def activated(gate, up):
    return (jax.nn.silu(gate) * up).astype(BF16)


def dot(a, b, dims):
    return lax.dot_general(a, b, (dims, ((), ())), preferred_element_type=F32)


def adamw(w, m, v, g):
    m = 0.9 * m + 0.1 * g
    v = 0.95 * v + 0.05 * g * g
    step = m * lax.rsqrt(v + 1e-8) + 0.1 * w
    return (w - 0.02 * step).astype(BF16), m, v


def others(d):
    x, c = d // 2, d % 2
    return d, 2 * x + 1 - c, 2 * (1 - x) + c, 2 * (1 - x) + 1 - c


def assemble_kernel(number, rows, own, own_c, rx, ry, rx_c, ry_c, out, buf, sem_in, sem_out):
    d, r = lax.axis_index("dp"), lax.axis_index("rep")
    half = rows // 2
    own_i, core_i, x_i, xc_i = others(d)
    at = lambda i, n: pl.ds(pl.multiple_of(i, 16), n)
    moves = [
        (own.at[number], own_i * rows, rows),
        (own_c.at[number], core_i * rows, rows),
        (rx, x_i * rows + r * half, half),
        (ry, x_i * rows + (1 - r) * half, half),
        (rx_c, xc_i * rows + r * half, half),
        (ry_c, xc_i * rows + (1 - r) * half, half),
    ]
    ins = [pltpu.make_async_copy(src, buf.at[at(i, n)], sem_in.at[k]) for k, (src, i, n) in enumerate(moves)]
    outs = [pltpu.make_async_copy(buf.at[at(i, n)], out.at[at(i, n)], sem_out.at[k]) for k, (src, i, n) in enumerate(moves)]
    for one in ins:
        one.start()
    for one, two in zip(ins, outs):
        one.wait()
        two.start()
    for one in outs:
        one.wait()


def assembled(number, own, own_c, rx, ry, rx_c, ry_c):
    _, rows, cols = own.shape
    any_space = pl.BlockSpec(memory_space=pl.ANY)
    return pl.pallas_call(
        functools.partial(assemble_kernel, number, rows),
        out_shape=jax.ShapeDtypeStruct((4 * rows, cols), BF16),
        in_specs=[any_space] * 6,
        out_specs=any_space,
        scratch_shapes=[pltpu.VMEM((4 * rows, cols), BF16), pltpu.SemaphoreType.DMA((6,)), pltpu.SemaphoreType.DMA((6,))],
        compiler_params=pltpu.CompilerParams(vmem_limit_bytes=24 << 20),
        cost_estimate=pl.CostEstimate(flops=10**9, bytes_accessed=8 * 4 * rows * cols, transcendentals=0),
        name="assemble",
    )(own, own_c, rx, ry, rx_c, ry_c)


def solution(mesh):
    def step(x, dy, *arrays):
        weights, m, v = (arrays[i : i + 3] for i in (0, 3, 6))
        d, r = lax.axis_index("dp"), lax.axis_index("rep")
        own_i, core_i, x_i, xc_i = others(d)
        layers = weights[0].shape[0]

        from_core = [lax.ppermute(w, "dp", OVER_CORE) for w in weights]

        def across(i, number):
            rows, cols = weights[i].shape[1:]
            half = rows // 2
            mine = lax.dynamic_slice(weights[i], (number, r * half, 0), (1, half, cols))[0]
            return lax.ppermute(mine, "dp", OVER_X)

        halves = {(i, number): across(i, number) for number in range(layers) for i in range(3)}

        def fetched(i, number, *behind):
            rx = halves[i, number]
            if behind:
                rx = lax.optimization_barrier((rx, *behind))[0]
            ry = lax.ppermute(rx, "rep", OVER_Y)
            rx_c = lax.ppermute(rx, "dp", OVER_CORE)
            ry_c = lax.ppermute(ry, "dp", OVER_CORE)
            return assembled(number, weights[i], from_core[i], rx, ry, rx_c, ry_c)

        last = []

        def ordered(*some):
            out = lax.optimization_barrier((*some, *last))[: len(some)] if last else some
            return out[0] if len(some) == 1 else out

        def noted(one):
            last[:] = [one]
            return one

        token = ((0,), (0,))

        def term(left, right, i, arrived=None, kind=BF16):
            rows = left.shape[1] // 4
            left = ordered(lax.dynamic_slice(left, (0, i * rows), (left.shape[0], rows)))
            out = dot(left, right, token)
            if arrived is not None:
                out = out + arrived.astype(F32)
            return out.astype(kind)

        kept, full = [], []
        h = x[0]
        for number in range(layers):
            a, back_norm = jax.vjp(normed, h)
            if number == 0:
                w_gate, w_up = fetched(0, 0), fetched(1, 0)
            gate = dot(a, w_gate, ((1,), (0,)))
            if number == 0:
                w_down = fetched(2, 0, gate)
            else:
                w_down = fetched(2, 1, gate)
            up = dot(ordered(a, gate)[0], w_up, ((1,), (0,)))
            hidden, back_act = jax.vjp(activated, gate, up)
            kept.append((a, back_norm, hidden, back_act))
            full.append((w_gate, w_up, w_down))
            if number == 0:
                w_gate = fetched(0, 1, hidden)
                h = h + dot(hidden, w_down, ((1,), (0,))).astype(BF16)
                w_up = fetched(1, 1, h)
        noted(hidden)

        by_h, mine, late = dy[0], [[None] * 3 for _ in range(layers)], []
        for number in reversed(range(layers)):
            w_gate, w_up, w_down = full[number]
            a, back_norm, hidden, back_act = kept[number]

            def start(i, left, right, number=number):
                a_mine = noted(term(left, right, xc_i))
                a_there = lax.ppermute(a_mine, "dp", OVER_CORE)
                b_mine = noted(term(left, right, core_i))
                b_there = lax.ppermute(b_mine, "dp", OVER_CORE)
                sent = noted(term(left, right, x_i, a_there))
                from_x = lax.ppermute(sent, "dp", OVER_X)
                late.append((i, number, from_x, lambda: noted(term(left, right, own_i, b_there, F32))))

            start(2, hidden, by_h)
            by_here = ordered(by_h)
            by_hidden = dot(by_here, w_down, ((1,), (1,))).astype(BF16)
            by_gate, by_up = (noted(t.astype(BF16)) for t in back_act(by_hidden))
            start(0, a, by_gate)
            start(1, a, by_up)
            if number > 0:
                by_a = noted(dot(ordered(by_gate), w_gate, ((1,), (1,))).astype(BF16))
                by_a = by_a + dot(ordered(by_up), w_up, ((1,), (1,))).astype(BF16)
                by_h = noted(by_h + back_norm(by_a)[0])
        owns = lax.optimization_barrier([own() for _, _, _, own in late])
        for (i, number, from_x, _), own in zip(late, owns):
            mine[number][i] = (own + from_x.astype(F32)).astype(BF16)

        squares = sum(jnp.sum(jnp.square(g.astype(F32))) for gs in mine for g in gs)
        squares = lax.psum(squares, "dp")
        count = 4 * sum(g.size for gs in mine for g in gs)
        factor = jnp.minimum(1.0, 0.5 * lax.rsqrt(squares / count + 1e-30))
        new = []
        for i in range(3):
            g = jnp.stack([mine[number][i] for number in range(layers)]).astype(F32) * factor
            new.append(adamw(weights[i].astype(F32), m[i], v[i], g))
        return tuple(one[which] for which in range(3) for one in new)

    states, cut = P(("rep", "dp"), None, None), P(None, "dp", None)
    return jax.shard_map(
        step,
        mesh=mesh,
        in_specs=(states, states) + (cut,) * 9,
        out_specs=(P("rep", "dp", None),) * 9,
        check_vma=False,
    )
```

time: 1200 us -> 1170 us (0.975)
  waiting for transfers between devices: 526 us -> 344 us
  matrix products: 513 us -> 558 us
  local copies, waits for them, and re-layouts: 36.8 us -> 81.7 us
  other arithmetic: 90.2 us -> 121 us
  starting transfers between devices: 0.49 us -> 25.7 us
  Pallas kernels: 0 us -> 22.7 us
    ppermute x0 -> x45, waiting for transfers between devices: none -> 344 us  [the longest x6 236 us: start(): from_x = lax.ppermute(sent, 'dp', OVER_X)]
    reduce_scatter x6 -> x0, waiting for transfers between devices: 284 us -> none  [step(): lax.psum_scatter(by_w[name], 'dp', scatter_dimension=0, tiled=True)]
    all_gather x6 -> x0, waiting for transfers between devices: 240 us -> none  [fetched(): lax.all_gather(w[number], 'dp', axis=0, tiled=True)]
    dot_general x15 -> x33, matrix products: 513 us -> 558 us  [dot(): return lax.dot_general(a, b, (dims, ((), ())), preferred_element_type=F32)]
    unnamed x18 -> x132, local copies, waits for them, and re-layouts: 20.6 us -> 48.2 us
    another operation x0 -> x5, other arithmetic: none -> 26.4 us  [step(): jnp.stack([mine[number][i] for number in range(layers)]).astype(F32)]
    ppermute x0 -> x45, starting transfers between devices: none -> 25.7 us  [the longest x6 6.97 us: fetched(): ry = lax.ppermute(rx, 'rep', OVER_Y)]
    dynamic_slice x0 -> x4, local copies, waits for them, and re-layouts: none -> 24 us  [term(): lax.dynamic_slice(left, (0, i * rows), (left.shape[0], rows))]
  transfers between devices with their start and end apart: 12 -> 45, of which waited for: 10 -> 10; matrix products, arithmetic and copies ran while one was open for 35% -> 34% of each run, Pallas kernels for 0% -> 2%
where the time goes in v1:
time: 1170 us
  matrix products  558 us (48%)
  waiting for transfers between devices  344 us (29%)
  other arithmetic  121 us (10%)
  local copies, waits for them, and re-layouts  81.7 us (7%)
  starting transfers between devices  25.7 us (2%)
  Pallas kernels  22.7 us (2%)
    dot_general x33, matrix products, dot(): return lax.dot_general(a, b, (dims, ((), ())), preferred_element_type=F32)  558 us
    ppermute x6, waiting for transfers between devices, start(): from_x = lax.ppermute(sent, 'dp', OVER_X)  236 us
    ppermute x6, waiting for transfers between devices, fetched(): ry = lax.ppermute(rx, 'rep', OVER_Y)  65.2 us
    convert_element_type x3, other arithmetic, adamw(): return ((w - 0.02 * step).astype(BF16), m, v)  64.8 us
    unnamed x132, local copies, waits for them, and re-layouts  48.2 us
    ppermute x6, waiting for transfers between devices, across(): return lax.ppermute(mine, 'dp', OVER_X)  41.9 us
    another operation x5, other arithmetic, step(): jnp.stack([mine[number][i] for number in range(layers)]).astype(F32)  26.4 us
    dynamic_slice x4, local copies, waits for them, and re-layouts, term(): lax.dynamic_slice(left, (0, i * rows), (left.shape[0], rows))  24 us
  transfers between devices with their start and end apart: 45, of which 10 were waited for; matrix products, arithmetic and copies ran while one was open for 34% of the time, Pallas kernels for 2%

profile of v1, /device:TPU:0, one launch (start us, length us, event | category | flops | bytes accessed | tf_op | source)
XLA Modules:
  0.0 1166.4 jit_solution(3984245407647007574)
XLA Ops:
  10.0 28.0 %collective-permute-done.1.rx = bf16[192,3584]{1,0:T(8,128)(2,1)S(1)} collective-permute-done((bf16[192,3584]{1,0:T(8,128)(2,1)S(1)}, bf16[192,3584]{1,0:T(8,128)(2,1)S(1)}, u32[]{:S(2)}, u32[]{:S(2)}) %collective-permute-start.1) | collective-permute-done | bytes 1376288 | tf_op jit(solution)/shard_map/ppermute | solution.py:95
  53.5 13.9 %collective-permute-done.6.rx = bf16[192,3584]{1,0:T(8,128)(2,1)} collective-permute-done((bf16[192,3584]{1,0:T(8,128)(2,1)S(1)}, bf16[192,3584]{1,0:T(8,128)(2,1)}, u32[]{:S(2)}, u32[]{:S(2)}) %collective-permute-start.6) | collective-permute-done | bytes 1376288 | tf_op jit(solution)/shard_map/ppermute | solution.py:95
  78.6 21.0 %collective-permute-done.7.ry = bf16[192,3584]{1,0:T(8,128)(2,1)S(1)} collective-permute-done((bf16[192,3584]{1,0:T(8,128)(2,1)}, bf16[192,3584]{1,0:T(8,128)(2,1)S(1)}, u32[]{:S(2)}, u32[]{:S(2)}) %collective-permute-start.7) | collective-permute-done | bytes 1376288 | tf_op jit(solution)/shard_map/ppermute | solution.py:103
  108.9 28.3 %fusion.56 = f32[2048,3584]{1,0:T(8,128)} fusion(bf16[2048,1536]{0,1:T(8,128)(2,1)} %fusion.11, bf16[1536,3584]{1,0:T(8,128)(2,1)S(1)} %assemble.6), kind=kOutput, calls=%fused_computation.148 | convolution fusion | flops 22548578304 | bytes 46661632 | tf_op jit(solution)/shard_map/dot_general | solution.py:28
  147.6 39.6 %multiply_convert_fusion.1 = (bf16[2048,3584]{1,0:T(8,128)(2,1)}, f32[2048,3584]{1,0:T(8,128)}) fusion(f32[2048,3584]{1,0:T(8,128)} %fusion.56, bf16[2048,1536]{0,1:T(8,128)(2,1)} %fusion.11, bf16[1536,3584]{1,0:T(8,128)(2,1)} %copy-done.7), kind=kOutput, calls=%fused_computation.17 | convolution fusion | flops 22592618496 | bytes 90701824 | tf_op jit(solution)/shard_map/dot_general | solution.py:28
  189.8 30.0 %collective-permute-done.16.ry = bf16[192,3584]{1,0:T(8,128)(2,1)} collective-permute-done((bf16[192,3584]{1,0:T(8,128)(2,1)}, bf16[192,3584]{1,0:T(8,128)(2,1)}, u32[]{:S(2)}, u32[]{:S(2)}) %collective-permute-start.16) | collective-permute-done | bytes 1376288 | tf_op jit(solution)/shard_map/ppermute | solution.py:103
  230.4 31.9 %fusion.14 = (f32[2048]{0:T(1024)S(1)}, bf16[2048,1536]{0,1:T(8,128)(2,1)}) fusion(bf16[2048,3584]{1,0:T(8,128)(2,1)} %get-tuple-element.132, bf16[3584,1536]{1,0:T(8,128)(2,1)} %copy-done.3, bf16[1,2048,1536]{1,2,0:T(8,128)(2,1)} %copy.20), kind=kOutput, calls=%fused_computation.42 | convolution fusion | flops 22564304896 | bytes 38281216 | tf_op jit(solution)/shard_map/dot_general | solution.py:28
  281.6 13.5 %collective-permute-done.20.ry = bf16[192,3584]{1,0:T(8,128)(2,1)S(1)} collective-permute-done((bf16[192,3584]{1,0:T(8,128)(2,1)}, bf16[192,3584]{1,0:T(8,128)(2,1)S(1)}, u32[]{:S(2)}, u32[]{:S(2)}) %collective-permute-start.20) | collective-permute-done | bytes 1376288 | tf_op jit(solution)/shard_map/ppermute | solution.py:103
  295.1 28.5 %fusion.57 = f32[2048,3584]{1,0:T(8,128)} fusion(bf16[2048,1536]{0,1:T(8,128)(2,1)} %fusion.15, bf16[1536,3584]{1,0:T(8,128)(2,1)S(1)} %assemble.9), kind=kOutput, calls=%fused_computation.149 | convolution fusion | flops 22548578304 | bytes 46661632 | tf_op jit(solution)/shard_map/dot_general | solution.py:28
  332.2 39.5 %multiply_convert_fusion = (bf16[2048,3584]{1,0:T(8,128)(2,1)}, f32[2048,3584]{1,0:T(8,128)}) fusion(f32[2048,3584]{1,0:T(8,128)} %fusion.57, bf16[2048,1536]{0,1:T(8,128)(2,1)} %fusion.15, bf16[1536,3584]{1,0:T(8,128)(2,1)} %copy-done.5), kind=kOutput, calls=%fused_computation.14 | convolution fusion | flops 22592618496 | bytes 90701824 | tf_op jit(solution)/shard_map/dot_general | solution.py:28
  432.8 48.5 %fusion = (bf16[2048,3584]{1,0:T(8,128)(2,1)}, bf16[2048,3584]{1,0:T(8,128)(2,1)}) fusion(f32[2048,3584]{1,0:T(8,128)} %fusion.57, f32[2048,3584]{1,0:T(8,128)} %get-tuple-element.137, bf16[2048,1536]{0,1:T(8,128)(2,1)} %bitcast.120, bf16[3584,1536]{1,0:T(8,128)(2,1)} %copy-done.6), kind=kOutput, calls=%fused_computation.6 | convolution fusion | flops 22666018816 | bytes 105381888 | tf_op jit(solution)/shard_map/dot_general | solution.py:28
  498.3 13.1 %add_convert_fusion.10 = bf16[384,3584]{1,0:T(8,128)(2,1)} fusion(bf16[384,3584]{1,0:T(8,128)(2,1)S(1)} %collective-permute-done.28, bf16[2048,384]{0,1:T(8,128)(2,1)S(1)} %copy-done.24, bf16[2048,3584]{1,0:T(8,128)(2,1)} %get-tuple-element.61), kind=kOutput, calls=%fused_computation.110 | convolution fusion | flops 5641273344 | bytes 21757952 | tf_op jit(solution)/shard_map/dot_general | solution.py:28
  554.8 27.2 %convolution_convert_fusion.3 = bf16[2048,1536]{0,1:T(8,128)(2,1)} fusion(bf16[2048,3584]{1,0:T(8,128)(2,1)} %get-tuple-element.61, bf16[1536,3584]{1,0:T(8,128)(2,1)S(1)} %bitcast.117), kind=kOutput, calls=%fused_computation.64 | convolution fusion | flops 22551724032 | bytes 31981568 | tf_op jit(solution)/shard_map/dot_general | solution.py:28
  582.1 29.0 %fusion.16 = (f32[2048]{0:T(1024)S(1)}, bf16[2048,1536]{0,1:T(8,128)(2,1)}) fusion(bf16[2048,1536]{0,1:T(8,128)(2,1)} %get-tuple-element.135, bf16[2048,1536]{0,1:T(8,128)(2,1)} %convolution_convert_fusion.3, bf16[2048,3584]{1,0:T(8,128)(2,1)} %get-tuple-element.62, bf16[1536,3584]{1,0:T(8,128)(2,1)S(1)} %bitcast.119), kind=kOutput, calls=%fused_computation.44 | convolution fusion | flops 22567450624 | bytes 44572672 | tf_op jit(solution)/shard_map/dot_general | solution.py:28
  644.3 48.7 %fusion.7 = (bf16[2048,3584]{1,0:T(8,128)(2,1)}, bf16[2048,3584]{1,0:T(8,128)(2,1)}) fusion(f32[2048,3584]{1,0:T(8,128)} %fusion.56, f32[2048,3584]{1,0:T(8,128)} %get-tuple-element.133, bf16[2048,1536]{0,1:T(8,128)(2,1)} %copy-done.15, bf16[3584,1536]{1,0:T(8,128)(2,1)} %copy-done.3), kind=kOutput, calls=%fused_computation.13 | convolution fusion | flops 22666018816 | bytes 105381888 | tf_op jit(solution)/shard_map/dot_general | solution.py:28
  798.2 13.2 %convert_add_fusion.1 = f32[384,3584]{1,0:T(8,128)} fusion(bf16[384,3584]{1,0:T(8,128)(2,1)} %collective-permute-done.37, bf16[2048,384]{0,1:T(8,128)(2,1)S(1)} %copy-done.23, bf16[2048,3584]{1,0:T(8,128)(2,1)} %get-tuple-element.94), kind=kOutput, calls=%fused_computation.101 | convolution fusion | flops 5639897088 | bytes 24510464 | tf_op jit(solution)/shard_map/dot_general | solution.py:28
  811.5 96.9 %collective-permute-done.42 = bf16[896,1536]{1,0:T(8,128)(2,1)} collective-permute-done((bf16[896,1536]{1,0:T(8,128)(2,1)}, bf16[896,1536]{1,0:T(8,128)(2,1)}, u32[]{:S(2)}, u32[]{:S(2)}) %collective-permute-start.42) | collective-permute-done | bytes 2752544 | tf_op jit(solution)/shard_map/ppermute | solution.py:160
  910.4 13.7 %convert_add_fusion = f32[384,3584]{1,0:T(8,128)} fusion(bf16[384,3584]{1,0:T(8,128)(2,1)} %collective-permute-done.38, bf16[2048,384]{0,1:T(8,128)(2,1)S(1)} %copy-done.23, bf16[2048,3584]{1,0:T(8,128)(2,1)} %get-tuple-element.95), kind=kOutput, calls=%fused_computation.100 | convolution fusion | flops 5639897088 | bytes 24510464 | tf_op jit(solution)/shard_map/dot_general | solution.py:28
  939.1 28.2 %collective-permute-done.43 = bf16[384,3584]{1,0:T(8,128)(2,1)} collective-permute-done((bf16[384,3584]{1,0:T(8,128)(2,1)}, bf16[384,3584]{1,0:T(8,128)(2,1)}, u32[]{:S(2)}, u32[]{:S(2)}) %collective-permute-start.43) | collective-permute-done | bytes 2752544 | tf_op jit(solution)/shard_map/ppermute | solution.py:160
  967.4 59.0 %collective-permute-done.39 = bf16[384,3584]{1,0:T(8,128)(2,1)} collective-permute-done((bf16[384,3584]{1,0:T(8,128)(2,1)}, bf16[384,3584]{1,0:T(8,128)(2,1)}, u32[]{:S(2)}, u32[]{:S(2)}) %collective-permute-start.39) | collective-permute-done | bytes 2752544 | tf_op jit(solution)/shard_map/ppermute | solution.py:160
  1032.4 52.3 %collective-permute-done.41 = bf16[384,3584]{1,0:T(8,128)(2,1)} collective-permute-done((bf16[384,3584]{1,0:T(8,128)(2,1)}, bf16[384,3584]{1,0:T(8,128)(2,1)}, u32[]{:S(2)}, u32[]{:S(2)}) %collective-permute-start.41) | collective-permute-done | bytes 2752544 | tf_op jit(solution)/shard_map/ppermute | solution.py:160
  1101.3 22.2 %fusion.25 = (bf16[2,896,1536]{2,1,0:T(8,128)(2,1)}, f32[2,896,1536]{2,1,0:T(8,128)}, f32[2,896,1536]{2,1,0:T(8,128)}) fusion(bf16[2,896,1536]{2,1,0:T(8,128)(2,1)} %own.11, f32[]{:T(128)S(6)} %min_shard_map.3, bf16[1,896,1536]{2,1,0:T(8,128)(2,1)} %get-tuple-element.108, bf16[1,896,1536]{2,1,0:T(8,128)(2,1)} %get-tuple-element.106, ...), kind=kLoop, calls=%fused_computation.53 | loop fusion | flops 55050240 | bytes 60555268 | tf_op jit(solution)/shard_map/convert_element_type | solution.py:35
  1123.6 23.1 %fusion.22 = (bf16[2,384,3584]{2,1,0:T(8,128)(2,1)}, f32[2,384,3584]{2,1,0:T(8,128)}, f32[2,384,3584]{2,1,0:T(8,128)}) fusion(bf16[2,384,3584]{2,1,0:T(8,128)(2,1)} %own.10, f32[]{:T(128)S(6)} %min_shard_map.3, bf16[1,384,3584]{2,1,0:T(8,128)(2,1)} %get-tuple-element.141, bf16[1,384,3584]{2,1,0:T(8,128)(2,1)S(1)} %copy-done.13, f32[2,384,3584]{2,1,0:T(8,128)} %param.20, ...), kind=kLoop, calls=%fused_computation.50 | loop fusion | flops 55050240 | bytes 60555268 | tf_op jit(solution)/shard_map/convert_element_type | solution.py:35
  1146.7 19.5 %fusion.19 = (bf16[2,384,3584]{2,1,0:T(8,128)(2,1)}, f32[2,384,3584]{2,1,0:T(8,128)}, f32[2,384,3584]{2,1,0:T(8,128)}) fusion(bf16[2,384,3584]{2,1,0:T(8,128)(2,1)S(1)} %bitcast.115, f32[]{:T(128)S(6)} %min_shard_map.3, bf16[1,384,3584]{2,1,0:T(8,128)(2,1)S(1)} %get-tuple-element.116, bf16[1,384,3584]{2,1,0:T(8,128)(2,1)S(1)} %copy-done.14, ...), kind=kLoop, calls=%fused_computation.47 | loop fusion | flops 55050240 | bytes 60555268 | tf_op jit(solution)/shard_map/convert_element_type | solution.py:35
  (271 shorter events, 391.5 us)
Async XLA Ops:
  0.6 101.5 %collective-permute-start = (bf16[2,384,3584]{2,1,0:T(8,128)(2,1)}, bf16[2,384,3584]{2,1,0:T(8,128)(2,1)}, u32[]{:S(2)}, u32[]{:S(2)}) collective-permute-start(bf16[2,384,3584]{2,1,0:T(8,128)(2,1)} %own.9), channel_id=1, source_target_pairs={{0,1},{1,0},{2,3},{3,2},{4,5},{5,4},{6,7},{7,6}} | collective-permute-start | bytes 16515080 | tf_op jit(solution)/shard_map/ppermute | solution.py:89
  10.0 57.4 %collective-permute-start.6 = (bf16[192,3584]{1,0:T(8,128)(2,1)S(1)}, bf16[192,3584]{1,0:T(8,128)(2,1)}, u32[]{:S(2)}, u32[]{:S(2)}) collective-permute-start(bf16[192,3584]{1,0:T(8,128)(2,1)S(1)} %get-tuple-element.131), channel_id=1, source_target_pairs={{0,2},{2,0},{1,3},{3,1},{4,6},{6,4},{5,7},{7,5}} | collective-permute-start | bytes 4128776 | tf_op jit(solution)/shard_map/ppermute | solution.py:95
  40.1 99.2 %collective-permute-start.5 = (bf16[2,384,3584]{2,1,0:T(8,128)(2,1)}, bf16[2,384,3584]{2,1,0:T(8,128)(2,1)}, u32[]{:S(2)}, u32[]{:S(2)}) collective-permute-start(bf16[2,384,3584]{2,1,0:T(8,128)(2,1)} %own.10), channel_id=1, source_target_pairs={{0,1},{1,0},{2,3},{3,2},{4,5},{5,4},{6,7},{7,6}} | collective-permute-start | bytes 16515080 | tf_op jit(solution)/shard_map/ppermute | solution.py:89
  78.1 111.2 %collective-permute-start.10 = (bf16[2,896,1536]{2,1,0:T(8,128)(2,1)}, bf16[2,896,1536]{2,1,0:T(8,128)(2,1)}, u32[]{:S(2)}, u32[]{:S(2)}) collective-permute-start(bf16[2,896,1536]{2,1,0:T(8,128)(2,1)} %own.11), channel_id=1, source_target_pairs={{0,1},{1,0},{2,3},{3,2},{4,5},{5,4},{6,7},{7,6}} | collective-permute-start | bytes 16515080 | tf_op jit(solution)/shard_map/ppermute | solution.py:89
  100.7 36.5 %collective-permute-start.11 = (bf16[448,1536]{1,0:T(8,128)(2,1)}, bf16[448,1536]{1,0:T(8,128)(2,1)S(1)}, u32[]{:S(2)}, u32[]{:S(2)}) collective-permute-start(bf16[448,1536]{1,0:T(8,128)(2,1)} %get-tuple-element.127), channel_id=1, source_target_pairs={{0,2},{2,0},{1,3},{3,1},{4,6},{6,4},{5,7},{7,5}} | collective-permute-start | bytes 4128776 | tf_op jit(solution)/shard_map/ppermute | solution.py:95
  102.2 35.6 %collective-permute-start.8 = (bf16[192,3584]{1,0:T(8,128)(2,1)}, bf16[192,3584]{1,0:T(8,128)(2,1)}, u32[]{:S(2)}, u32[]{:S(2)}) collective-permute-start(bf16[192,3584]{1,0:T(8,128)(2,1)} %collective-permute-done.6.rx), channel_id=1, source_target_pairs={{0,1},{1,0},{2,3},{3,2},{4,5},{5,4},{6,7},{7,6}} | collective-permute-start | bytes 4128776 | tf_op jit(solution)/shard_map/ppermute | solution.py:104
  137.2 50.0 %collective-permute-start.15 = (bf16[192,3584]{1,0:T(8,128)(2,1)}, bf16[192,3584]{1,0:T(8,128)(2,1)}, u32[]{:S(2)}, u32[]{:S(2)}) collective-permute-start(bf16[192,3584]{1,0:T(8,128)(2,1)} %get-tuple-element.128), channel_id=1, source_target_pairs={{0,2},{2,0},{1,3},{3,1},{4,6},{6,4},{5,7},{7,5}} | collective-permute-start | bytes 4128776 | tf_op jit(solution)/shard_map/ppermute | solution.py:95
  137.8 52.1 %collective-permute-start.13 = (bf16[448,1536]{1,0:T(8,128)(2,1)S(1)}, bf16[448,1536]{1,0:T(8,128)(2,1)}, u32[]{:S(2)}, u32[]{:S(2)}) collective-permute-start(bf16[448,1536]{1,0:T(8,128)(2,1)S(1)} %collective-permute-done.11.rx), channel_id=1, source_target_pairs={{0,1},{1,0},{2,3},{3,2},{4,5},{5,4},{6,7},{7,6}} | collective-permute-start | bytes 4128776 | tf_op jit(solution)/shard_map/ppermute | solution.py:104
  137.8 50.0 %collective-permute-start.12 = (bf16[448,1536]{1,0:T(8,128)(2,1)S(1)}, bf16[448,1536]{1,0:T(8,128)(2,1)}, u32[]{:S(2)}, u32[]{:S(2)}) collective-permute-start(bf16[448,1536]{1,0:T(8,128)(2,1)S(1)} %collective-permute-done.11.rx), channel_id=1, source_target_pairs={{0,4},{4,0},{1,5},{5,1},{2,6},{6,2},{3,7},{7,3}} | collective-permute-start | bytes 4128776 | tf_op jit(solution)/shard_map/ppermute | solution.py:103
  187.8 135.8 %collective-permute-start.24 = (bf16[448,1536]{1,0:T(8,128)(2,1)}, bf16[448,1536]{1,0:T(8,128)(2,1)S(1)}, u32[]{:S(2)}, u32[]{:S(2)}) collective-permute-start(bf16[448,1536]{1,0:T(8,128)(2,1)} %get-tuple-element.126), channel_id=1, source_target_pairs={{0,2},{2,0},{1,3},{3,1},{4,6},{6,4},{5,7},{7,5}} | collective-permute-start | bytes 4128776 | tf_op jit(solution)/shard_map/ppermute | solution.py:95
  189.3 73.0 %collective-permute-start.19 = (bf16[192,3584]{1,0:T(8,128)(2,1)}, bf16[192,3584]{1,0:T(8,128)(2,1)}, u32[]{:S(2)}, u32[]{:S(2)}) collective-permute-start(bf16[192,3584]{1,0:T(8,128)(2,1)} %get-tuple-element.130), channel_id=1, source_target_pairs={{0,2},{2,0},{1,3},{3,1},{4,6},{6,4},{5,7},{7,5}} | collective-permute-start | bytes 4128776 | tf_op jit(solution)/shard_map/ppermute | solution.py:95
  189.8 73.5 %collective-permute-start.17 = (bf16[192,3584]{1,0:T(8,128)(2,1)}, bf16[192,3584]{1,0:T(8,128)(2,1)}, u32[]{:S(2)}, u32[]{:S(2)}) collective-permute-start(bf16[192,3584]{1,0:T(8,128)(2,1)} %collective-permute-done.15.rx), channel_id=1, source_target_pairs={{0,1},{1,0},{2,3},{3,2},{4,5},{5,4},{6,7},{7,6}} | collective-permute-start | bytes 4128776 | tf_op jit(solution)/shard_map/ppermute | solution.py:104
  219.9 43.4 %collective-permute-start.18 = (bf16[192,3584]{1,0:T(8,128)(2,1)}, bf16[192,3584]{1,0:T(8,128)(2,1)}, u32[]{:S(2)}, u32[]{:S(2)}) collective-permute-start(bf16[192,3584]{1,0:T(8,128)(2,1)} %collective-permute-done.16.ry), channel_id=1, source_target_pairs={{0,1},{1,0},{2,3},{3,2},{4,5},{5,4},{6,7},{7,6}} | collective-permute-start | bytes 4128776 | tf_op jit(solution)/shard_map/ppermute | solution.py:105
  262.2 61.9 %collective-permute-start.21 = (bf16[192,3584]{1,0:T(8,128)(2,1)}, bf16[192,3584]{1,0:T(8,128)(2,1)S(1)}, u32[]{:S(2)}, u32[]{:S(2)}) collective-permute-start(bf16[192,3584]{1,0:T(8,128)(2,1)} %collective-permute-done.19.rx), channel_id=1, source_target_pairs={{0,1},{1,0},{2,3},{3,2},{4,5},{5,4},{6,7},{7,6}} | collective-permute-start | bytes 4128776 | tf_op jit(solution)/shard_map/ppermute | solution.py:104
  323.6 82.8 %collective-permute-start.25 = (bf16[448,1536]{1,0:T(8,128)(2,1)S(1)}, bf16[448,1536]{1,0:T(8,128)(2,1)S(1)}, u32[]{:S(2)}, u32[]{:S(2)}) collective-permute-start(bf16[448,1536]{1,0:T(8,128)(2,1)S(1)} %collective-permute-done.24.rx), channel_id=1, source_target_pairs={{0,4},{4,0},{1,5},{5,1},{2,6},{6,2},{3,7},{7,3}} | collective-permute-start | bytes 4128776 | tf_op jit(solution)/shard_map/ppermute | solution.py:103
  727.3 36.9 %collective-permute-start.34 = (bf16[384,3584]{1,0:T(8,128)(2,1)S(1)}, bf16[384,3584]{1,0:T(8,128)(2,1)S(1)}, u32[]{:S(2)}, u32[]{:S(2)}) collective-permute-start(bf16[384,3584]{1,0:T(8,128)(2,1)S(1)} %copy-done.33), channel_id=1, source_target_pairs={{0,1},{1,0},{2,3},{3,2},{4,5},{5,4},{6,7},{7,6}} | collective-permute-start | bytes 8257544 | tf_op jit(solution)/shard_map/ppermute | solution.py:158
  727.5 206.0 %collective-permute-start.44 = (bf16[896,1536]{1,0:T(8,128)(2,1)}, bf16[896,1536]{1,0:T(8,128)(2,1)}, u32[]{:S(2)}, u32[]{:S(2)}) collective-permute-start(bf16[896,1536]{1,0:T(8,128)(2,1)} %add_convert_fusion.11), channel_id=1, source_target_pairs={{0,2},{2,0},{1,3},{3,1},{4,6},{6,4},{5,7},{7,5}} | collective-permute-start | bytes 8257544 | tf_op jit(solution)/shard_map/ppermute | solution.py:160
  729.0 46.9 %collective-permute-start.35 = (bf16[384,3584]{1,0:T(8,128)(2,1)}, bf16[384,3584]{1,0:T(8,128)(2,1)}, u32[]{:S(2)}, u32[]{:S(2)}) collective-permute-start(bf16[384,3584]{1,0:T(8,128)(2,1)} %convolution_convert_fusion.9), channel_id=1, source_target_pairs={{0,1},{1,0},{2,3},{3,2},{4,5},{5,4},{6,7},{7,6}} | collective-permute-start | bytes 8257544 | tf_op jit(solution)/shard_map/ppermute | solution.py:158
  741.3 188.3 %collective-permute-start.40 = (bf16[384,3584]{1,0:T(8,128)(2,1)}, bf16[384,3584]{1,0:T(8,128)(2,1)}, u32[]{:S(2)}, u32[]{:S(2)}) collective-permute-start(bf16[384,3584]{1,0:T(8,128)(2,1)} %add_convert_fusion.10), channel_id=1, source_target_pairs={{0,2},{2,0},{1,3},{3,1},{4,6},{6,4},{5,7},{7,5}} | collective-permute-start | bytes 8257544 | tf_op jit(solution)/shard_map/ppermute | solution.py:160
  775.9 132.5 %collective-permute-start.42 = (bf16[896,1536]{1,0:T(8,128)(2,1)}, bf16[896,1536]{1,0:T(8,128)(2,1)}, u32[]{:S(2)}, u32[]{:S(2)}) collective-permute-start(bf16[896,1536]{1,0:T(8,128)(2,1)} %add_convert_fusion.8), channel_id=1, source_target_pairs={{0,2},{2,0},{1,3},{3,1},{4,6},{6,4},{5,7},{7,5}} | collective-permute-start | bytes 8257544 | tf_op jit(solution)/shard_map/ppermute | solution.py:160
  788.4 121.4 %collective-permute-start.38 = (bf16[384,3584]{1,0:T(8,128)(2,1)}, bf16[384,3584]{1,0:T(8,128)(2,1)}, u32[]{:S(2)}, u32[]{:S(2)}) collective-permute-start(bf16[384,3584]{1,0:T(8,128)(2,1)} %convolution_convert_fusion.5), channel_id=1, source_target_pairs={{0,1},{1,0},{2,3},{3,2},{4,5},{5,4},{6,7},{7,6}} | collective-permute-start | bytes 8257544 | tf_op jit(solution)/shard_map/ppermute | solution.py:158
  797.4 170.0 %collective-permute-start.43 = (bf16[384,3584]{1,0:T(8,128)(2,1)}, bf16[384,3584]{1,0:T(8,128)(2,1)}, u32[]{:S(2)}, u32[]{:S(2)}) collective-permute-start(bf16[384,3584]{1,0:T(8,128)(2,1)} %add_convert_fusion.9), channel_id=1, source_target_pairs={{0,2},{2,0},{1,3},{3,1},{4,6},{6,4},{5,7},{7,5}} | collective-permute-start | bytes 8257544 | tf_op jit(solution)/shard_map/ppermute | solution.py:160
  908.4 118.0 %collective-permute-start.39 = (bf16[384,3584]{1,0:T(8,128)(2,1)}, bf16[384,3584]{1,0:T(8,128)(2,1)}, u32[]{:S(2)}, u32[]{:S(2)}) collective-permute-start(bf16[384,3584]{1,0:T(8,128)(2,1)} %add_convert_fusion.7), channel_id=1, source_target_pairs={{0,2},{2,0},{1,3},{3,1},{4,6},{6,4},{5,7},{7,5}} | collective-permute-start | bytes 8257544 | tf_op jit(solution)/shard_map/ppermute | solution.py:160
  909.8 174.8 %collective-permute-start.41 = (bf16[384,3584]{1,0:T(8,128)(2,1)}, bf16[384,3584]{1,0:T(8,128)(2,1)}, u32[]{:S(2)}, u32[]{:S(2)}) collective-permute-start(bf16[384,3584]{1,0:T(8,128)(2,1)} %add_convert_fusion.6), channel_id=1, source_target_pairs={{0,2},{2,0},{1,3},{3,1},{4,6},{6,4},{5,7},{7,5}} | collective-permute-start | bytes 8257544 | tf_op jit(solution)/shard_map/ppermute | solution.py:160
  (86 other events, 1948.0 us)

commit v2 on v1

v2 whole, which is shorter than its diff:
```python
import functools

import jax
import jax.numpy as jnp
from jax import lax
from jax.experimental import pallas as pl
from jax.experimental.pallas import tpu as pltpu
from jax.sharding import PartitionSpec as P


F32, BF16 = jnp.float32, jnp.bfloat16
OVER_X = [(0, 2), (2, 0), (1, 3), (3, 1)]
OVER_CORE = [(0, 1), (1, 0), (2, 3), (3, 2)]
OVER_Y = [(0, 1), (1, 0)]


def normed(h):
    wide = h.astype(F32)
    scale = lax.rsqrt(jnp.mean(wide**2, -1, keepdims=True) + 1e-6)
    return (wide * scale).astype(BF16)


def adamw(w, m, v, g):
    m = 0.9 * m + 0.1 * g
    v = 0.95 * v + 0.05 * g * g
    step = m * lax.rsqrt(v + 1e-8) + 0.1 * w
    return (w - 0.02 * step).astype(BF16), m, v


def others(d):
    x, c = d // 2, d % 2
    return d, 2 * x + 1 - c, 2 * (1 - x) + c, 2 * (1 - x) + 1 - c


def assemble_kernel(number, rows, own, own_c, rx, ry, rx_c, ry_c, out, buf, sem_in, sem_out):
    d, r = lax.axis_index("dp"), lax.axis_index("rep")
    half = rows // 2
    own_i, core_i, x_i, xc_i = others(d)
    at = lambda i, n: pl.ds(pl.multiple_of(i, 16), n)
    moves = [
        (own.at[number], own_i * rows, rows),
        (own_c.at[number], core_i * rows, rows),
        (rx, x_i * rows + r * half, half),
        (ry, x_i * rows + (1 - r) * half, half),
        (rx_c, xc_i * rows + r * half, half),
        (ry_c, xc_i * rows + (1 - r) * half, half),
    ]
    ins = [pltpu.make_async_copy(src, buf.at[at(i, n)], sem_in.at[k]) for k, (src, i, n) in enumerate(moves)]
    outs = [pltpu.make_async_copy(buf.at[at(i, n)], out.at[at(i, n)], sem_out.at[k]) for k, (src, i, n) in enumerate(moves)]
    for one in ins:
        one.start()
    for one, two in zip(ins, outs):
        one.wait()
        two.start()
    for one in outs:
        one.wait()


def assembled(number, own, own_c, rx, ry, rx_c, ry_c):
    _, rows, cols = own.shape
    any_space = pl.BlockSpec(memory_space=pl.ANY)
    return pl.pallas_call(
        functools.partial(assemble_kernel, number, rows),
        out_shape=jax.ShapeDtypeStruct((4 * rows, cols), BF16),
        in_specs=[any_space] * 6,
        out_specs=any_space,
        scratch_shapes=[pltpu.VMEM((4 * rows, cols), BF16), pltpu.SemaphoreType.DMA((6,)), pltpu.SemaphoreType.DMA((6,))],
        compiler_params=pltpu.CompilerParams(vmem_limit_bytes=VMEM),
        cost_estimate=pl.CostEstimate(flops=10**9, bytes_accessed=8 * 4 * rows * cols, transcendentals=0),
        name="assemble",
    )(own, own_c, rx, ry, rx_c, ry_c)


VMEM = 63 << 20


def call(kernel, out_shape, grid, in_specs, out_specs, flops, moved, prefetch=None, scratch=()):
    gs = pltpu.PrefetchScalarGridSpec(
        num_scalar_prefetch=0 if prefetch is None else 1,
        grid=grid,
        in_specs=in_specs,
        out_specs=out_specs,
        scratch_shapes=list(scratch),
    )
    return pl.pallas_call(
        kernel,
        out_shape=out_shape,
        grid_spec=gs,
        compiler_params=pltpu.CompilerParams(vmem_limit_bytes=VMEM),
        cost_estimate=pl.CostEstimate(flops=flops, bytes_accessed=moved, transcendentals=0),
    )


def shaped(shape, kind=BF16):
    return jax.ShapeDtypeStruct(shape, kind)


def resident(shape):
    return pl.BlockSpec(shape, lambda *_: (0,) * len(shape), pipeline_mode=pl.Buffered(1))


def turned_of(a):
    return a.astype(F32).T.astype(BF16)


def norm_kernel(x, a, a_t):
    out = normed(x[...])
    a[...] = out
    a_t[...] = turned_of(out)


def turn_kernel(x, x_t):
    x_t[...] = turned_of(x[...])


def back_norm_kernel(by_a, h, by_h, out, out_t):
    new = by_h[...] + jax.vjp(normed, h[...])[1](by_a[...])[0]
    out[...] = new
    out_t[...] = turned_of(new)


def by_rows(kernel, kinds, *arrays, bm=256):
    m, n = arrays[0].shape
    straight, across = pl.BlockSpec((bm, n), lambda i: (i, 0)), pl.BlockSpec((n, bm), lambda i: (0, i))
    return call(
        kernel, [shaped((n, m) if kind == "t" else (m, n)) for kind in kinds], (m // bm,), [straight] * len(arrays),
        [across if kind == "t" else straight for kind in kinds], 10**9, 2 * m * n * (len(arrays) + len(kinds)),
    )(*arrays)


def gate_up_kernel(number, width, at, a, *refs):
    sources, outs, (buf, sem) = (refs[:4], refs[4:8]), refs[-7:-2], refs[-2:]
    gate, up, hidden, wg, wu = outs
    t = pl.program_id(0)
    tile = gate.shape[1]
    rows = buf.shape[2] // 4
    here = lambda first: pl.ds(pl.multiple_of(first, 128), tile)

    def copies(t):
        slot = lax.rem(t, 2)
        out = []
        for p in range(2):
            own, own_c, rx, rx_c = sources[p]
            cut = [own.at[number, :, here(at[4] * width + t * tile)], own_c.at[number, :, here(at[4] * width + t * tile)]]
            cut += [rx.at[:, here(t * tile)], rx_c.at[:, here(t * tile)]]
            for k, src in enumerate(cut):
                dst = buf.at[slot, p, pl.ds(pl.multiple_of(at[k] * rows, rows), rows)]
                out.append(pltpu.make_async_copy(src, dst, sem.at[slot, p, k]))
        return out

    @pl.when(t == 0)
    def _():
        for one in copies(t):
            one.start()

    @pl.when(t + 1 < pl.num_programs(0))
    def _():
        for one in copies(t + 1):
            one.start()

    for one in copies(t):
        one.wait()
    slot = lax.rem(t, 2)
    wg[...] = buf[slot, 0]
    wu[...] = buf[slot, 1]
    g = jnp.dot(a[...], buf[slot, 0], preferred_element_type=F32)
    u = jnp.dot(a[...], buf[slot, 1], preferred_element_type=F32)
    gate[...] = g
    up[...] = u
    hidden[...] = (jax.nn.silu(g) * u).astype(BF16)


def gate_up(number, at, a, gates, ups, before=()):
    m, k = a.shape
    n, width = gates[0].shape[2], gates[2].shape[1]
    bn = 256
    tiles = width // bn
    any_space = pl.BlockSpec(memory_space=pl.ANY)
    place = lambda t, at: (0, at[4] * tiles + t)
    out, w = pl.BlockSpec((m, bn), place), pl.BlockSpec((k, bn), place)
    return pl.pallas_call(
        functools.partial(gate_up_kernel, number, width),
        out_shape=[shaped((m, n), F32), shaped((m, n), F32), shaped((m, n)), shaped((k, n)), shaped((k, n))],
        grid_spec=pltpu.PrefetchScalarGridSpec(
            num_scalar_prefetch=1,
            grid=(tiles,),
            in_specs=[resident((m, k))] + [any_space] * (8 + len(before)),
            out_specs=[out] * 3 + [w] * 2,
            scratch_shapes=[pltpu.VMEM((2, 2, k, bn), BF16), pltpu.SemaphoreType.DMA((2, 2, 4))],
        ),
        input_output_aliases={10 + i: i for i in range(len(before))},
        compiler_params=pltpu.CompilerParams(vmem_limit_bytes=VMEM),
        cost_estimate=pl.CostEstimate(flops=4 * m * width * k, bytes_accessed=10 * m * width + 4 * k * width, transcendentals=0),
        name="gate_up",
    )(at, a, *gates, *ups, *before)


def down_kernel(hidden, w, x, h, a, a_t):
    out = x[...] + jnp.dot(hidden[...], w[...], preferred_element_type=F32).astype(BF16)
    h[...] = out
    out = normed(out)
    a[...] = out
    a_t[...] = turned_of(out)


def down(hidden, w, x, bm=256):
    m, k = hidden.shape
    n = w.shape[1]
    out = pl.BlockSpec((bm, n), lambda i: (i, 0))
    return call(
        down_kernel, [shaped((m, n))] * 2 + [shaped((n, m))], (m // bm,),
        [pl.BlockSpec((bm, k), lambda i: (i, 0)), resident((k, n)), out], [out] * 2 + [pl.BlockSpec((n, bm), lambda i: (0, i))],
        2 * m * n * k, 2 * k * n + 2 * m * k,
    )(hidden, w, x)


NT = (((1,), (1,)), ((), ()))


def by_hidden_kernel(dy, w, gate, up, dg, du):
    by = lax.dot_general(dy[...], w[...], NT, preferred_element_type=F32).astype(BF16).astype(F32)
    g, u = gate[...], up[...]
    s = jax.nn.sigmoid(g)
    silu = g * s
    dg[...] = (by * u * (s + silu * (1 - s))).astype(BF16)
    du[...] = (by * silu).astype(BF16)


def by_hidden(dy, w, gate, up, bm=2048, bn=512):
    m, k = dy.shape
    n = w.shape[0]
    out = pl.BlockSpec((bm, bn), lambda j, i: (i, j))
    return call(
        by_hidden_kernel, [shaped((m, n))] * 2, (n // bn, m // bm),
        [resident((m, k)), pl.BlockSpec((bn, k), lambda j, i: (j, 0)), out, out], [out] * 2,
        2 * m * n * k, 12 * m * n,
    )(dy, w, gate, up)


def by_a_kernel(dg, du, wg, wu, out):
    one = lax.dot_general(dg[...], wg[...], NT, preferred_element_type=F32).astype(BF16)
    two = lax.dot_general(du[...], wu[...], NT, preferred_element_type=F32).astype(BF16)
    out[...] = one + two


def by_a(dg, du, wg, wu, bm=1024, bn=512):
    m, k = dg.shape
    n = wg.shape[0]
    lhs = pl.BlockSpec((bm, k), lambda i, j: (i, 0))
    w = pl.BlockSpec((bn, k), lambda i, j: (j, 0))
    return call(
        by_a_kernel, shaped((m, n)), (m // bm, n // bn), [lhs, lhs, w, w], pl.BlockSpec((bm, bn), lambda i, j: (i, j)),
        4 * m * n * k, 4 * m * k + 4 * n * k * (m // bm),
    )(dg, du, wg, wu)


TILE = 512


def exchange(d, src, dst, send_sem, recv_sem):
    return pltpu.make_async_remote_copy(
        src_ref=src, dst_ref=dst, send_sem=send_sem, recv_sem=recv_sem, device_id={"dp": others(d)[1]}, device_id_type=pl.DeviceIdType.MESH
    )


def greet(d):
    barrier = pltpu.get_barrier_semaphore()
    pl.semaphore_signal(barrier, inc=1, device_id={"dp": others(d)[1]}, device_id_type=pl.DeviceIdType.MESH)
    pl.semaphore_wait(barrier, 1)


def term_rows_kernel(left, right, send, own, full, there, send_sem, recv_sem):
    d = lax.axis_index("dp")
    own_i, core_i, x_i, xc_i = others(d)
    rows, tile = send.shape
    tiles = full.shape[1] // tile
    j = pl.program_id(0)
    cols = lambda k: pl.ds(pl.multiple_of(k * tile, tile), tile)
    at = lambda i: pl.ds(pl.multiple_of(i * rows, rows), rows)

    def copies(k):
        return [
            exchange(d, full.at[at(i), cols(k)], there.at[n, :, cols(k)], send_sem.at[n, k], recv_sem.at[n, k])
            for n, i in enumerate((core_i, xc_i))
        ]

    @pl.when(j == 0)
    def _():
        greet(d)

    @pl.when((j >= 1) & (j <= tiles))
    def _():
        for one in copies(j - 1):
            one.start()

    @pl.when(j < tiles)
    def _():
        full[:, cols(j)] = jnp.dot(left[...], right[...], preferred_element_type=F32).astype(BF16)

    @pl.when(j >= 2)
    def _():
        k = j - 2
        for one in copies(k):
            one.wait()
        own[...] = full[at(own_i), cols(k)].astype(F32) + there[0, :, cols(k)].astype(F32)
        send[...] = (full[at(x_i), cols(k)].astype(F32) + there[1, :, cols(k)].astype(F32)).astype(BF16)


def term_rows(left, right):
    m, k = left.shape
    n, rows, tiles = right.shape[1], m // 4, right.shape[1] // TILE
    out = pl.BlockSpec((rows, TILE), lambda j: (0, jnp.maximum(j - 2, 0)))
    return pl.pallas_call(
        term_rows_kernel,
        out_shape=[shaped((rows, n)), shaped((rows, n), F32)],
        grid=(tiles + 2,),
        in_specs=[resident((m, k)), pl.BlockSpec((k, TILE), lambda j: (0, jnp.minimum(j, tiles - 1)))],
        out_specs=[out, out],
        scratch_shapes=[pltpu.VMEM((m, n), BF16), pltpu.VMEM((2, rows, n), BF16), pltpu.SemaphoreType.DMA((2, tiles)), pltpu.SemaphoreType.DMA((2, tiles))],
        compiler_params=pltpu.CompilerParams(vmem_limit_bytes=VMEM, collective_id=0, has_side_effects=True),
        cost_estimate=pl.CostEstimate(flops=2 * m * n * k, bytes_accessed=2 * (m * k + k * n + m * n), transcendentals=0),
        name="term_rows",
    )(left, right)


def term_columns_kernel(left, right, send, own, full, there, send_sem, recv_sem):
    d = lax.axis_index("dp")
    x, c = d // 2, d % 2
    wide = send.shape[1]
    tile = right.shape[1]
    tiles = full.shape[1] // tile
    j = pl.program_id(0)

    def pieces(s):
        first, end = s * wide, (s + 1) * wide
        if s < 3:
            return [(first, wide, (end - 1) // tile)]
        cut = (tiles - 1) * tile
        return [(first, cut - first, (cut - 1) // tile), (cut, end - cut, tiles - 1)]

    def copies(s):
        out = []
        for p, (first, width, last) in enumerate(pieces(s)):
            n = jnp.where(x == s // 2, 0, 1)
            dst = there.at[n, :, pl.ds(first - s * wide, width)]
            out.append((last, exchange(d, full.at[:, pl.ds(first, width)], dst, send_sem.at[s, p], recv_sem.at[s, p])))
        return out

    @pl.when(j == 0)
    def _():
        greet(d)

    for s in range(4):
        for last, one in copies(s):

            @pl.when((j == last + 1) & (c != s % 2))
            def _(one=one):
                one.start()

    @pl.when(j < tiles)
    def _():
        here = pl.ds(pl.multiple_of(j * tile, tile), tile)
        full[:, here] = jnp.dot(left[...], right[...], preferred_element_type=F32).astype(BF16)

    @pl.when(j == tiles + 1)
    def _():
        for s in range(4):
            for last, one in copies(s):

                @pl.when(c != s % 2)
                def _(one=one):
                    one.wait_send()

                @pl.when(c == s % 2)
                def _(one=one):
                    one.wait_recv()

            @pl.when((c == s % 2) & (x == s // 2))
            def _(s=s):
                own[...] = full[:, pl.ds(s * wide, wide)].astype(F32) + there[0].astype(F32)

            @pl.when((c == s % 2) & (x != s // 2))
            def _(s=s):
                send[...] = (full[:, pl.ds(s * wide, wide)].astype(F32) + there[1].astype(F32)).astype(BF16)


def term_columns(left, right):
    m, k = left.shape
    n, wide, tiles = right.shape[1], right.shape[1] // 4, right.shape[1] // TILE
    return pl.pallas_call(
        term_columns_kernel,
        out_shape=[shaped((m, wide)), shaped((m, wide), F32)],
        grid=(tiles + 2,),
        in_specs=[resident((m, k)), pl.BlockSpec((k, TILE), lambda j: (0, jnp.minimum(j, tiles - 1)))],
        out_specs=[pl.BlockSpec((m, wide), lambda j: (0, 0))] * 2,
        scratch_shapes=[pltpu.VMEM((m, n), BF16), pltpu.VMEM((2, m, wide), BF16), pltpu.SemaphoreType.DMA((4, 2)), pltpu.SemaphoreType.DMA((4, 2))],
        compiler_params=pltpu.CompilerParams(vmem_limit_bytes=VMEM, collective_id=1, has_side_effects=True),
        cost_estimate=pl.CostEstimate(flops=2 * m * n * k, bytes_accessed=2 * (m * k + k * n + m * n), transcendentals=0),
        name="term_columns",
    )(left, right)


def turned_kernel(own, arrived, out, squares):
    g = (own[...] + arrived[...].astype(F32)).astype(BF16).astype(F32)

    @pl.when(pl.program_id(0) == 0)
    def _():
        squares[0, 0] = 0.0

    squares[0, 0] += jnp.sum(g * g)
    out[...] = g.T.astype(BF16)


def turned(own, arrived):
    m, n = own.shape
    bn = 128
    spec = pl.BlockSpec((m, bn), lambda j: (0, j))
    g, squares = pl.pallas_call(
        turned_kernel,
        out_shape=[shaped((n, m)), shaped((1, 1), F32)],
        grid=(n // bn,),
        in_specs=[spec, spec],
        out_specs=[pl.BlockSpec((bn, m), lambda j: (j, 0)), pl.BlockSpec(memory_space=pltpu.SMEM)],
        compiler_params=pltpu.CompilerParams(vmem_limit_bytes=VMEM),
        cost_estimate=pl.CostEstimate(flops=4 * m * n, bytes_accessed=8 * m * n, transcendentals=0),
        name="turned",
    )(own, arrived)
    return g, squares[0, 0]


def solution(mesh):
    def step(x, dy, *arrays):
        weights, m, v = (arrays[i : i + 3] for i in (0, 3, 6))
        d, r = lax.axis_index("dp"), lax.axis_index("rep")
        own_i, core_i, x_i, xc_i = others(d)
        layers = weights[0].shape[0]

        from_core = [lax.ppermute(w, "dp", OVER_CORE) for w in weights]

        def across(i, number):
            rows, cols = weights[i].shape[1:]
            if i == 2:
                mine = lax.dynamic_slice(weights[i], (number, r * (rows // 2), 0), (1, rows // 2, cols))[0]
            else:
                mine = lax.dynamic_slice(weights[i], (number, 0, r * (cols // 2)), (1, rows, cols // 2))[0]
            return lax.ppermute(mine, "dp", OVER_X)

        halves = {(i, number): across(i, number) for number in range(layers) for i in range(3)}

        def first(i, number, *behind):
            rx = halves[i, number]
            if behind:
                rx = lax.optimization_barrier((rx, *behind))[0]
            return lax.ppermute(rx, "dp", OVER_CORE)

        def second(i, number, *behind):
            rx = halves[i, number]
            if behind:
                rx = lax.optimization_barrier((rx, *behind))[0]
            ry = lax.ppermute(rx, "rep", OVER_Y)
            return ry, lax.ppermute(ry, "dp", OVER_CORE)

        def whole_down(number, behind):
            ry, ry_c = second(2, number, behind)
            return assembled(number, weights[2], from_core[2], halves[2, number], ry, first(2, number), ry_c)

        last = []

        def ordered(*some):
            out = lax.optimization_barrier((*some, *last))[: len(some)] if last else some
            return out[0] if len(some) == 1 else out

        def noted(one):
            last[:] = [one]
            return one

        at = jnp.stack([own_i, core_i, x_i, xc_i, r]).astype(jnp.int32)
        at_b = jnp.stack([own_i, core_i, x_i, xc_i, 1 - r]).astype(jnp.int32)

        def ab(number, a, behind):
            arrived = [(weights[i], from_core[i], halves[i, number], first(i, number, *behind[i])) for i in (0, 1)]
            outs = gate_up(number, at, a, *arrived)
            return outs, [(weights[i], from_core[i], *second(i, number, *behind[i])) for i in (0, 1)]

        a0, a0_t = by_rows(norm_kernel, " t", x[0])
        (dy_t,) = by_rows(turn_kernel, "t", dy[0])
        a0, a0_t, dy_t = lax.optimization_barrier((a0, a0_t, dy_t))
        outs, arrived = ab(0, a0, ((), ()))
        w_down0 = whole_down(0, outs[2])
        gate0, up0, hidden0, _, _ = gate_up(0, at_b, a0, *arrived, outs)
        h1, a1, a1_t = down(hidden0, w_down0, x[0])
        outs, arrived = ab(1, a1, ((hidden0,), (h1,)))
        w_down1 = whole_down(1, outs[2])
        gate1, up1, hidden1, w_gate1, w_up1 = gate_up(1, at_b, a1, *arrived, outs)
        noted(hidden1)

        mine, late = [[None] * 3 for _ in range(layers)], []

        def term(i, number, kernel, left, right):
            send, own = kernel(left, ordered(right))
            noted(send)
            late.append((i, number, lax.ppermute(send, "dp", OVER_X), own))

        term(2, 1, term_columns, dy_t, hidden1)
        by_gate, by_up = by_hidden(ordered(dy[0]), w_down1, gate1, up1)
        noted(by_gate)
        term(0, 1, term_rows, a1_t, by_gate)
        term(1, 1, term_rows, a1_t, by_up)
        by_in = by_a(ordered(by_gate), by_up, w_gate1, w_up1)
        by_h, by_h_t = by_rows(back_norm_kernel, " t", by_in, h1, dy[0])
        noted(by_h)
        term(2, 0, term_columns, by_h_t, hidden0)
        by_gate, by_up = by_hidden(ordered(by_h), w_down0, gate0, up0)
        noted(by_gate)
        term(0, 0, term_rows, a0_t, by_gate)
        term(1, 0, term_rows, a0_t, by_up)
        squares = 0.0
        for i, number, from_x, own in late:
            if i == 2:
                mine[number][i], more = turned(own, from_x)
            else:
                mine[number][i] = g = (own + from_x.astype(F32)).astype(BF16)
                more = jnp.sum(jnp.square(g.astype(F32)))
            squares += more

        squares = lax.psum(squares, "dp")
        count = 4 * sum(g.size for gs in mine for g in gs)
        factor = jnp.minimum(1.0, 0.5 * lax.rsqrt(squares / count + 1e-30))
        new = []
        for i in range(3):
            g = jnp.stack([mine[number][i] for number in range(layers)]).astype(F32) * factor
            new.append(adamw(weights[i].astype(F32), m[i], v[i], g))
        return tuple(one[which] for which in range(3) for one in new)

    states, cut = P(("rep", "dp"), None, None), P(None, "dp", None)
    return jax.shard_map(
        step,
        mesh=mesh,
        in_specs=(states, states) + (cut,) * 9,
        out_specs=(P("rep", "dp", None),) * 9,
        check_vma=False,
    )
```

time: 1170 us -> 919 us (0.79)
  matrix products: 558 us -> 0 us
  Pallas kernels: 22.7 us -> 578 us
  waiting for transfers between devices: 344 us -> 199 us
  local copies, waits for them, and re-layouts: 81.7 us -> 9.18 us
  other arithmetic: 121 us -> 86.5 us
    pallas_call x0 -> x19, Pallas kernels: none -> 561 us  [the longest x4 134 us: gate_up(): pl.pallas_call(functools.partial(gate_up_kernel, number, width), out_shap...]
    dot_general x33 -> x0, matrix products: 558 us -> none  [dot(): return lax.dot_general(a, b, (dims, ((), ())), preferred_element_type=F32)]
    ppermute x36 -> x24, waiting for transfers between devices: 302 us -> 141 us  [the longest x6 94.6 us: second(): ry = lax.ppermute(rx, 'rep', OVER_Y)]
    unnamed x132 -> x4, local copies, waits for them, and re-layouts: 48.2 us -> 0.01 us
    dynamic_slice x4 -> x0, local copies, waits for them, and re-layouts: 24 us -> none  [term(): lax.dynamic_slice(left, (0, i * rows), (left.shape[0], rows))]
    convert_element_type x2 -> x0, other arithmetic: 16.3 us -> none  [normed(): return (wide * scale).astype(BF16)]
    ppermute x6, waiting for transfers between devices: 41.9 us -> 58 us  [across(): return lax.ppermute(mine, 'dp', OVER_X)]
    convert_element_type x3 -> x2, other arithmetic: 64.8 us -> 58.9 us  [adamw(): return ((w - 0.02 * step).astype(BF16), m, v)]
  transfers between devices with their start and end apart: 45 -> 33, of which waited for: 10 -> 7; matrix products, arithmetic and copies ran while one was open for 34% -> 3% of each run, Pallas kernels for 2% -> 64%
where the time goes in v2:
time: 919 us; the launch traced here: 910 us
  Pallas kernels  578 us (63%)
  waiting for transfers between devices  199 us (22%)
  other arithmetic  86.5 us (9%)
  starting transfers between devices  24.4 us (3%)
    pallas_call x4, Pallas kernels, gate_up(): pl.pallas_call(functools.partial(gate_up_kernel, number, width), out_shap...  134 us
    pallas_call x4, Pallas kernels, term_rows(): pl.pallas_call(term_rows_kernel, out_shape=[shaped((rows, n)), shaped((ro...  132 us
    ppermute x6, waiting for transfers between devices, second(): ry = lax.ppermute(rx, 'rep', OVER_Y)  94.6 us
    pallas_call x2, Pallas kernels, by_hidden(): call(by_hidden_kernel, [shaped((m, n))] * 2, (n // bn, m // bm), [residen...  88.5 us
    pallas_call x2, Pallas kernels, term_columns(): pl.pallas_call(term_columns_kernel, out_shape=[shaped((m, wide)), shaped(...  69.3 us
    convert_element_type x2, other arithmetic, adamw(): return ((w - 0.02 * step).astype(BF16), m, v)  58.9 us
    ppermute x6, waiting for transfers between devices, across(): return lax.ppermute(mine, 'dp', OVER_X)  58 us
    pallas_call x1, Pallas kernels, by_a(): call(by_a_kernel, shaped((m, n)), (m // bm, n // bn), [lhs, lhs, w, w], p...  55 us
  transfers between devices with their start and end apart: 33, of which 7 were waited for; matrix products, arithmetic and copies ran while one was open for 3% of the time, Pallas kernels for 64%

profile of v2, /device:TPU:0, one launch (start us, length us, event | category | flops | bytes accessed | tf_op | source)
XLA Modules:
  0.0 909.6 jit_solution(6803599144046917268)
XLA Ops:
  9.6 29.2 %collective-permute-done.1.refs_2_ = bf16[384,1792]{1,0:T(8,128)(2,1)} collective-permute-done((bf16[384,1792]{1,0:T(8,128)(2,1)S(1)}, bf16[384,1792]{1,0:T(8,128)(2,1)}, u32[]{:S(2)}, u32[]{:S(2)}) %collective-permute-start.1) | collective-permute-done | bytes 1376288 | tf_op jit(solution)/shard_map/ppermute | solution.py:446
  38.8 28.8 %collective-permute-done.5.refs_6_ = bf16[384,1792]{1,0:T(8,128)(2,1)} collective-permute-done((bf16[384,1792]{1,0:T(8,128)(2,1)S(1)}, bf16[384,1792]{1,0:T(8,128)(2,1)}, u32[]{:S(2)}, u32[]{:S(2)}) %collective-permute-start.5) | collective-permute-done | bytes 1376288 | tf_op jit(solution)/shard_map/ppermute | solution.py:446
  69.7 10.1 %shard_map.178 = (bf16[2048,1536]{1,0:T(8,128)(2,1)}, bf16[1536,2048]{1,0:T(8,128)(2,1)}) custom-call(bf16[2048,1536]{1,0:T(8,128)(2,1)} %bitcast.35), custom_call_target="tpu_custom_call" | custom-call | flops 1000000000 | bytes 18874368 | tf_op jit(solution)/shard_map/pallas_call | solution.py:125
  102.7 27.3 %collective-permute-done.6.refs_6_ = bf16[384,1792]{1,0:T(8,128)(2,1)} collective-permute-done((bf16[384,1792]{1,0:T(8,128)(2,1)}, bf16[384,1792]{1,0:T(8,128)(2,1)}, u32[]{:S(2)}, u32[]{:S(2)}) %collective-permute-start.6) | collective-permute-done | bytes 1376288 | tf_op jit(solution)/shard_map/ppermute | solution.py:460
  130.6 33.3 %gate_up.4 = (f32[2048,3584]{1,0:T(8,128)}, f32[2048,3584]{1,0:T(8,128)}, bf16[2048,3584]{1,0:T(8,128)(2,1)}, bf16[1536,3584]{1,0:T(8,128)(2,1)}, bf16[1536,3584]{1,0:T(8,128)(2,1)}) custom-call(s32[5]{0:T(128)} %stack.62.at, bf16[2048,1536]{1,0:T(8,128)(2,1)} %get-tuple-element.72.a, bf16[2,384,3584]{2,1,0:T(8,128)(2,1)} %refs_0_.7, ...), custom_call_target="tpu_custom_call" | custom-call | flops 22548578304 | bytes 47710208 | tf_op jit(solution)/shard_map/gate_up/pallas_call | solution.py:181
  168.4 28.0 %collective-permute-done.12.ry = bf16[448,1536]{1,0:T(8,128)(2,1)} collective-permute-done((bf16[448,1536]{1,0:T(8,128)(2,1)}, bf16[448,1536]{1,0:T(8,128)(2,1)}, u32[]{:S(2)}, u32[]{:S(2)}) %collective-permute-start.12) | collective-permute-done | bytes 1376288 | tf_op jit(solution)/shard_map/ppermute | solution.py:460
  196.4 33.3 %gate_up.5 = (f32[2048,3584]{1,0:T(8,128)}, f32[2048,3584]{1,0:T(8,128)}, bf16[2048,3584]{1,0:T(8,128)(2,1)}, bf16[1536,3584]{1,0:T(8,128)(2,1)}, bf16[1536,3584]{1,0:T(8,128)(2,1)}) custom-call(s32[5]{0:T(128)} %stack.60.at, bf16[2048,1536]{1,0:T(8,128)(2,1)} %get-tuple-element.72.a, ...), custom_call_target="tpu_custom_call", output_to_operand_aliasing={{0}: (10, {}), {1}: (11, {}), {2}: (12, {}), {3}: (13, {}),... | custom-call | flops 22548578304 | bytes 47710208 | tf_op jit(solution)/shard_map/gate_up/pallas_call | solution.py:181
  241.2 33.5 %shard_map.180 = (bf16[2048,1536]{1,0:T(8,128)(2,1)}, bf16[2048,1536]{1,0:T(8,128)(2,1)}, bf16[1536,2048]{1,0:T(8,128)(2,1)}) custom-call(bf16[2048,3584]{1,0:T(8,128)(2,1)} %get-tuple-element.107.hidden.right, bf16[3584,1536]{1,0:T(8,128)(2,1)} %assemble.2.w, bf16[2048,1536]{1,0:T(8,128)(2,1)} %bitcast.36), custom_call_target="tpu_custom_call" | custom-call | flops 22548578304 | bytes 25690112 | tf_op jit(solution)/shard_map/pallas_call | solution.py:210
  276.2 30.8 %collective-permute-done.19.refs_6_ = bf16[384,1792]{1,0:T(8,128)(2,1)} collective-permute-done((bf16[384,1792]{1,0:T(8,128)(2,1)}, bf16[384,1792]{1,0:T(8,128)(2,1)}, u32[]{:S(2)}, u32[]{:S(2)}) %collective-permute-start.19) | collective-permute-done | bytes 1376288 | tf_op jit(solution)/shard_map/ppermute | solution.py:460
  307.1 33.8 %gate_up.6 = (f32[2048,3584]{1,0:T(8,128)}, f32[2048,3584]{1,0:T(8,128)}, bf16[2048,3584]{1,0:T(8,128)(2,1)}, bf16[1536,3584]{1,0:T(8,128)(2,1)}, bf16[1536,3584]{1,0:T(8,128)(2,1)}) custom-call(s32[5]{0:T(128)} %stack.62.at, bf16[2048,1536]{1,0:T(8,128)(2,1)} %get-tuple-element.80.a, bf16[2,384,3584]{2,1,0:T(8,128)(2,1)} %refs_0_.7, ...), custom_call_target="tpu_custom_call" | custom-call | flops 22548578304 | bytes 47710208 | tf_op jit(solution)/shard_map/gate_up/pallas_call | solution.py:181
  341.4 33.3 %gate_up.7 = (f32[2048,3584]{1,0:T(8,128)}, f32[2048,3584]{1,0:T(8,128)}, bf16[2048,3584]{1,0:T(8,128)(2,1)}, bf16[1536,3584]{1,0:T(8,128)(2,1)}, bf16[1536,3584]{1,0:T(8,128)(2,1)}) custom-call(s32[5]{0:T(128)} %stack.60.at, bf16[2048,1536]{1,0:T(8,128)(2,1)} %get-tuple-element.80.a, ...), custom_call_target="tpu_custom_call", output_to_operand_aliasing={{0}: (10, {}), {1}: (11, {}), {2}: (12, {}), {3}: (13, {}),... | custom-call | flops 22548578304 | bytes 47710208 | tf_op jit(solution)/shard_map/gate_up/pallas_call | solution.py:181
  375.0 34.7 %term_columns.2 = (bf16[1536,896]{1,0:T(8,128)(2,1)}, f32[1536,896]{1,0:T(8,128)}) custom-call(bf16[1536,2048]{1,0:T(8,128)(2,1)} %shard_map.179.left, bf16[2048,3584]{1,0:T(8,128)(2,1)} %get-tuple-element.89.right), custom_call_target="tpu_custom_call" | custom-call | flops 22548578304 | bytes 31981568 | tf_op jit(solution)/shard_map/term_columns/pallas_call | solution.py:390
  418.3 44.3 %shard_map.181 = (bf16[2048,3584]{1,0:T(8,128)(2,1)}, bf16[2048,3584]{1,0:T(8,128)(2,1)}) custom-call(bf16[2048,1536]{1,0:T(8,128)(2,1)} %bitcast.33, bf16[3584,1536]{1,0:T(8,128)(2,1)} %assemble.3.w, f32[2048,3584]{1,0:T(8,128)} %get-tuple-element.93.gate, f32[2048,3584]{1,0:T(8,128)} %get-tuple-element.94.up), custom_call_target="tpu_custom_call" | custom-call | flops 22548578304 | bytes 88080384 | tf_op jit(solution)/shard_map/pallas_call | solution.py:233
  462.6 33.1 %term_rows.4 = (bf16[384,3584]{1,0:T(8,128)(2,1)}, f32[384,3584]{1,0:T(8,128)}) custom-call(bf16[1536,2048]{1,0:T(8,128)(2,1)} %get-tuple-element.96.left, bf16[2048,3584]{1,0:T(8,128)(2,1)} %get-tuple-element.102.right.dg), custom_call_target="tpu_custom_call" | custom-call | flops 22548578304 | bytes 31981568 | tf_op jit(solution)/shard_map/term_rows/pallas_call | solution.py:313
  497.5 32.6 %term_rows.5 = (bf16[384,3584]{1,0:T(8,128)(2,1)}, f32[384,3584]{1,0:T(8,128)}) custom-call(bf16[1536,2048]{1,0:T(8,128)(2,1)} %get-tuple-element.96.left, bf16[2048,3584]{1,0:T(8,128)(2,1)} %get-tuple-element.100.right.du), custom_call_target="tpu_custom_call" | custom-call | flops 22548578304 | bytes 31981568 | tf_op jit(solution)/shard_map/term_rows/pallas_call | solution.py:313
  530.4 55.0 %shard_map.182.by_a = bf16[2048,1536]{1,0:T(8,128)(2,1)} custom-call(bf16[2048,3584]{1,0:T(8,128)(2,1)} %get-tuple-element.102.right.dg, bf16[2048,3584]{1,0:T(8,128)(2,1)} %get-tuple-element.100.right.du, bf16[1536,3584]{1,0:T(8,128)(2,1)} %get-tuple-element.103.wg, bf16[1536,3584]{1,0:T(8,128)(2,1)} %get-tuple-element.104.wu), custom_call_target="tpu_custom_call" | custom-call | flops 45097156608 | bytes 73400320 | tf_op jit(solution)/shard_map/pallas_call | solution.py:251
  585.4 15.1 %shard_map.183 = (bf16[2048,1536]{1,0:T(8,128)(2,1)}, bf16[1536,2048]{1,0:T(8,128)(2,1)}) custom-call(bf16[2048,1536]{1,0:T(8,128)(2,1)} %shard_map.182.by_a, bf16[2048,1536]{1,0:T(8,128)(2,1)} %get-tuple-element.82.h, bf16[2048,1536]{1,0:T(8,128)(2,1)} %bitcast.34), custom_call_target="tpu_custom_call" | custom-call | flops 1000000000 | bytes 31457280 | tf_op jit(solution)/shard_map/pallas_call | solution.py:125
  600.6 34.6 %term_columns.3 = (bf16[1536,896]{1,0:T(8,128)(2,1)}, f32[1536,896]{1,0:T(8,128)}) custom-call(bf16[1536,2048]{1,0:T(8,128)(2,1)} %get-tuple-element.106.left, bf16[2048,3584]{1,0:T(8,128)(2,1)} %get-tuple-element.107.hidden.right), custom_call_target="tpu_custom_call" | custom-call | flops 22548578304 | bytes 31981568 | tf_op jit(solution)/shard_map/term_columns/pallas_call | solution.py:390
  636.9 44.3 %shard_map.184 = (bf16[2048,3584]{1,0:T(8,128)(2,1)}, bf16[2048,3584]{1,0:T(8,128)(2,1)}) custom-call(bf16[2048,1536]{1,0:T(8,128)(2,1)} %get-tuple-element.109.dy, bf16[3584,1536]{1,0:T(8,128)(2,1)} %assemble.2.w, f32[2048,3584]{1,0:T(8,128)} %get-tuple-element.110.gate, f32[2048,3584]{1,0:T(8,128)} %get-tuple-element.111.up), custom_call_target="tpu_custom_call" | custom-call | flops 22548578304 | bytes 88080384 | tf_op jit(solution)/shard_map/pallas_call | solution.py:233
  681.1 33.3 %term_rows.6 = (bf16[384,3584]{1,0:T(8,128)(2,1)}, f32[384,3584]{1,0:T(8,128)}) custom-call(bf16[1536,2048]{1,0:T(8,128)(2,1)} %get-tuple-element.70.left, bf16[2048,3584]{1,0:T(8,128)(2,1)} %get-tuple-element.112.right), custom_call_target="tpu_custom_call" | custom-call | flops 22548578304 | bytes 31981568 | tf_op jit(solution)/shard_map/term_rows/pallas_call | solution.py:313
  714.9 32.6 %term_rows.7 = (bf16[384,3584]{1,0:T(8,128)(2,1)}, f32[384,3584]{1,0:T(8,128)}) custom-call(bf16[1536,2048]{1,0:T(8,128)(2,1)} %get-tuple-element.70.left, bf16[2048,3584]{1,0:T(8,128)(2,1)} %get-tuple-element.122.right), custom_call_target="tpu_custom_call" | custom-call | flops 22548578304 | bytes 31981568 | tf_op jit(solution)/shard_map/term_rows/pallas_call | solution.py:313
  789.0 46.8 %collective-permute-done.32 = bf16[384,3584]{1,0:T(8,128)(2,1)} collective-permute-done((bf16[384,3584]{1,0:T(8,128)(2,1)}, bf16[384,3584]{1,0:T(8,128)(2,1)}, u32[]{:S(2)}, u32[]{:S(2)}) %collective-permute-start.32) | collective-permute-done | bytes 2752544 | tf_op jit(solution)/shard_map/ppermute | solution.py:502
  850.5 22.2 %fusion.8 = (bf16[2,896,1536]{2,1,0:T(8,128)(2,1)}, f32[2,896,1536]{2,1,0:T(8,128)}, f32[2,896,1536]{2,1,0:T(8,128)}) fusion(bf16[2,896,1536]{2,1,0:T(8,128)(2,1)} %own.3, f32[]{:T(128)S(6)} %min_shard_map.3, bf16[1,896,1536]{2,1,0:T(8,128)(2,1)} %bitcast.37, bf16[1,896,1536]{2,1,0:T(8,128)(2,1)} %bitcast.38, f32[2,896,1536]{2,1,0:T(8,128)} %param.21, ...), kind=kLoop, calls=%fused_computation.17 | loop fusion | flops 55050240 | bytes 60555268 | tf_op jit(solution)/shard_map/convert_element_type | solution.py:27
  872.7 36.7 %fusion.2 = (bf16[2,384,3584]{2,1,0:T(8,128)(2,1)}, f32[2,384,3584]{2,1,0:T(8,128)}, f32[2,384,3584]{2,1,0:T(8,128)}, bf16[2,384,3584]{2,1,0:T(8,128)(2,1)}, f32...) fusion(bf16[2,384,3584]{2,1,0:T(8,128)(2,1)} %refs_0_.7, f32[]{:T(128)S(6)} %min_shard_map.3, ...), kind=kLoop, calls=%fused_computation.11 | loop fusion | flops 110100480 | bytes 121110528 | tf_op jit(solution)/shard_map/convert_element_type | solution.py:27
  (79 shorter events, 117.1 us)
Async XLA Ops:
  0.6 129.4 %collective-permute-start = (bf16[2,384,3584]{2,1,0:T(8,128)(2,1)}, bf16[2,384,3584]{2,1,0:T(8,128)(2,1)}, u32[]{:S(2)}, u32[]{:S(2)}) collective-permute-start(bf16[2,384,3584]{2,1,0:T(8,128)(2,1)} %refs_0_.7), channel_id=1, source_target_pairs={{0,1},{1,0},{2,3},{3,2},{4,5},{5,4},{6,7},{7,6}} | collective-permute-start | bytes 16515080 | tf_op jit(solution)/shard_map/ppermute | solution.py:438
  1.5 129.1 %collective-permute-start.4 = (bf16[2,384,3584]{2,1,0:T(8,128)(2,1)}, bf16[2,384,3584]{2,1,0:T(8,128)(2,1)}, u32[]{:S(2)}, u32[]{:S(2)}) collective-permute-start(bf16[2,384,3584]{2,1,0:T(8,128)(2,1)} %refs_4_.7), channel_id=1, source_target_pairs={{0,1},{1,0},{2,3},{3,2},{4,5},{5,4},{6,7},{7,6}} | collective-permute-start | bytes 16515080 | tf_op jit(solution)/shard_map/ppermute | solution.py:438
  8.9 58.7 %collective-permute-start.5 = (bf16[384,1792]{1,0:T(8,128)(2,1)S(1)}, bf16[384,1792]{1,0:T(8,128)(2,1)}, u32[]{:S(2)}, u32[]{:S(2)}) collective-permute-start(bf16[384,1792]{1,0:T(8,128)(2,1)S(1)} %get-tuple-element.147), channel_id=1, source_target_pairs={{0,2},{2,0},{1,3},{3,1},{4,6},{6,4},{5,7},{7,5}} | collective-permute-start | bytes 4128776 | tf_op jit(solution)/shard_map/ppermute | solution.py:446
  69.4 60.7 %collective-permute-start.6 = (bf16[384,1792]{1,0:T(8,128)(2,1)}, bf16[384,1792]{1,0:T(8,128)(2,1)}, u32[]{:S(2)}, u32[]{:S(2)}) collective-permute-start(bf16[384,1792]{1,0:T(8,128)(2,1)} %collective-permute-done.5.refs_6_), channel_id=1, source_target_pairs={{0,4},{4,0},{1,5},{5,1},{2,6},{6,2},{3,7},{7,3}} | collective-permute-start | bytes 4128776 | tf_op jit(solution)/shard_map/ppermute | solution.py:460
  92.5 140.5 %collective-permute-start.10 = (bf16[2,896,1536]{2,1,0:T(8,128)(2,1)}, bf16[2,896,1536]{2,1,0:T(8,128)(2,1)}, u32[]{:S(2)}, u32[]{:S(2)}) collective-permute-start(bf16[2,896,1536]{2,1,0:T(8,128)(2,1)} %own.3), channel_id=1, source_target_pairs={{0,1},{1,0},{2,3},{3,2},{4,5},{5,4},{6,7},{7,6}} | collective-permute-start | bytes 16515080 | tf_op jit(solution)/shard_map/ppermute | solution.py:438
  101.0 62.9 %collective-permute-start.11 = (bf16[448,1536]{1,0:T(8,128)(2,1)}, bf16[448,1536]{1,0:T(8,128)(2,1)}, u32[]{:S(2)}, u32[]{:S(2)}) collective-permute-start(bf16[448,1536]{1,0:T(8,128)(2,1)} %get-tuple-element.145), channel_id=1, source_target_pairs={{0,2},{2,0},{1,3},{3,1},{4,6},{6,4},{5,7},{7,5}} | collective-permute-start | bytes 4128776 | tf_op jit(solution)/shard_map/ppermute | solution.py:446
  130.1 37.8 %collective-permute-start.3 = (bf16[384,1792]{1,0:T(8,128)(2,1)}, bf16[384,1792]{1,0:T(8,128)(2,1)}, u32[]{:S(2)}, u32[]{:S(2)}) collective-permute-start(bf16[384,1792]{1,0:T(8,128)(2,1)} %collective-permute-done.2.refs_2_), channel_id=1, source_target_pairs={{0,1},{1,0},{2,3},{3,2},{4,5},{5,4},{6,7},{7,6}} | collective-permute-start | bytes 4128776 | tf_op jit(solution)/shard_map/ppermute | solution.py:461
  130.1 38.3 %collective-permute-start.7 = (bf16[384,1792]{1,0:T(8,128)(2,1)}, bf16[384,1792]{1,0:T(8,128)(2,1)}, u32[]{:S(2)}, u32[]{:S(2)}) collective-permute-start(bf16[384,1792]{1,0:T(8,128)(2,1)} %collective-permute-done.6.refs_6_), channel_id=1, source_target_pairs={{0,1},{1,0},{2,3},{3,2},{4,5},{5,4},{6,7},{7,6}} | collective-permute-start | bytes 4128776 | tf_op jit(solution)/shard_map/ppermute | solution.py:461
  165.7 110.0 %collective-permute-start.23 = (bf16[448,1536]{1,0:T(8,128)(2,1)}, bf16[448,1536]{1,0:T(8,128)(2,1)}, u32[]{:S(2)}, u32[]{:S(2)}) collective-permute-start(bf16[448,1536]{1,0:T(8,128)(2,1)} %get-tuple-element.144), channel_id=1, source_target_pairs={{0,2},{2,0},{1,3},{3,1},{4,6},{6,4},{5,7},{7,5}} | collective-permute-start | bytes 4128776 | tf_op jit(solution)/shard_map/ppermute | solution.py:446
  167.8 61.9 %collective-permute-start.15 = (bf16[384,1792]{1,0:T(8,128)(2,1)}, bf16[384,1792]{1,0:T(8,128)(2,1)}, u32[]{:S(2)}, u32[]{:S(2)}) collective-permute-start(bf16[384,1792]{1,0:T(8,128)(2,1)} %get-tuple-element.148), channel_id=1, source_target_pairs={{0,2},{2,0},{1,3},{3,1},{4,6},{6,4},{5,7},{7,5}} | collective-permute-start | bytes 4128776 | tf_op jit(solution)/shard_map/ppermute | solution.py:446
  168.4 63.1 %collective-permute-start.13 = (bf16[448,1536]{1,0:T(8,128)(2,1)}, bf16[448,1536]{1,0:T(8,128)(2,1)}, u32[]{:S(2)}, u32[]{:S(2)}) collective-permute-start(bf16[448,1536]{1,0:T(8,128)(2,1)} %collective-permute-done.11.rx), channel_id=1, source_target_pairs={{0,1},{1,0},{2,3},{3,2},{4,5},{5,4},{6,7},{7,6}} | collective-permute-start | bytes 4128776 | tf_op jit(solution)/shard_map/ppermute | solution.py:454
  196.4 36.6 %collective-permute-start.14 = (bf16[448,1536]{1,0:T(8,128)(2,1)}, bf16[448,1536]{1,0:T(8,128)(2,1)}, u32[]{:S(2)}, u32[]{:S(2)}) collective-permute-start(bf16[448,1536]{1,0:T(8,128)(2,1)} %collective-permute-done.12.ry), channel_id=1, source_target_pairs={{0,1},{1,0},{2,3},{3,2},{4,5},{5,4},{6,7},{7,6}} | collective-permute-start | bytes 4128776 | tf_op jit(solution)/shard_map/ppermute | solution.py:461
  229.7 45.0 %collective-permute-start.18 = (bf16[384,1792]{1,0:T(8,128)(2,1)}, bf16[384,1792]{1,0:T(8,128)(2,1)}, u32[]{:S(2)}, u32[]{:S(2)}) collective-permute-start(bf16[384,1792]{1,0:T(8,128)(2,1)} %get-tuple-element.146), channel_id=1, source_target_pairs={{0,2},{2,0},{1,3},{3,1},{4,6},{6,4},{5,7},{7,5}} | collective-permute-start | bytes 4128776 | tf_op jit(solution)/shard_map/ppermute | solution.py:446
  231.5 44.3 %collective-permute-start.16 = (bf16[384,1792]{1,0:T(8,128)(2,1)}, bf16[384,1792]{1,0:T(8,128)(2,1)}, u32[]{:S(2)}, u32[]{:S(2)}) collective-permute-start(bf16[384,1792]{1,0:T(8,128)(2,1)} %collective-permute-done.15.refs_2_), channel_id=1, source_target_pairs={{0,4},{4,0},{1,5},{5,1},{2,6},{6,2},{3,7},{7,3}} | collective-permute-start | bytes 4128776 | tf_op jit(solution)/shard_map/ppermute | solution.py:460
  275.7 134.4 %collective-permute-start.25 = (bf16[448,1536]{1,0:T(8,128)(2,1)}, bf16[448,1536]{1,0:T(8,128)(2,1)}, u32[]{:S(2)}, u32[]{:S(2)}) collective-permute-start(bf16[448,1536]{1,0:T(8,128)(2,1)} %collective-permute-done.23.rx), channel_id=1, source_target_pairs={{0,1},{1,0},{2,3},{3,2},{4,5},{5,4},{6,7},{7,6}} | collective-permute-start | bytes 4128776 | tf_op jit(solution)/shard_map/ppermute | solution.py:454
  275.7 65.7 %collective-permute-start.17 = (bf16[384,1792]{1,0:T(8,128)(2,1)}, bf16[384,1792]{1,0:T(8,128)(2,1)}, u32[]{:S(2)}, u32[]{:S(2)}) collective-permute-start(bf16[384,1792]{1,0:T(8,128)(2,1)} %collective-permute-done.16.refs_2_), channel_id=1, source_target_pairs={{0,1},{1,0},{2,3},{3,2},{4,5},{5,4},{6,7},{7,6}} | collective-permute-start | bytes 4128776 | tf_op jit(solution)/shard_map/ppermute | solution.py:461
  307.0 34.4 %collective-permute-start.20 = (bf16[384,1792]{1,0:T(8,128)(2,1)}, bf16[384,1792]{1,0:T(8,128)(2,1)}, u32[]{:S(2)}, u32[]{:S(2)}) collective-permute-start(bf16[384,1792]{1,0:T(8,128)(2,1)} %collective-permute-done.19.refs_6_), channel_id=1, source_target_pairs={{0,1},{1,0},{2,3},{3,2},{4,5},{5,4},{6,7},{7,6}} | collective-permute-start | bytes 4128776 | tf_op jit(solution)/shard_map/ppermute | solution.py:461
  374.8 35.3 %collective-permute-start.26 = (bf16[448,1536]{1,0:T(8,128)(2,1)}, bf16[448,1536]{1,0:T(8,128)(2,1)}, u32[]{:S(2)}, u32[]{:S(2)}) collective-permute-start(bf16[448,1536]{1,0:T(8,128)(2,1)} %collective-permute-done.24.ry), channel_id=1, source_target_pairs={{0,1},{1,0},{2,3},{3,2},{4,5},{5,4},{6,7},{7,6}} | collective-permute-start | bytes 4128776 | tf_op jit(solution)/shard_map/ppermute | solution.py:461
  409.7 337.8 %collective-permute-start.29 = (bf16[1536,896]{1,0:T(8,128)(2,1)}, bf16[1536,896]{1,0:T(8,128)(2,1)}, u32[]{:S(2)}, u32[]{:S(2)}) collective-permute-start(bf16[1536,896]{1,0:T(8,128)(2,1)} %get-tuple-element.90), channel_id=1, source_target_pairs={{0,2},{2,0},{1,3},{3,1},{4,6},{6,4},{5,7},{7,5}} | collective-permute-start | bytes 8257544 | tf_op jit(solution)/shard_map/ppermute | solution.py:502
  495.8 261.3 %collective-permute-start.28 = (bf16[384,3584]{1,0:T(8,128)(2,1)}, bf16[384,3584]{1,0:T(8,128)(2,1)}, u32[]{:S(2)}, u32[]{:S(2)}) collective-permute-start(bf16[384,3584]{1,0:T(8,128)(2,1)} %get-tuple-element.99), channel_id=1, source_target_pairs={{0,2},{2,0},{1,3},{3,1},{4,6},{6,4},{5,7},{7,5}} | collective-permute-start | bytes 8257544 | tf_op jit(solution)/shard_map/ppermute | solution.py:502
  530.1 235.2 %collective-permute-start.30 = (bf16[384,3584]{1,0:T(8,128)(2,1)}, bf16[384,3584]{1,0:T(8,128)(2,1)}, u32[]{:S(2)}, u32[]{:S(2)}) collective-permute-start(bf16[384,3584]{1,0:T(8,128)(2,1)} %get-tuple-element.101), channel_id=1, source_target_pairs={{0,2},{2,0},{1,3},{3,1},{4,6},{6,4},{5,7},{7,5}} | collective-permute-start | bytes 8257544 | tf_op jit(solution)/shard_map/ppermute | solution.py:502
  635.1 137.7 %collective-permute-start.31 = (bf16[1536,896]{1,0:T(8,128)(2,1)}, bf16[1536,896]{1,0:T(8,128)(2,1)}, u32[]{:S(2)}, u32[]{:S(2)}) collective-permute-start(bf16[1536,896]{1,0:T(8,128)(2,1)} %get-tuple-element.108), channel_id=1, source_target_pairs={{0,2},{2,0},{1,3},{3,1},{4,6},{6,4},{5,7},{7,5}} | collective-permute-start | bytes 8257544 | tf_op jit(solution)/shard_map/ppermute | solution.py:502
  714.5 66.9 %collective-permute-start.27 = (bf16[384,3584]{1,0:T(8,128)(2,1)}, bf16[384,3584]{1,0:T(8,128)(2,1)}, u32[]{:S(2)}, u32[]{:S(2)}) collective-permute-start(bf16[384,3584]{1,0:T(8,128)(2,1)} %get-tuple-element.114), channel_id=1, source_target_pairs={{0,2},{2,0},{1,3},{3,1},{4,6},{6,4},{5,7},{7,5}} | collective-permute-start | bytes 8257544 | tf_op jit(solution)/shard_map/ppermute | solution.py:502
  747.6 88.2 %collective-permute-start.32 = (bf16[384,3584]{1,0:T(8,128)(2,1)}, bf16[384,3584]{1,0:T(8,128)(2,1)}, u32[]{:S(2)}, u32[]{:S(2)}) collective-permute-start(bf16[384,3584]{1,0:T(8,128)(2,1)} %get-tuple-element.124), channel_id=1, source_target_pairs={{0,2},{2,0},{1,3},{3,1},{4,6},{6,4},{5,7},{7,5}} | collective-permute-start | bytes 8257544 | tf_op jit(solution)/shard_map/ppermute | solution.py:502
  (11 other events, 313.6 us)

commit v3 on v2

--- a/solution.py
+++ b/solution.py
@@ -128,11 +128,11 @@
     )(*arrays)
 
 
-def gate_up_kernel(number, width, at, a, *refs):
-    sources, outs, (buf, sem) = (refs[:4], refs[4:8]), refs[-7:-2], refs[-2:]
-    gate, up, hidden, wg, wu = outs
+def gate_up_kernel(number, width, outputs, at, a, *refs):
+    sources, outs, (buf, sem) = (refs[:4], refs[4:8]), refs[-2 - outputs : -2], refs[-2:]
+    by_gate, by_up, hidden = outs[:3]
     t = pl.program_id(0)
-    tile = gate.shape[1]
+    tile = hidden.shape[1]
     rows = buf.shape[2] // 4
     here = lambda first: pl.ds(pl.multiple_of(first, 128), tile)
 
@@ -161,13 +161,15 @@
     for one in copies(t):
         one.wait()
     slot = lax.rem(t, 2)
-    wg[...] = buf[slot, 0]
-    wu[...] = buf[slot, 1]
+    for p, whole in enumerate(outs[3:]):
+        whole[...] = buf[slot, p]
     g = jnp.dot(a[...], buf[slot, 0], preferred_element_type=F32)
     u = jnp.dot(a[...], buf[slot, 1], preferred_element_type=F32)
-    gate[...] = g
-    up[...] = u
-    hidden[...] = (jax.nn.silu(g) * u).astype(BF16)
+    s = jax.nn.sigmoid(g)
+    silu = g * s
+    by_gate[...] = u * (s + silu * (1 - s))
+    by_up[...] = silu
+    hidden[...] = (silu * u).astype(BF16)
 
 
 def gate_up(number, at, a, gates, ups, before=()):
@@ -179,13 +181,13 @@
     place = lambda t, at: (0, at[4] * tiles + t)
     out, w = pl.BlockSpec((m, bn), place), pl.BlockSpec((k, bn), place)
     return pl.pallas_call(
-        functools.partial(gate_up_kernel, number, width),
-        out_shape=[shaped((m, n), F32), shaped((m, n), F32), shaped((m, n)), shaped((k, n)), shaped((k, n))],
+        functools.partial(gate_up_kernel, number, width, 5 if number else 3),
+        out_shape=[shaped((m, n), F32), shaped((m, n), F32), shaped((m, n))] + [shaped((k, n))] * (2 if number else 0),
         grid_spec=pltpu.PrefetchScalarGridSpec(
             num_scalar_prefetch=1,
             grid=(tiles,),
             in_specs=[resident((m, k))] + [any_space] * (8 + len(before)),
-            out_specs=[out] * 3 + [w] * 2,
+            out_specs=[out] * 3 + [w] * (2 if number else 0),
             scratch_shapes=[pltpu.VMEM((2, 2, k, bn), BF16), pltpu.SemaphoreType.DMA((2, 2, 4))],
         ),
         input_output_aliases={10 + i: i for i in range(len(before))},
@@ -219,11 +221,8 @@
 
 def by_hidden_kernel(dy, w, gate, up, dg, du):
     by = lax.dot_general(dy[...], w[...], NT, preferred_element_type=F32).astype(BF16).astype(F32)
-    g, u = gate[...], up[...]
-    s = jax.nn.sigmoid(g)
-    silu = g * s
-    dg[...] = (by * u * (s + silu * (1 - s))).astype(BF16)
-    du[...] = (by * silu).astype(BF16)
+    dg[...] = (by * gate[...]).astype(BF16)
+    du[...] = (by * up[...]).astype(BF16)
 
 
 def by_hidden(dy, w, gate, up, bm=2048, bn=512):
@@ -269,24 +268,25 @@
     pl.semaphore_wait(barrier, 1)
 
 
-def term_rows_kernel(left, right, send, own, full, there, send_sem, recv_sem):
+def term_rows_kernel(left, right, send, kept, three, full, there, send_sem, recv_sem):
     d = lax.axis_index("dp")
-    own_i, core_i, x_i, xc_i = others(d)
+    _, core_i, x_i, xc_i = others(d)
     rows, tile = send.shape
     tiles = full.shape[1] // tile
     j = pl.program_id(0)
     cols = lambda k: pl.ds(pl.multiple_of(k * tile, tile), tile)
-    at = lambda i: pl.ds(pl.multiple_of(i * rows, rows), rows)
 
     def copies(k):
         return [
-            exchange(d, full.at[at(i), cols(k)], there.at[n, :, cols(k)], send_sem.at[n, k], recv_sem.at[n, k])
-            for n, i in enumerate((core_i, xc_i))
+            exchange(d, full.at[pl.ds(n * rows, rows), cols(k)], there.at[n, :, cols(k)], send_sem.at[n, k], recv_sem.at[n, k])
+            for n in range(2)
         ]
 
     @pl.when(j == 0)
     def _():
         greet(d)
+        for n, i in enumerate((core_i, xc_i, x_i)):
+            three[pl.ds(n * rows, rows), :] = left[pl.ds(pl.multiple_of(i * rows, rows), rows), :]
 
     @pl.when((j >= 1) & (j <= tiles))
     def _():
@@ -295,15 +295,15 @@
 
     @pl.when(j < tiles)
     def _():
-        full[:, cols(j)] = jnp.dot(left[...], right[...], preferred_element_type=F32).astype(BF16)
+        full[:, cols(j)] = jnp.dot(three[...], right[...], preferred_element_type=F32).astype(BF16)
 
     @pl.when(j >= 2)
     def _():
         k = j - 2
         for one in copies(k):
             one.wait()
-        own[...] = full[at(own_i), cols(k)].astype(F32) + there[0, :, cols(k)].astype(F32)
-        send[...] = (full[at(x_i), cols(k)].astype(F32) + there[1, :, cols(k)].astype(F32)).astype(BF16)
+        kept[...] = there[0, :, cols(k)]
+        send[...] = (full[pl.ds(2 * rows, rows), cols(k)].astype(F32) + there[1, :, cols(k)].astype(F32)).astype(BF16)
 
 
 def term_rows(left, right):
@@ -312,15 +312,68 @@
     out = pl.BlockSpec((rows, TILE), lambda j: (0, jnp.maximum(j - 2, 0)))
     return pl.pallas_call(
         term_rows_kernel,
-        out_shape=[shaped((rows, n)), shaped((rows, n), F32)],
+        out_shape=[shaped((rows, n)), shaped((rows, n))],
         grid=(tiles + 2,),
         in_specs=[resident((m, k)), pl.BlockSpec((k, TILE), lambda j: (0, jnp.minimum(j, tiles - 1)))],
         out_specs=[out, out],
-        scratch_shapes=[pltpu.VMEM((m, n), BF16), pltpu.VMEM((2, rows, n), BF16), pltpu.SemaphoreType.DMA((2, tiles)), pltpu.SemaphoreType.DMA((2, tiles))],
+        scratch_shapes=[
+            pltpu.VMEM((3 * rows, k), BF16),
+            pltpu.VMEM((3 * rows, n), BF16),
+            pltpu.VMEM((2, rows, n), BF16),
+            pltpu.SemaphoreType.DMA((2, tiles)),
+            pltpu.SemaphoreType.DMA((2, tiles)),
+        ],
         compiler_params=pltpu.CompilerParams(vmem_limit_bytes=VMEM, collective_id=0, has_side_effects=True),
-        cost_estimate=pl.CostEstimate(flops=2 * m * n * k, bytes_accessed=2 * (m * k + k * n + m * n), transcendentals=0),
+        cost_estimate=pl.CostEstimate(flops=3 * m * n * k // 2, bytes_accessed=2 * (m * k + k * n + m * n), transcendentals=0),
         name="term_rows",
     )(left, right)
+
+
+def count(squares, g):
+    @pl.when(pl.program_id(0) == 0)
+    def _():
+        squares[0, 0] = 0.0
+
+    squares[0, 0] += jnp.sum(g * g)
+
+
+def own_rows_kernel(at, left, right, kept, out):
+    out[...] = jnp.dot(left[...], right[...], preferred_element_type=F32) + kept[...].astype(F32)
+
+
+def own_rows_end_kernel(at, left, right, kept, arrived, out, squares):
+    total = jnp.dot(left[...], right[...], preferred_element_type=F32) + kept[...].astype(F32)
+    g = (total + arrived[...].astype(F32)).astype(BF16)
+    out[...] = g
+    count(squares, g.astype(F32))
+
+
+def own_rows(at, left, right, kept, arrived=None):
+    m, k = left.shape
+    n, rows = right.shape[1], m // 4
+    out = pl.BlockSpec((rows, TILE), lambda j, at: (0, j))
+    ins = [pl.BlockSpec((rows, k), lambda j, at: (at[0], 0)), pl.BlockSpec((k, TILE), lambda j, at: (0, j)), out]
+    if arrived is None:
+        return call(own_rows_kernel, shaped((rows, n), F32), (n // TILE,), ins, out, 2 * rows * n * k, 2 * k * n, at)(at, left, right, kept)
+    return call(
+        own_rows_end_kernel, [shaped((rows, n)), shaped((1, 1), F32)], (n // TILE,), ins + [out],
+        [out, pl.BlockSpec(memory_space=pltpu.SMEM)], 2 * rows * n * k, 2 * k * n, at,
+    )(at, left, right, kept, arrived)
+
+
+def ended_kernel(own, arrived, out, squares):
+    g = (own[...] + arrived[...].astype(F32)).astype(BF16)
+    out[...] = g
+    count(squares, g.astype(F32))
+
+
+def ended(own, arrived):
+    m, n = own.shape
+    spec = pl.BlockSpec((m, TILE), lambda j: (0, j))
+    return call(
+        ended_kernel, [shaped((m, n)), shaped((1, 1), F32)], (n // TILE,), [spec, spec], [spec, pl.BlockSpec(memory_space=pltpu.SMEM)],
+        4 * m * n, 8 * m * n,
+    )(own, arrived)
 
 
 def term_columns_kernel(left, right, send, own, full, there, send_sem, recv_sem):
@@ -402,12 +455,7 @@
 
 def turned_kernel(own, arrived, out, squares):
     g = (own[...] + arrived[...].astype(F32)).astype(BF16).astype(F32)
-
-    @pl.when(pl.program_id(0) == 0)
-    def _():
-        squares[0, 0] = 0.0
-
-    squares[0, 0] += jnp.sum(g * g)
+    count(squares, g)
     out[...] = g.T.astype(BF16)
 
 
@@ -425,7 +473,7 @@
         cost_estimate=pl.CostEstimate(flops=4 * m * n, bytes_accessed=8 * m * n, transcendentals=0),
         name="turned",
     )(own, arrived)
-    return g, squares[0, 0]
+    return g, squares
 
 
 def solution(mesh):
@@ -483,23 +531,23 @@
             return outs, [(weights[i], from_core[i], *second(i, number, *behind[i])) for i in (0, 1)]
 
         a0, a0_t = by_rows(norm_kernel, " t", x[0])
-        (dy_t,) = by_rows(turn_kernel, "t", dy[0])
+        (dy_t,) = by_rows(turn_kernel, "t", lax.optimization_barrier((dy[0], a0, halves[0, 0]))[0])
         a0, a0_t, dy_t = lax.optimization_barrier((a0, a0_t, dy_t))
         outs, arrived = ab(0, a0, ((), ()))
         w_down0 = whole_down(0, outs[2])
-        gate0, up0, hidden0, _, _ = gate_up(0, at_b, a0, *arrived, outs)
+        gate0, up0, hidden0 = gate_up(0, at_b, a0, *arrived, outs)
         h1, a1, a1_t = down(hidden0, w_down0, x[0])
         outs, arrived = ab(1, a1, ((hidden0,), (h1,)))
         w_down1 = whole_down(1, outs[2])
         gate1, up1, hidden1, w_gate1, w_up1 = gate_up(1, at_b, a1, *arrived, outs)
         noted(hidden1)
 
-        mine, late = [[None] * 3 for _ in range(layers)], []
+        mine, late = [[None] * 3 for _ in range(layers)], {}
 
         def term(i, number, kernel, left, right):
-            send, own = kernel(left, ordered(right))
+            send, kept = kernel(left, ordered(right))
             noted(send)
-            late.append((i, number, lax.ppermute(send, "dp", OVER_X), own))
+            late[i, number] = lax.ppermute(send, "dp", OVER_X), kept, left, right
 
         term(2, 1, term_columns, dy_t, hidden1)
         by_gate, by_up = by_hidden(ordered(dy[0]), w_down1, gate1, up1)
@@ -514,14 +562,19 @@
         noted(by_gate)
         term(0, 0, term_rows, a0_t, by_gate)
         term(1, 0, term_rows, a0_t, by_up)
+        _, kept, left, right = late[1, 0]
+        last_own = noted(own_rows(at, left, ordered(right), kept))
         squares = 0.0
-        for i, number, from_x, own in late:
+        for i, number in ((0, 1), (1, 1), (2, 1), (2, 0), (0, 0), (1, 0)):
+            from_x, kept, left, right = late[i, number]
             if i == 2:
-                mine[number][i], more = turned(own, from_x)
+                g, more = turned(ordered(kept), from_x)
+            elif (i, number) == (1, 0):
+                g, more = ended(ordered(last_own), from_x)
             else:
-                mine[number][i] = g = (own + from_x.astype(F32)).astype(BF16)
-                more = jnp.sum(jnp.square(g.astype(F32)))
-            squares += more
+                g, more = own_rows(at, left, ordered(right), kept, from_x)
+            mine[number][i] = noted(g)
+            squares += more[0, 0]
 
         squares = lax.psum(squares, "dp")
         count = 4 * sum(g.size for gs in mine for g in gs)

time: 919 us -> 911 us (level)
  Pallas kernels: 578 us -> 626 us
  waiting for transfers between devices: 199 us -> 169 us
  other arithmetic: 86.5 us -> 59.1 us
    pallas_call x4 -> x9, Pallas kernels: 134 us -> 203 us  [the longest x4 139 us: gate_up(): pl.pallas_call(functools.partial(gate_up_kernel, number, width, 5 if numb...]
    ppermute x6, waiting for transfers between devices: 46.8 us -> 17.3 us  [term(): late[i, number] = (lax.ppermute(send, 'dp', OVER_X), kept, left, right)]
    another operation x4 -> x0, other arithmetic: 27.6 us -> none  [step(): jnp.stack([mine[number][i] for number in range(layers)]).astype(F32)]
    pallas_call x4, Pallas kernels: 132 us -> 108 us  [term_rows(): pl.pallas_call(term_rows_kernel, out_shape=[shaped((rows, n)), shaped((ro...]
  transfers between devices with their start and end apart: 33 -> 33, of which waited for: 7 -> 7; matrix products, arithmetic and copies ran while one was open for 3% -> 1% of each run, Pallas kernels for 64% -> 69%
where the time goes in v3:
time: 911 us; the launch traced here: 901 us
  Pallas kernels  626 us (69%)
  waiting for transfers between devices  169 us (19%)
  other arithmetic  59.1 us (6%)
  starting transfers between devices  23.7 us (3%)
  local copies, waits for them, and re-layouts  10.8 us (1%)
    pallas_call x4, Pallas kernels, gate_up(): pl.pallas_call(functools.partial(gate_up_kernel, number, width, 5 if numb...  139 us
    pallas_call x4, Pallas kernels, term_rows(): pl.pallas_call(term_rows_kernel, out_shape=[shaped((rows, n)), shaped((ro...  108 us
    ppermute x6, waiting for transfers between devices, second(): ry = lax.ppermute(rx, 'rep', OVER_Y)  94.6 us
    pallas_call x2, Pallas kernels, by_hidden(): call(by_hidden_kernel, [shaped((m, n))] * 2, (n // bn, m // bm), [residen...  90.2 us
    pallas_call x2, Pallas kernels, term_columns(): pl.pallas_call(term_columns_kernel, out_shape=[shaped((m, wide)), shaped(...  69.6 us
    convert_element_type x2, other arithmetic, adamw(): return ((w - 0.02 * step).astype(BF16), m, v)  59.1 us
    ppermute x6, waiting for transfers between devices, across(): return lax.ppermute(mine, 'dp', OVER_X)  57 us
    pallas_call x1, Pallas kernels, by_a(): call(by_a_kernel, shaped((m, n)), (m // bm, n // bn), [lhs, lhs, w, w], p...  55 us
  transfers between devices with their start and end apart: 33, of which 7 were waited for; matrix products, arithmetic and copies ran while one was open for 1% of the time, Pallas kernels for 69%

profile of v3, /device:TPU:0, one launch (start us, length us, event | category | flops | bytes accessed | tf_op | source)
XLA Modules:
  0.0 901.3 jit_solution(2563112517030327507)
XLA Ops:
  10.5 28.1 %collective-permute-done.refs_2_ = bf16[384,1792]{1,0:T(8,128)(2,1)} collective-permute-done((bf16[384,1792]{1,0:T(8,128)(2,1)S(1)}, bf16[384,1792]{1,0:T(8,128)(2,1)}, u32[]{:S(2)}, u32[]{:S(2)}) %collective-permute-start) | collective-permute-done | bytes 1376288 | tf_op jit(solution)/shard_map/ppermute | solution.py:494
  38.6 28.8 %collective-permute-done.5.refs_6_ = bf16[384,1792]{1,0:T(8,128)(2,1)} collective-permute-done((bf16[384,1792]{1,0:T(8,128)(2,1)S(1)}, bf16[384,1792]{1,0:T(8,128)(2,1)}, u32[]{:S(2)}, u32[]{:S(2)}) %collective-permute-start.5) | collective-permute-done | bytes 1376288 | tf_op jit(solution)/shard_map/ppermute | solution.py:494
  102.6 27.3 %collective-permute-done.6.refs_6_ = bf16[384,1792]{1,0:T(8,128)(2,1)} collective-permute-done((bf16[384,1792]{1,0:T(8,128)(2,1)}, bf16[384,1792]{1,0:T(8,128)(2,1)}, u32[]{:S(2)}, u32[]{:S(2)}) %collective-permute-start.6) | collective-permute-done | bytes 1376288 | tf_op jit(solution)/shard_map/ppermute | solution.py:508
  130.4 34.2 %gate_up.4 = (f32[2048,3584]{1,0:T(8,128)}, f32[2048,3584]{1,0:T(8,128)}, bf16[2048,3584]{1,0:T(8,128)(2,1)}) custom-call(s32[5]{0:T(128)} %stack.60.at, bf16[2048,1536]{1,0:T(8,128)(2,1)} %get-tuple-element.88.a, bf16[2,384,3584]{2,1,0:T(8,128)(2,1)} %refs_0_.7, bf16[2,384,3584]{2,1,0:T(8,128)(2,1)} %collective-permute-done.1.refs_1_, ...), custom_call_target="tpu_custom_call" | custom-call | flops 22548578304 | bytes 47710208 | tf_op jit(solution)/shard_map/gate_up/pallas_call | solution.py:183
  169.1 28.0 %collective-permute-done.12.ry = bf16[448,1536]{1,0:T(8,128)(2,1)} collective-permute-done((bf16[448,1536]{1,0:T(8,128)(2,1)}, bf16[448,1536]{1,0:T(8,128)(2,1)}, u32[]{:S(2)}, u32[]{:S(2)}) %collective-permute-start.12) | collective-permute-done | bytes 1376288 | tf_op jit(solution)/shard_map/ppermute | solution.py:508
  197.1 34.2 %gate_up.5 = (f32[2048,3584]{1,0:T(8,128)}, f32[2048,3584]{1,0:T(8,128)}, bf16[2048,3584]{1,0:T(8,128)(2,1)}) custom-call(s32[5]{0:T(128)} %stack.62.at, bf16[2048,1536]{1,0:T(8,128)(2,1)} %get-tuple-element.88.a, bf16[2,384,3584]{2,1,0:T(8,128)(2,1)} %refs_0_.7, ...), custom_call_target="tpu_custom_call", output_to_operand_aliasing={{0}: (10, {}), {1}: (11, {}), {2}: (12, {})} | custom-call | flops 22548578304 | bytes 47710208 | tf_op jit(solution)/shard_map/gate_up/pallas_call | solution.py:183
  242.8 33.6 %shard_map.180 = (bf16[2048,1536]{1,0:T(8,128)(2,1)}, bf16[2048,1536]{1,0:T(8,128)(2,1)}, bf16[1536,2048]{1,0:T(8,128)(2,1)}) custom-call(bf16[2048,3584]{1,0:T(8,128)(2,1)} %get-tuple-element.121.hidden.right, bf16[3584,1536]{1,0:T(8,128)(2,1)} %assemble.2.w, bf16[2048,1536]{1,0:T(8,128)(2,1)} %bitcast.31), custom_call_target="tpu_custom_call" | custom-call | flops 22548578304 | bytes 25690112 | tf_op jit(solution)/shard_map/pallas_call | solution.py:212
  277.9 30.8 %collective-permute-done.19.refs_6_ = bf16[384,1792]{1,0:T(8,128)(2,1)} collective-permute-done((bf16[384,1792]{1,0:T(8,128)(2,1)}, bf16[384,1792]{1,0:T(8,128)(2,1)}, u32[]{:S(2)}, u32[]{:S(2)}) %collective-permute-start.19) | collective-permute-done | bytes 1376288 | tf_op jit(solution)/shard_map/ppermute | solution.py:508
  308.7 35.5 %gate_up.6 = (f32[2048,3584]{1,0:T(8,128)}, f32[2048,3584]{1,0:T(8,128)}, bf16[2048,3584]{1,0:T(8,128)(2,1)}, bf16[1536,3584]{1,0:T(8,128)(2,1)}, bf16[1536,3584]{1,0:T(8,128)(2,1)}) custom-call(s32[5]{0:T(128)} %stack.60.at, bf16[2048,1536]{1,0:T(8,128)(2,1)} %get-tuple-element.94.a, bf16[2,384,3584]{2,1,0:T(8,128)(2,1)} %refs_0_.7, ...), custom_call_target="tpu_custom_call" | custom-call | flops 22548578304 | bytes 47710208 | tf_op jit(solution)/shard_map/gate_up/pallas_call | solution.py:183
  344.7 35.2 %gate_up.7 = (f32[2048,3584]{1,0:T(8,128)}, f32[2048,3584]{1,0:T(8,128)}, bf16[2048,3584]{1,0:T(8,128)(2,1)}, bf16[1536,3584]{1,0:T(8,128)(2,1)}, bf16[1536,3584]{1,0:T(8,128)(2,1)}) custom-call(s32[5]{0:T(128)} %stack.62.at, bf16[2048,1536]{1,0:T(8,128)(2,1)} %get-tuple-element.94.a, ...), custom_call_target="tpu_custom_call", output_to_operand_aliasing={{0}: (10, {}), {1}: (11, {}), {2}: (12, {}), {3}: (13, {}),... | custom-call | flops 22548578304 | bytes 47710208 | tf_op jit(solution)/shard_map/gate_up/pallas_call | solution.py:183
  380.2 35.0 %term_columns.2 = (bf16[1536,896]{1,0:T(8,128)(2,1)}, f32[1536,896]{1,0:T(8,128)}) custom-call(bf16[1536,2048]{1,0:T(8,128)(2,1)} %shard_map.179.left, bf16[2048,3584]{1,0:T(8,128)(2,1)} %get-tuple-element.103.right), custom_call_target="tpu_custom_call" | custom-call | flops 22548578304 | bytes 31981568 | tf_op jit(solution)/shard_map/term_columns/pallas_call | solution.py:443
  423.9 45.1 %shard_map.181 = (bf16[2048,3584]{1,0:T(8,128)(2,1)}, bf16[2048,3584]{1,0:T(8,128)(2,1)}) custom-call(bf16[2048,1536]{1,0:T(8,128)(2,1)} %bitcast.28, bf16[3584,1536]{1,0:T(8,128)(2,1)} %assemble.3.w, f32[2048,3584]{1,0:T(8,128)} %get-tuple-element.107.gate, f32[2048,3584]{1,0:T(8,128)} %get-tuple-element.108.up), custom_call_target="tpu_custom_call" | custom-call | flops 22548578304 | bytes 88080384 | tf_op jit(solution)/shard_map/pallas_call | solution.py:232
  469.0 27.3 %term_rows.4 = (bf16[384,3584]{1,0:T(8,128)(2,1)}, bf16[384,3584]{1,0:T(8,128)(2,1)}) custom-call(bf16[1536,2048]{1,0:T(8,128)(2,1)} %get-tuple-element.110.left, bf16[2048,3584]{1,0:T(8,128)(2,1)} %get-tuple-element.136.right.dg), custom_call_target="tpu_custom_call" | custom-call | flops 16911433728 | bytes 31981568 | tf_op jit(solution)/shard_map/term_rows/pallas_call | solution.py:313
  498.0 26.8 %term_rows.5 = (bf16[384,3584]{1,0:T(8,128)(2,1)}, bf16[384,3584]{1,0:T(8,128)(2,1)}) custom-call(bf16[1536,2048]{1,0:T(8,128)(2,1)} %get-tuple-element.110.left, bf16[2048,3584]{1,0:T(8,128)(2,1)} %get-tuple-element.139.right.du), custom_call_target="tpu_custom_call" | custom-call | flops 16911433728 | bytes 31981568 | tf_op jit(solution)/shard_map/term_rows/pallas_call | solution.py:313
  525.1 55.0 %shard_map.182.by_a = bf16[2048,1536]{1,0:T(8,128)(2,1)} custom-call(bf16[2048,3584]{1,0:T(8,128)(2,1)} %get-tuple-element.136.right.dg, bf16[2048,3584]{1,0:T(8,128)(2,1)} %get-tuple-element.139.right.du, bf16[1536,3584]{1,0:T(8,128)(2,1)} %get-tuple-element.117.wg, bf16[1536,3584]{1,0:T(8,128)(2,1)} %get-tuple-element.118.wu), custom_call_target="tpu_custom_call" | custom-call | flops 45097156608 | bytes 73400320 | tf_op jit(solution)/shard_map/pallas_call | solution.py:250
  580.1 15.1 %shard_map.183 = (bf16[2048,1536]{1,0:T(8,128)(2,1)}, bf16[1536,2048]{1,0:T(8,128)(2,1)}) custom-call(bf16[2048,1536]{1,0:T(8,128)(2,1)} %shard_map.182.by_a, bf16[2048,1536]{1,0:T(8,128)(2,1)} %get-tuple-element.96.h, bf16[2048,1536]{1,0:T(8,128)(2,1)} %bitcast.29), custom_call_target="tpu_custom_call" | custom-call | flops 1000000000 | bytes 31457280 | tf_op jit(solution)/shard_map/pallas_call | solution.py:125
  595.3 34.6 %term_columns.3 = (bf16[1536,896]{1,0:T(8,128)(2,1)}, f32[1536,896]{1,0:T(8,128)}) custom-call(bf16[1536,2048]{1,0:T(8,128)(2,1)} %get-tuple-element.120.left, bf16[2048,3584]{1,0:T(8,128)(2,1)} %get-tuple-element.121.hidden.right), custom_call_target="tpu_custom_call" | custom-call | flops 22548578304 | bytes 31981568 | tf_op jit(solution)/shard_map/term_columns/pallas_call | solution.py:443
  631.6 45.1 %shard_map.184 = (bf16[2048,3584]{1,0:T(8,128)(2,1)}, bf16[2048,3584]{1,0:T(8,128)(2,1)}) custom-call(bf16[2048,1536]{1,0:T(8,128)(2,1)} %get-tuple-element.123.dy, bf16[3584,1536]{1,0:T(8,128)(2,1)} %assemble.2.w, f32[2048,3584]{1,0:T(8,128)} %get-tuple-element.124.gate, f32[2048,3584]{1,0:T(8,128)} %get-tuple-element.125.up), custom_call_target="tpu_custom_call" | custom-call | flops 22548578304 | bytes 88080384 | tf_op jit(solution)/shard_map/pallas_call | solution.py:232
  676.7 27.3 %term_rows.6 = (bf16[384,3584]{1,0:T(8,128)(2,1)}, bf16[384,3584]{1,0:T(8,128)(2,1)}) custom-call(bf16[1536,2048]{1,0:T(8,128)(2,1)} %get-tuple-element.86.left, bf16[2048,3584]{1,0:T(8,128)(2,1)} %get-tuple-element.146.right), custom_call_target="tpu_custom_call" | custom-call | flops 16911433728 | bytes 31981568 | tf_op jit(solution)/shard_map/term_rows/pallas_call | solution.py:313
  704.4 26.7 %term_rows.7 = (bf16[384,3584]{1,0:T(8,128)(2,1)}, bf16[384,3584]{1,0:T(8,128)(2,1)}) custom-call(bf16[1536,2048]{1,0:T(8,128)(2,1)} %get-tuple-element.86.left, bf16[2048,3584]{1,0:T(8,128)(2,1)} %get-tuple-element.134.right), custom_call_target="tpu_custom_call" | custom-call | flops 16911433728 | bytes 31981568 | tf_op jit(solution)/shard_map/term_rows/pallas_call | solution.py:313
  790.5 14.2 %shard_map.188 = (bf16[384,3584]{1,0:T(8,128)(2,1)}, f32[1,1]{1,0:T(1,128)}) custom-call(s32[5]{0:T(128)} %stack.60.at, bf16[1536,2048]{1,0:T(8,128)(2,1)} %get-tuple-element.86.left, bf16[2048,3584]{1,0:T(8,128)(2,1)} %get-tuple-element.146.right, bf16[384,3584]{1,0:T(8,128)(2,1)} %get-tuple-element.147.kept, bf16[384,3584]{1,0:T(8,128)(2,1)} %collective-permute-done.31.arrived), custom_call_target="tpu_custom_call" | custom-call | flops 5637144576 | bytes 14680064 | tf_op jit(solution)/shard_map/pallas_call | solution.py:358
  808.0 17.3 %collective-permute-done.32.arrived = bf16[384,3584]{1,0:T(8,128)(2,1)} collective-permute-done((bf16[384,3584]{1,0:T(8,128)(2,1)}, bf16[384,3584]{1,0:T(8,128)(2,1)}, u32[]{:S(2)}, u32[]{:S(2)}) %collective-permute-start.32) | collective-permute-done | bytes 2752544 | tf_op jit(solution)/shard_map/ppermute | solution.py:550
  841.7 22.2 %fusion.8 = (bf16[2,896,1536]{2,1,0:T(8,128)(2,1)}, f32[2,896,1536]{2,1,0:T(8,128)}, f32[2,896,1536]{2,1,0:T(8,128)}) fusion(bf16[2,896,1536]{2,1,0:T(8,128)(2,1)} %own.3, f32[]{:T(128)S(6)} %min_shard_map.3, bf16[1,896,1536]{2,1,0:T(8,128)(2,1)} %bitcast.36, bf16[1,896,1536]{2,1,0:T(8,128)(2,1)} %bitcast.37, f32[2,896,1536]{2,1,0:T(8,128)} %param.21, ...), kind=kLoop, calls=%fused_computation.17 | loop fusion | flops 55050240 | bytes 60555268 | tf_op jit(solution)/shard_map/convert_element_type | solution.py:27
  863.9 36.9 %fusion.2 = (bf16[2,384,3584]{2,1,0:T(8,128)(2,1)}, f32[2,384,3584]{2,1,0:T(8,128)}, f32[2,384,3584]{2,1,0:T(8,128)}, bf16[2,384,3584]{2,1,0:T(8,128)(2,1)}, f32...) fusion(bf16[2,384,3584]{2,1,0:T(8,128)(2,1)} %refs_0_.7, f32[]{:T(128)S(6)} %min_shard_map.3, ...), kind=kLoop, calls=%fused_computation.11 | loop fusion | flops 110100480 | bytes 121110528 | tf_op jit(solution)/shard_map/convert_element_type | solution.py:27
  (78 shorter events, 151.1 us)
Async XLA Ops:
  0.6 129.3 %collective-permute-start.1 = (bf16[2,384,3584]{2,1,0:T(8,128)(2,1)}, bf16[2,384,3584]{2,1,0:T(8,128)(2,1)}, u32[]{:S(2)}, u32[]{:S(2)}) collective-permute-start(bf16[2,384,3584]{2,1,0:T(8,128)(2,1)} %refs_0_.7), channel_id=1, source_target_pairs={{0,1},{1,0},{2,3},{3,2},{4,5},{5,4},{6,7},{7,6}} | collective-permute-start | bytes 16515080 | tf_op jit(solution)/shard_map/ppermute | solution.py:486
  1.5 128.9 %collective-permute-start.4 = (bf16[2,384,3584]{2,1,0:T(8,128)(2,1)}, bf16[2,384,3584]{2,1,0:T(8,128)(2,1)}, u32[]{:S(2)}, u32[]{:S(2)}) collective-permute-start(bf16[2,384,3584]{2,1,0:T(8,128)(2,1)} %refs_4_.7), channel_id=1, source_target_pairs={{0,1},{1,0},{2,3},{3,2},{4,5},{5,4},{6,7},{7,6}} | collective-permute-start | bytes 16515080 | tf_op jit(solution)/shard_map/ppermute | solution.py:486
  10.5 57.0 %collective-permute-start.5 = (bf16[384,1792]{1,0:T(8,128)(2,1)S(1)}, bf16[384,1792]{1,0:T(8,128)(2,1)}, u32[]{:S(2)}, u32[]{:S(2)}) collective-permute-start(bf16[384,1792]{1,0:T(8,128)(2,1)S(1)} %get-tuple-element.169), channel_id=1, source_target_pairs={{0,2},{2,0},{1,3},{3,1},{4,6},{6,4},{5,7},{7,5}} | collective-permute-start | bytes 4128776 | tf_op jit(solution)/shard_map/ppermute | solution.py:494
  69.2 60.7 %collective-permute-start.6 = (bf16[384,1792]{1,0:T(8,128)(2,1)}, bf16[384,1792]{1,0:T(8,128)(2,1)}, u32[]{:S(2)}, u32[]{:S(2)}) collective-permute-start(bf16[384,1792]{1,0:T(8,128)(2,1)} %collective-permute-done.5.refs_6_), channel_id=1, source_target_pairs={{0,4},{4,0},{1,5},{5,1},{2,6},{6,2},{3,7},{7,3}} | collective-permute-start | bytes 4128776 | tf_op jit(solution)/shard_map/ppermute | solution.py:508
  92.4 142.2 %collective-permute-start.10 = (bf16[2,896,1536]{2,1,0:T(8,128)(2,1)}, bf16[2,896,1536]{2,1,0:T(8,128)(2,1)}, u32[]{:S(2)}, u32[]{:S(2)}) collective-permute-start(bf16[2,896,1536]{2,1,0:T(8,128)(2,1)} %own.3), channel_id=1, source_target_pairs={{0,1},{1,0},{2,3},{3,2},{4,5},{5,4},{6,7},{7,6}} | collective-permute-start | bytes 16515080 | tf_op jit(solution)/shard_map/ppermute | solution.py:486
  100.8 63.8 %collective-permute-start.11 = (bf16[448,1536]{1,0:T(8,128)(2,1)}, bf16[448,1536]{1,0:T(8,128)(2,1)}, u32[]{:S(2)}, u32[]{:S(2)}) collective-permute-start(bf16[448,1536]{1,0:T(8,128)(2,1)} %get-tuple-element.167), channel_id=1, source_target_pairs={{0,2},{2,0},{1,3},{3,1},{4,6},{6,4},{5,7},{7,5}} | collective-permute-start | bytes 4128776 | tf_op jit(solution)/shard_map/ppermute | solution.py:494
  129.9 38.7 %collective-permute-start.3 = (bf16[384,1792]{1,0:T(8,128)(2,1)}, bf16[384,1792]{1,0:T(8,128)(2,1)}, u32[]{:S(2)}, u32[]{:S(2)}) collective-permute-start(bf16[384,1792]{1,0:T(8,128)(2,1)} %collective-permute-done.2.refs_2_), channel_id=1, source_target_pairs={{0,1},{1,0},{2,3},{3,2},{4,5},{5,4},{6,7},{7,6}} | collective-permute-start | bytes 4128776 | tf_op jit(solution)/shard_map/ppermute | solution.py:509
  129.9 39.2 %collective-permute-start.7 = (bf16[384,1792]{1,0:T(8,128)(2,1)}, bf16[384,1792]{1,0:T(8,128)(2,1)}, u32[]{:S(2)}, u32[]{:S(2)}) collective-permute-start(bf16[384,1792]{1,0:T(8,128)(2,1)} %collective-permute-done.6.refs_6_), channel_id=1, source_target_pairs={{0,1},{1,0},{2,3},{3,2},{4,5},{5,4},{6,7},{7,6}} | collective-permute-start | bytes 4128776 | tf_op jit(solution)/shard_map/ppermute | solution.py:509
  166.4 111.0 %collective-permute-start.23 = (bf16[448,1536]{1,0:T(8,128)(2,1)}, bf16[448,1536]{1,0:T(8,128)(2,1)}, u32[]{:S(2)}, u32[]{:S(2)}) collective-permute-start(bf16[448,1536]{1,0:T(8,128)(2,1)} %get-tuple-element.166), channel_id=1, source_target_pairs={{0,2},{2,0},{1,3},{3,1},{4,6},{6,4},{5,7},{7,5}} | collective-permute-start | bytes 4128776 | tf_op jit(solution)/shard_map/ppermute | solution.py:494
  168.6 62.7 %collective-permute-start.15 = (bf16[384,1792]{1,0:T(8,128)(2,1)}, bf16[384,1792]{1,0:T(8,128)(2,1)}, u32[]{:S(2)}, u32[]{:S(2)}) collective-permute-start(bf16[384,1792]{1,0:T(8,128)(2,1)} %get-tuple-element.170), channel_id=1, source_target_pairs={{0,2},{2,0},{1,3},{3,1},{4,6},{6,4},{5,7},{7,5}} | collective-permute-start | bytes 4128776 | tf_op jit(solution)/shard_map/ppermute | solution.py:494
  169.1 64.0 %collective-permute-start.13 = (bf16[448,1536]{1,0:T(8,128)(2,1)}, bf16[448,1536]{1,0:T(8,128)(2,1)}, u32[]{:S(2)}, u32[]{:S(2)}) collective-permute-start(bf16[448,1536]{1,0:T(8,128)(2,1)} %collective-permute-done.11.rx), channel_id=1, source_target_pairs={{0,1},{1,0},{2,3},{3,2},{4,5},{5,4},{6,7},{7,6}} | collective-permute-start | bytes 4128776 | tf_op jit(solution)/shard_map/ppermute | solution.py:502
  197.1 37.5 %collective-permute-start.14 = (bf16[448,1536]{1,0:T(8,128)(2,1)}, bf16[448,1536]{1,0:T(8,128)(2,1)}, u32[]{:S(2)}, u32[]{:S(2)}) collective-permute-start(bf16[448,1536]{1,0:T(8,128)(2,1)} %collective-permute-done.12.ry), channel_id=1, source_target_pairs={{0,1},{1,0},{2,3},{3,2},{4,5},{5,4},{6,7},{7,6}} | collective-permute-start | bytes 4128776 | tf_op jit(solution)/shard_map/ppermute | solution.py:509
  231.3 45.1 %collective-permute-start.18 = (bf16[384,1792]{1,0:T(8,128)(2,1)}, bf16[384,1792]{1,0:T(8,128)(2,1)}, u32[]{:S(2)}, u32[]{:S(2)}) collective-permute-start(bf16[384,1792]{1,0:T(8,128)(2,1)} %get-tuple-element.168), channel_id=1, source_target_pairs={{0,2},{2,0},{1,3},{3,1},{4,6},{6,4},{5,7},{7,5}} | collective-permute-start | bytes 4128776 | tf_op jit(solution)/shard_map/ppermute | solution.py:494
  233.0 44.4 %collective-permute-start.16 = (bf16[384,1792]{1,0:T(8,128)(2,1)}, bf16[384,1792]{1,0:T(8,128)(2,1)}, u32[]{:S(2)}, u32[]{:S(2)}) collective-permute-start(bf16[384,1792]{1,0:T(8,128)(2,1)} %collective-permute-done.15.refs_2_), channel_id=1, source_target_pairs={{0,4},{4,0},{1,5},{5,1},{2,6},{6,2},{3,7},{7,3}} | collective-permute-start | bytes 4128776 | tf_op jit(solution)/shard_map/ppermute | solution.py:508
  277.4 138.2 %collective-permute-start.25 = (bf16[448,1536]{1,0:T(8,128)(2,1)}, bf16[448,1536]{1,0:T(8,128)(2,1)}, u32[]{:S(2)}, u32[]{:S(2)}) collective-permute-start(bf16[448,1536]{1,0:T(8,128)(2,1)} %collective-permute-done.23.rx), channel_id=1, source_target_pairs={{0,1},{1,0},{2,3},{3,2},{4,5},{5,4},{6,7},{7,6}} | collective-permute-start | bytes 4128776 | tf_op jit(solution)/shard_map/ppermute | solution.py:502
  277.4 67.3 %collective-permute-start.17 = (bf16[384,1792]{1,0:T(8,128)(2,1)}, bf16[384,1792]{1,0:T(8,128)(2,1)}, u32[]{:S(2)}, u32[]{:S(2)}) collective-permute-start(bf16[384,1792]{1,0:T(8,128)(2,1)} %collective-permute-done.16.refs_2_), channel_id=1, source_target_pairs={{0,1},{1,0},{2,3},{3,2},{4,5},{5,4},{6,7},{7,6}} | collective-permute-start | bytes 4128776 | tf_op jit(solution)/shard_map/ppermute | solution.py:509
  308.7 36.0 %collective-permute-start.20 = (bf16[384,1792]{1,0:T(8,128)(2,1)}, bf16[384,1792]{1,0:T(8,128)(2,1)}, u32[]{:S(2)}, u32[]{:S(2)}) collective-permute-start(bf16[384,1792]{1,0:T(8,128)(2,1)} %collective-permute-done.19.refs_6_), channel_id=1, source_target_pairs={{0,1},{1,0},{2,3},{3,2},{4,5},{5,4},{6,7},{7,6}} | collective-permute-start | bytes 4128776 | tf_op jit(solution)/shard_map/ppermute | solution.py:509
  344.2 35.8 %collective-permute-start.24 = (bf16[448,1536]{1,0:T(8,128)(2,1)}, bf16[448,1536]{1,0:T(8,128)(2,1)}, u32[]{:S(2)}, u32[]{:S(2)}) collective-permute-start(bf16[448,1536]{1,0:T(8,128)(2,1)} %collective-permute-done.23.rx), channel_id=1, source_target_pairs={{0,4},{4,0},{1,5},{5,1},{2,6},{6,2},{3,7},{7,3}} | collective-permute-start | bytes 4128776 | tf_op jit(solution)/shard_map/ppermute | solution.py:508
  415.3 359.4 %collective-permute-start.29 = (bf16[1536,896]{1,0:T(8,128)(2,1)}, bf16[1536,896]{1,0:T(8,128)(2,1)}, u32[]{:S(2)}, u32[]{:S(2)}) collective-permute-start(bf16[1536,896]{1,0:T(8,128)(2,1)} %get-tuple-element.104), channel_id=1, source_target_pairs={{0,2},{2,0},{1,3},{3,1},{4,6},{6,4},{5,7},{7,5}} | collective-permute-start | bytes 8257544 | tf_op jit(solution)/shard_map/ppermute | solution.py:550
  496.2 234.9 %collective-permute-start.27 = (bf16[384,3584]{1,0:T(8,128)(2,1)}, bf16[384,3584]{1,0:T(8,128)(2,1)}, u32[]{:S(2)}, u32[]{:S(2)}) collective-permute-start(bf16[384,3584]{1,0:T(8,128)(2,1)} %get-tuple-element.113), channel_id=1, source_target_pairs={{0,2},{2,0},{1,3},{3,1},{4,6},{6,4},{5,7},{7,5}} | collective-permute-start | bytes 8257544 | tf_op jit(solution)/shard_map/ppermute | solution.py:550
  524.8 235.8 %collective-permute-start.28 = (bf16[384,3584]{1,0:T(8,128)(2,1)}, bf16[384,3584]{1,0:T(8,128)(2,1)}, u32[]{:S(2)}, u32[]{:S(2)}) collective-permute-start(bf16[384,3584]{1,0:T(8,128)(2,1)} %get-tuple-element.115), channel_id=1, source_target_pairs={{0,2},{2,0},{1,3},{3,1},{4,6},{6,4},{5,7},{7,5}} | collective-permute-start | bytes 8257544 | tf_op jit(solution)/shard_map/ppermute | solution.py:550
  629.8 152.8 %collective-permute-start.30 = (bf16[1536,896]{1,0:T(8,128)(2,1)}, bf16[1536,896]{1,0:T(8,128)(2,1)}, u32[]{:S(2)}, u32[]{:S(2)}) collective-permute-start(bf16[1536,896]{1,0:T(8,128)(2,1)} %get-tuple-element.122), channel_id=1, source_target_pairs={{0,2},{2,0},{1,3},{3,1},{4,6},{6,4},{5,7},{7,5}} | collective-permute-start | bytes 8257544 | tf_op jit(solution)/shard_map/ppermute | solution.py:550
  704.0 86.5 %collective-permute-start.31 = (bf16[384,3584]{1,0:T(8,128)(2,1)}, bf16[384,3584]{1,0:T(8,128)(2,1)}, u32[]{:S(2)}, u32[]{:S(2)}) collective-permute-start(bf16[384,3584]{1,0:T(8,128)(2,1)} %get-tuple-element.131), channel_id=1, source_target_pairs={{0,2},{2,0},{1,3},{3,1},{4,6},{6,4},{5,7},{7,5}} | collective-permute-start | bytes 8257544 | tf_op jit(solution)/shard_map/ppermute | solution.py:550
  731.2 94.1 %collective-permute-start.32 = (bf16[384,3584]{1,0:T(8,128)(2,1)}, bf16[384,3584]{1,0:T(8,128)(2,1)}, u32[]{:S(2)}, u32[]{:S(2)}) collective-permute-start(bf16[384,3584]{1,0:T(8,128)(2,1)} %get-tuple-element.133), channel_id=1, source_target_pairs={{0,2},{2,0},{1,3},{3,1},{4,6},{6,4},{5,7},{7,5}} | collective-permute-start | bytes 8257544 | tf_op jit(solution)/shard_map/ppermute | solution.py:550
  (10 other events, 309.3 us)

commit v4 on v3

--- a/solution.py
+++ b/solution.py
@@ -30,45 +30,6 @@
 def others(d):
     x, c = d // 2, d % 2
     return d, 2 * x + 1 - c, 2 * (1 - x) + c, 2 * (1 - x) + 1 - c
-
-
-def assemble_kernel(number, rows, own, own_c, rx, ry, rx_c, ry_c, out, buf, sem_in, sem_out):
-    d, r = lax.axis_index("dp"), lax.axis_index("rep")
-    half = rows // 2
-    own_i, core_i, x_i, xc_i = others(d)
-    at = lambda i, n: pl.ds(pl.multiple_of(i, 16), n)
-    moves = [
-        (own.at[number], own_i * rows, rows),
-        (own_c.at[number], core_i * rows, rows),
-        (rx, x_i * rows + r * half, half),
-        (ry, x_i * rows + (1 - r) * half, half),
-        (rx_c, xc_i * rows + r * half, half),
-        (ry_c, xc_i * rows + (1 - r) * half, half),
-    ]
-    ins = [pltpu.make_async_copy(src, buf.at[at(i, n)], sem_in.at[k]) for k, (src, i, n) in enumerate(moves)]
-    outs = [pltpu.make_async_copy(buf.at[at(i, n)], out.at[at(i, n)], sem_out.at[k]) for k, (src, i, n) in enumerate(moves)]
-    for one in ins:
-        one.start()
-    for one, two in zip(ins, outs):
-        one.wait()
-        two.start()
-    for one in outs:
-        one.wait()
-
-
-def assembled(number, own, own_c, rx, ry, rx_c, ry_c):
-    _, rows, cols = own.shape
-    any_space = pl.BlockSpec(memory_space=pl.ANY)
-    return pl.pallas_call(
-        functools.partial(assemble_kernel, number, rows),
-        out_shape=jax.ShapeDtypeStruct((4 * rows, cols), BF16),
-        in_specs=[any_space] * 6,
-        out_specs=any_space,
-        scratch_shapes=[pltpu.VMEM((4 * rows, cols), BF16), pltpu.SemaphoreType.DMA((6,)), pltpu.SemaphoreType.DMA((6,))],
-        compiler_params=pltpu.CompilerParams(vmem_limit_bytes=VMEM),
-        cost_estimate=pl.CostEstimate(flops=10**9, bytes_accessed=8 * 4 * rows * cols, transcendentals=0),
-        name="assemble",
-    )(own, own_c, rx, ry, rx_c, ry_c)
 
 
 VMEM = 63 << 20
@@ -197,23 +158,59 @@
     )(at, a, *gates, *ups, *before)
 
 
-def down_kernel(hidden, w, x, h, a, a_t):
-    out = x[...] + jnp.dot(hidden[...], w[...], preferred_element_type=F32).astype(BF16)
+def arriving(number, rows, pieces, buf, sem):
+    own, own_c, rx, ry, rx_c, ry_c = pieces
+    d, r = lax.axis_index("dp"), lax.axis_index("rep")
+    half = rows // 2
+    own_i, core_i, x_i, xc_i = others(d)
+    at = lambda i, n: buf.at[pl.ds(pl.multiple_of(i, 16), n)]
+    moves = [
+        (own.at[number], at(own_i * rows, rows)),
+        (own_c.at[number], at(core_i * rows, rows)),
+        (rx, at(x_i * rows + r * half, half)),
+        (ry, at(x_i * rows + (1 - r) * half, half)),
+        (rx_c, at(xc_i * rows + r * half, half)),
+        (ry_c, at(xc_i * rows + (1 - r) * half, half)),
+    ]
+    return [pltpu.make_async_copy(src, dst, sem.at[k]) for k, (src, dst) in enumerate(moves)]
+
+
+def down_kernel(number, rows, hidden, x, *refs):
+    pieces, (h, a, a_t, whole, buf, sem, out_sem) = refs[:6], refs[6:]
+    i = pl.program_id(0)
+    put = pltpu.make_async_copy(buf, whole, out_sem)
+
+    @pl.when(i == 0)
+    def _():
+        ins = arriving(number, rows, pieces, buf, sem)
+        for one in ins:
+            one.start()
+        for one in ins:
+            one.wait()
+        put.start()
+
+    out = x[...] + jnp.dot(hidden[...], buf[...], preferred_element_type=F32).astype(BF16)
     h[...] = out
     out = normed(out)
     a[...] = out
     a_t[...] = turned_of(out)
 
-
-def down(hidden, w, x, bm=256):
+    @pl.when(i == pl.num_programs(0) - 1)
+    def _():
+        put.wait()
+
+
+def down(number, hidden, x, pieces, bm=256):
     m, k = hidden.shape
-    n = w.shape[1]
+    n, rows = pieces[0].shape[2], pieces[0].shape[1]
     out = pl.BlockSpec((bm, n), lambda i: (i, 0))
+    any_space = pl.BlockSpec(memory_space=pl.ANY)
     return call(
-        down_kernel, [shaped((m, n))] * 2 + [shaped((n, m))], (m // bm,),
-        [pl.BlockSpec((bm, k), lambda i: (i, 0)), resident((k, n)), out], [out] * 2 + [pl.BlockSpec((n, bm), lambda i: (0, i))],
-        2 * m * n * k, 2 * k * n + 2 * m * k,
-    )(hidden, w, x)
+        functools.partial(down_kernel, number, rows), [shaped((m, n))] * 2 + [shaped((n, m)), shaped((k, n))], (m // bm,),
+        [pl.BlockSpec((bm, k), lambda i: (i, 0)), out] + [any_space] * 6,
+        [out] * 2 + [pl.BlockSpec((n, bm), lambda i: (0, i)), any_space], 2 * m * n * k, 4 * k * n + 2 * m * k,
+        scratch=[pltpu.VMEM((k, n), BF16), pltpu.SemaphoreType.DMA((6,)), pltpu.SemaphoreType.DMA],
+    )(hidden, x, *pieces)
 
 
 NT = (((1,), (1,)), ((), ()))
@@ -225,15 +222,43 @@
     du[...] = (by * up[...]).astype(BF16)
 
 
-def by_hidden(dy, w, gate, up, bm=2048, bn=512):
+def by_hidden(dy, w, gate, up, bn=512):
     m, k = dy.shape
     n = w.shape[0]
-    out = pl.BlockSpec((bm, bn), lambda j, i: (i, j))
+    out = pl.BlockSpec((m, bn), lambda j: (0, j))
     return call(
-        by_hidden_kernel, [shaped((m, n))] * 2, (n // bn, m // bm),
-        [resident((m, k)), pl.BlockSpec((bn, k), lambda j, i: (j, 0)), out, out], [out] * 2,
-        2 * m * n * k, 12 * m * n,
+        by_hidden_kernel, [shaped((m, n))] * 2, (n // bn,),
+        [resident((m, k)), pl.BlockSpec((bn, k), lambda j: (j, 0)), out, out], [out] * 2, 2 * m * n * k, 12 * m * n,
     )(dy, w, gate, up)
+
+
+def by_hidden_pieces_kernel(number, rows, dy, gate, up, *refs):
+    pieces, (dg, du, buf, sem) = refs[:6], refs[6:]
+    j, bn = pl.program_id(0), dg.shape[1]
+
+    @pl.when(j == 0)
+    def _():
+        ins = arriving(number, rows, pieces, buf, sem)
+        for one in ins:
+            one.start()
+        for one in ins:
+            one.wait()
+
+    w = buf[pl.ds(pl.multiple_of(j * bn, bn), bn), :]
+    by = lax.dot_general(dy[...], w, NT, preferred_element_type=F32).astype(BF16).astype(F32)
+    dg[...] = (by * gate[...]).astype(BF16)
+    du[...] = (by * up[...]).astype(BF16)
+
+
+def by_hidden_pieces(number, dy, pieces, gate, up, bn=512):
+    m, k = dy.shape
+    n, rows = gate.shape[1], pieces[0].shape[1]
+    out = pl.BlockSpec((m, bn), lambda j: (0, j))
+    return call(
+        functools.partial(by_hidden_pieces_kernel, number, rows), [shaped((m, n))] * 2, (n // bn,),
+        [resident((m, k)), out, out] + [pl.BlockSpec(memory_space=pl.ANY)] * 6, [out] * 2, 2 * m * n * k, 12 * m * n,
+        scratch=[pltpu.VMEM((n, k), BF16), pltpu.SemaphoreType.DMA((6,))],
+    )(dy, gate, up, *pieces)
 
 
 def by_a_kernel(dg, du, wg, wu, out):
@@ -361,19 +386,62 @@
     )(at, left, right, kept, arrived)
 
 
-def ended_kernel(own, arrived, out, squares):
+def ended_kernel(elements, own, arrived, before, out, factor, acc, mine, got, send_sem, recv_sem):
+    d = lax.axis_index("dp")
+    j, last = pl.program_id(0), pl.num_programs(0) - 1
+    peers = [lax.rem(d + k, 4) for k in (1, 2, 3)]
+    barrier = pltpu.get_barrier_semaphore()
+
+    @pl.when(j == 0)
+    def _():
+        for peer in peers:
+            pl.semaphore_signal(barrier, inc=1, device_id={"dp": peer}, device_id_type=pl.DeviceIdType.MESH)
+        acc[...] = jnp.zeros_like(acc)
+
     g = (own[...] + arrived[...].astype(F32)).astype(BF16)
     out[...] = g
-    count(squares, g.astype(F32))
-
-
-def ended(own, arrived):
+    g = g.astype(F32)
+    acc[...] += jnp.sum((g * g).reshape(g.shape[0] // 8, 8, g.shape[1]), axis=0)
+
+    @pl.when(j == last)
+    def _():
+        mine[...] = jnp.full(mine.shape, jnp.sum(acc[...]) + before[0, 0], F32)
+        pl.semaphore_wait(barrier, 3)
+        copies = [
+            pltpu.make_async_remote_copy(
+                src_ref=mine, dst_ref=got.at[k], send_sem=send_sem.at[k], recv_sem=recv_sem.at[k],
+                device_id={"dp": peer}, device_id_type=pl.DeviceIdType.MESH,
+            )
+            for k, peer in enumerate(peers)
+        ]
+        for one in copies:
+            one.start()
+        for one in copies:
+            one.wait()
+        squares = mine[...] + got[0] + got[1] + got[2]
+        factor[...] = jnp.minimum(1.0, 0.5 * lax.rsqrt(squares / elements + 1e-30))
+
+
+def ended(own, arrived, before, elements):
     m, n = own.shape
     spec = pl.BlockSpec((m, TILE), lambda j: (0, j))
-    return call(
-        ended_kernel, [shaped((m, n)), shaped((1, 1), F32)], (n // TILE,), [spec, spec], [spec, pl.BlockSpec(memory_space=pltpu.SMEM)],
-        4 * m * n, 8 * m * n,
-    )(own, arrived)
+    return pl.pallas_call(
+        functools.partial(ended_kernel, elements),
+        out_shape=[shaped((m, n)), shaped((8, 128), F32)],
+        grid=(n // TILE,),
+        in_specs=[spec, spec, pl.BlockSpec(memory_space=pltpu.SMEM)],
+        out_specs=[spec, pl.BlockSpec((8, 128), lambda j: (0, 0))],
+        scratch_shapes=[
+            pltpu.VMEM((8, TILE), F32),
+            pltpu.VMEM((8, 128), F32),
+            pltpu.VMEM((3, 8, 128), F32),
+            pltpu.SemaphoreType.DMA((3,)),
+            pltpu.SemaphoreType.DMA((3,)),
+        ],
+        compiler_params=pltpu.CompilerParams(vmem_limit_bytes=VMEM, collective_id=2, has_side_effects=True),
+        cost_estimate=pl.CostEstimate(flops=4 * m * n, bytes_accessed=8 * m * n, transcendentals=0),
+        name="ended",
+    )(own, arrived, before)
 
 
 def term_columns_kernel(left, right, send, own, full, there, send_sem, recv_sem):
@@ -508,9 +576,9 @@
             ry = lax.ppermute(rx, "rep", OVER_Y)
             return ry, lax.ppermute(ry, "dp", OVER_CORE)
 
-        def whole_down(number, behind):
+        def down_pieces(number, behind):
             ry, ry_c = second(2, number, behind)
-            return assembled(number, weights[2], from_core[2], halves[2, number], ry, first(2, number), ry_c)
+            return weights[2], from_core[2], halves[2, number], ry, first(2, number), ry_c
 
         last = []
 
@@ -534,11 +602,11 @@
         (dy_t,) = by_rows(turn_kernel, "t", lax.optimization_barrier((dy[0], a0, halves[0, 0]))[0])
         a0, a0_t, dy_t = lax.optimization_barrier((a0, a0_t, dy_t))
         outs, arrived = ab(0, a0, ((), ()))
-        w_down0 = whole_down(0, outs[2])
+        pieces0 = down_pieces(0, outs[2])
         gate0, up0, hidden0 = gate_up(0, at_b, a0, *arrived, outs)
-        h1, a1, a1_t = down(hidden0, w_down0, x[0])
+        h1, a1, a1_t, w_down0 = down(0, hidden0, x[0], pieces0)
         outs, arrived = ab(1, a1, ((hidden0,), (h1,)))
-        w_down1 = whole_down(1, outs[2])
+        pieces1 = down_pieces(1, outs[2])
         gate1, up1, hidden1, w_gate1, w_up1 = gate_up(1, at_b, a1, *arrived, outs)
         noted(hidden1)
 
@@ -550,7 +618,7 @@
             late[i, number] = lax.ppermute(send, "dp", OVER_X), kept, left, right
 
         term(2, 1, term_columns, dy_t, hidden1)
-        by_gate, by_up = by_hidden(ordered(dy[0]), w_down1, gate1, up1)
+        by_gate, by_up = by_hidden_pieces(1, ordered(dy[0]), pieces1, gate1, up1)
         noted(by_gate)
         term(0, 1, term_rows, a1_t, by_gate)
         term(1, 1, term_rows, a1_t, by_up)
@@ -565,20 +633,17 @@
         _, kept, left, right = late[1, 0]
         last_own = noted(own_rows(at, left, ordered(right), kept))
         squares = 0.0
-        for i, number in ((0, 1), (1, 1), (2, 1), (2, 0), (0, 0), (1, 0)):
+        for i, number in ((0, 1), (1, 1), (2, 1), (2, 0), (0, 0)):
             from_x, kept, left, right = late[i, number]
             if i == 2:
                 g, more = turned(ordered(kept), from_x)
-            elif (i, number) == (1, 0):
-                g, more = ended(ordered(last_own), from_x)
             else:
                 g, more = own_rows(at, left, ordered(right), kept, from_x)
             mine[number][i] = noted(g)
-            squares += more[0, 0]
-
-        squares = lax.psum(squares, "dp")
-        count = 4 * sum(g.size for gs in mine for g in gs)
-        factor = jnp.minimum(1.0, 0.5 * lax.rsqrt(squares / count + 1e-30))
+            squares += more
+        count = 4 * sum(w.size for w in weights)
+        mine[0][1], factor = ended(ordered(last_own), late[1, 0][0], squares, count)
+        factor = factor[0, 0]
         new = []
         for i in range(3):
             g = jnp.stack([mine[number][i] for number in range(layers)]).astype(F32) * factor

time: 911 us -> 893 us (0.980)
  Pallas kernels: 626 us -> 613 us
    pallas_call x6 -> x4, Pallas kernels: 148 us -> 135 us  [the longest x1 45 us: by_hidden(): call(by_hidden_kernel, [shaped((m, n))] * 2, (n // bn,), [resident((m, k)...]
  transfers between devices with their start and end apart: 33 -> 33, of which waited for: 7 -> 7; matrix products, arithmetic and copies ran while one was open for 1% -> 1% of each run, Pallas kernels for 69% -> 68%
where the time goes in v4:
time: 893 us; the launch traced here: 882 us
  Pallas kernels  613 us (69%)
  waiting for transfers between devices  169 us (19%)
  other arithmetic  60.4 us (7%)
  starting transfers between devices  23.7 us (3%)
  local copies, waits for them, and re-layouts  11.9 us (1%)
    pallas_call x4, Pallas kernels, gate_up(): pl.pallas_call(functools.partial(gate_up_kernel, number, width, 5 if numb...  139 us
    pallas_call x4, Pallas kernels, term_rows(): pl.pallas_call(term_rows_kernel, out_shape=[shaped((rows, n)), shaped((ro...  108 us
    ppermute x6, waiting for transfers between devices, second(): ry = lax.ppermute(rx, 'rep', OVER_Y)  94.6 us
    pallas_call x2, Pallas kernels, term_columns(): pl.pallas_call(term_columns_kernel, out_shape=[shaped((m, wide)), shaped(...  69.6 us
    convert_element_type x2, other arithmetic, adamw(): return ((w - 0.02 * step).astype(BF16), m, v)  60.4 us
    ppermute x6, waiting for transfers between devices, across(): return lax.ppermute(mine, 'dp', OVER_X)  57 us
    pallas_call x1, Pallas kernels, by_a(): call(by_a_kernel, shaped((m, n)), (m // bm, n // bn), [lhs, lhs, w, w], p...  55 us
    pallas_call x1, Pallas kernels, by_hidden(): call(by_hidden_kernel, [shaped((m, n))] * 2, (n // bn,), [resident((m, k)...  45 us
  transfers between devices with their start and end apart: 33, of which 7 were waited for; matrix products, arithmetic and copies ran while one was open for 1% of the time, Pallas kernels for 68%

profile of v4, /device:TPU:0, one launch (start us, length us, event | category | flops | bytes accessed | tf_op | source)
XLA Modules:
  0.0 882.4 jit_solution(16622282910307361158)
XLA Ops:
  10.5 28.1 %collective-permute-done.refs_2_ = bf16[384,1792]{1,0:T(8,128)(2,1)} collective-permute-done((bf16[384,1792]{1,0:T(8,128)(2,1)S(1)}, bf16[384,1792]{1,0:T(8,128)(2,1)}, u32[]{:S(2)}, u32[]{:S(2)}) %collective-permute-start) | collective-permute-done | bytes 1376288 | tf_op jit(solution)/shard_map/ppermute | solution.py:562
  38.6 28.8 %collective-permute-done.5.refs_6_ = bf16[384,1792]{1,0:T(8,128)(2,1)} collective-permute-done((bf16[384,1792]{1,0:T(8,128)(2,1)S(1)}, bf16[384,1792]{1,0:T(8,128)(2,1)}, u32[]{:S(2)}, u32[]{:S(2)}) %collective-permute-start.5) | collective-permute-done | bytes 1376288 | tf_op jit(solution)/shard_map/ppermute | solution.py:562
  102.6 27.3 %collective-permute-done.6.refs_6_ = bf16[384,1792]{1,0:T(8,128)(2,1)} collective-permute-done((bf16[384,1792]{1,0:T(8,128)(2,1)}, bf16[384,1792]{1,0:T(8,128)(2,1)}, u32[]{:S(2)}, u32[]{:S(2)}) %collective-permute-start.6) | collective-permute-done | bytes 1376288 | tf_op jit(solution)/shard_map/ppermute | solution.py:576
  130.4 34.2 %gate_up.4 = (f32[2048,3584]{1,0:T(8,128)}, f32[2048,3584]{1,0:T(8,128)}, bf16[2048,3584]{1,0:T(8,128)(2,1)}) custom-call(s32[5]{0:T(128)} %stack.60.at, bf16[2048,1536]{1,0:T(8,128)(2,1)} %get-tuple-element.89.a, bf16[2,384,3584]{2,1,0:T(8,128)(2,1)} %refs_0_.10, bf16[2,384,3584]{2,1,0:T(8,128)(2,1)} %collective-permute-done.1.refs_1_, ...), custom_call_target="tpu_custom_call" | custom-call | flops 22548578304 | bytes 47710208 | tf_op jit(solution)/shard_map/gate_up/pallas_call | solution.py:144
  169.1 28.0 %collective-permute-done.12.refs_3_ = bf16[448,1536]{1,0:T(8,128)(2,1)} collective-permute-done((bf16[448,1536]{1,0:T(8,128)(2,1)}, bf16[448,1536]{1,0:T(8,128)(2,1)}, u32[]{:S(2)}, u32[]{:S(2)}) %collective-permute-start.12) | collective-permute-done | bytes 1376288 | tf_op jit(solution)/shard_map/ppermute | solution.py:576
  197.1 34.2 %gate_up.5 = (f32[2048,3584]{1,0:T(8,128)}, f32[2048,3584]{1,0:T(8,128)}, bf16[2048,3584]{1,0:T(8,128)(2,1)}) custom-call(s32[5]{0:T(128)} %stack.62.at, bf16[2048,1536]{1,0:T(8,128)(2,1)} %get-tuple-element.89.a, bf16[2,384,3584]{2,1,0:T(8,128)(2,1)} %refs_0_.10, ...), custom_call_target="tpu_custom_call", output_to_operand_aliasing={{0}: (10, {}), {1}: (11, {}), {2}: (12, {})} | custom-call | flops 22548578304 | bytes 47710208 | tf_op jit(solution)/shard_map/gate_up/pallas_call | solution.py:144
  234.7 36.1 %shard_map.180 = (bf16[2048,1536]{1,0:T(8,128)(2,1)}, bf16[2048,1536]{1,0:T(8,128)(2,1)}, bf16[1536,2048]{1,0:T(8,128)(2,1)}, bf16[3584,1536]{1,0:T(8,128)(2,1)}) custom-call(bf16[2048,3584]{1,0:T(8,128)(2,1)} %get-tuple-element.122.hidden.right, bf16[2048,1536]{1,0:T(8,128)(2,1)} %bitcast.31, bf16[2,896,1536]{2,1,0:T(8,128)(2,1)} %refs_0_.11, ...), custom_call_target="tpu_custom_call" | custom-call | flops 22548578304 | bytes 36700160 | tf_op jit(solution)/shard_map/pallas_call | solution.py:208
  272.4 30.8 %collective-permute-done.19.refs_6_ = bf16[384,1792]{1,0:T(8,128)(2,1)} collective-permute-done((bf16[384,1792]{1,0:T(8,128)(2,1)}, bf16[384,1792]{1,0:T(8,128)(2,1)}, u32[]{:S(2)}, u32[]{:S(2)}) %collective-permute-start.19) | collective-permute-done | bytes 1376288 | tf_op jit(solution)/shard_map/ppermute | solution.py:576
  303.2 35.5 %gate_up.6 = (f32[2048,3584]{1,0:T(8,128)}, f32[2048,3584]{1,0:T(8,128)}, bf16[2048,3584]{1,0:T(8,128)(2,1)}, bf16[1536,3584]{1,0:T(8,128)(2,1)}, bf16[1536,3584]{1,0:T(8,128)(2,1)}) custom-call(s32[5]{0:T(128)} %stack.60.at, bf16[2048,1536]{1,0:T(8,128)(2,1)} %get-tuple-element.95.a, bf16[2,384,3584]{2,1,0:T(8,128)(2,1)} %refs_0_.10, ...), custom_call_target="tpu_custom_call" | custom-call | flops 22548578304 | bytes 47710208 | tf_op jit(solution)/shard_map/gate_up/pallas_call | solution.py:144
  339.2 35.2 %gate_up.7 = (f32[2048,3584]{1,0:T(8,128)}, f32[2048,3584]{1,0:T(8,128)}, bf16[2048,3584]{1,0:T(8,128)(2,1)}, bf16[1536,3584]{1,0:T(8,128)(2,1)}, bf16[1536,3584]{1,0:T(8,128)(2,1)}) custom-call(s32[5]{0:T(128)} %stack.62.at, bf16[2048,1536]{1,0:T(8,128)(2,1)} %get-tuple-element.95.a, ...), custom_call_target="tpu_custom_call", output_to_operand_aliasing={{0}: (10, {}), {1}: (11, {}), {2}: (12, {}), {3}: (13, {}),... | custom-call | flops 22548578304 | bytes 47710208 | tf_op jit(solution)/shard_map/gate_up/pallas_call | solution.py:144
  374.7 35.0 %term_columns.2 = (bf16[1536,896]{1,0:T(8,128)(2,1)}, f32[1536,896]{1,0:T(8,128)}) custom-call(bf16[1536,2048]{1,0:T(8,128)(2,1)} %shard_map.179.left, bf16[2048,3584]{1,0:T(8,128)(2,1)} %get-tuple-element.104.right), custom_call_target="tpu_custom_call" | custom-call | flops 22548578304 | bytes 31981568 | tf_op jit(solution)/shard_map/term_columns/pallas_call | solution.py:511
  410.1 44.5 %shard_map.181 = (bf16[2048,3584]{1,0:T(8,128)(2,1)}, bf16[2048,3584]{1,0:T(8,128)(2,1)}) custom-call(bf16[2048,1536]{1,0:T(8,128)(2,1)} %bitcast.28, f32[2048,3584]{1,0:T(8,128)} %get-tuple-element.107.gate, f32[2048,3584]{1,0:T(8,128)} %get-tuple-element.108.up, bf16[2,896,1536]{2,1,0:T(8,128)(2,1)} %refs_0_.11, ...), custom_call_target="tpu_custom_call" | custom-call | flops 22548578304 | bytes 88080384 | tf_op jit(solution)/shard_map/pallas_call | solution.py:257
  454.5 27.3 %term_rows.4 = (bf16[384,3584]{1,0:T(8,128)(2,1)}, bf16[384,3584]{1,0:T(8,128)(2,1)}) custom-call(bf16[1536,2048]{1,0:T(8,128)(2,1)} %get-tuple-element.111.left, bf16[2048,3584]{1,0:T(8,128)(2,1)} %get-tuple-element.138.right.dg), custom_call_target="tpu_custom_call" | custom-call | flops 16911433728 | bytes 31981568 | tf_op jit(solution)/shard_map/term_rows/pallas_call | solution.py:338
  483.6 26.8 %term_rows.5 = (bf16[384,3584]{1,0:T(8,128)(2,1)}, bf16[384,3584]{1,0:T(8,128)(2,1)}) custom-call(bf16[1536,2048]{1,0:T(8,128)(2,1)} %get-tuple-element.111.left, bf16[2048,3584]{1,0:T(8,128)(2,1)} %get-tuple-element.141.right.du), custom_call_target="tpu_custom_call" | custom-call | flops 16911433728 | bytes 31981568 | tf_op jit(solution)/shard_map/term_rows/pallas_call | solution.py:338
  510.7 55.0 %shard_map.182.by_a = bf16[2048,1536]{1,0:T(8,128)(2,1)} custom-call(bf16[2048,3584]{1,0:T(8,128)(2,1)} %get-tuple-element.138.right.dg, bf16[2048,3584]{1,0:T(8,128)(2,1)} %get-tuple-element.141.right.du, bf16[1536,3584]{1,0:T(8,128)(2,1)} %get-tuple-element.118.wg, bf16[1536,3584]{1,0:T(8,128)(2,1)} %get-tuple-element.119.wu), custom_call_target="tpu_custom_call" | custom-call | flops 45097156608 | bytes 73400320 | tf_op jit(solution)/shard_map/pallas_call | solution.py:275
  565.7 15.1 %shard_map.183 = (bf16[2048,1536]{1,0:T(8,128)(2,1)}, bf16[1536,2048]{1,0:T(8,128)(2,1)}) custom-call(bf16[2048,1536]{1,0:T(8,128)(2,1)} %shard_map.182.by_a, bf16[2048,1536]{1,0:T(8,128)(2,1)} %get-tuple-element.97.h, bf16[2048,1536]{1,0:T(8,128)(2,1)} %bitcast.29), custom_call_target="tpu_custom_call" | custom-call | flops 1000000000 | bytes 31457280 | tf_op jit(solution)/shard_map/pallas_call | solution.py:86
  580.9 34.6 %term_columns.3 = (bf16[1536,896]{1,0:T(8,128)(2,1)}, f32[1536,896]{1,0:T(8,128)}) custom-call(bf16[1536,2048]{1,0:T(8,128)(2,1)} %get-tuple-element.121.left, bf16[2048,3584]{1,0:T(8,128)(2,1)} %get-tuple-element.122.hidden.right), custom_call_target="tpu_custom_call" | custom-call | flops 22548578304 | bytes 31981568 | tf_op jit(solution)/shard_map/term_columns/pallas_call | solution.py:511
  617.2 45.0 %shard_map.184 = (bf16[2048,3584]{1,0:T(8,128)(2,1)}, bf16[2048,3584]{1,0:T(8,128)(2,1)}) custom-call(bf16[2048,1536]{1,0:T(8,128)(2,1)} %get-tuple-element.124.dy, bf16[3584,1536]{1,0:T(8,128)(2,1)} %get-tuple-element.125.w, f32[2048,3584]{1,0:T(8,128)} %get-tuple-element.126.gate, f32[2048,3584]{1,0:T(8,128)} %get-tuple-element.127.up), custom_call_target="tpu_custom_call" | custom-call | flops 22548578304 | bytes 88080384 | tf_op jit(solution)/shard_map/pallas_call | solution.py:229
  662.2 27.3 %term_rows.6 = (bf16[384,3584]{1,0:T(8,128)(2,1)}, bf16[384,3584]{1,0:T(8,128)(2,1)}) custom-call(bf16[1536,2048]{1,0:T(8,128)(2,1)} %get-tuple-element.87.left, bf16[2048,3584]{1,0:T(8,128)(2,1)} %get-tuple-element.148.right), custom_call_target="tpu_custom_call" | custom-call | flops 16911433728 | bytes 31981568 | tf_op jit(solution)/shard_map/term_rows/pallas_call | solution.py:338
  690.0 26.8 %term_rows.7 = (bf16[384,3584]{1,0:T(8,128)(2,1)}, bf16[384,3584]{1,0:T(8,128)(2,1)}) custom-call(bf16[1536,2048]{1,0:T(8,128)(2,1)} %get-tuple-element.87.left, bf16[2048,3584]{1,0:T(8,128)(2,1)} %get-tuple-element.136.right), custom_call_target="tpu_custom_call" | custom-call | flops 16911433728 | bytes 31981568 | tf_op jit(solution)/shard_map/term_rows/pallas_call | solution.py:338
  746.2 14.1 %shard_map.187 = (bf16[384,3584]{1,0:T(8,128)(2,1)}, f32[1,1]{1,0:T(1,128)}) custom-call(s32[5]{0:T(128)} %stack.60.at, bf16[1536,2048]{1,0:T(8,128)(2,1)} %get-tuple-element.111.left, bf16[2048,3584]{1,0:T(8,128)(2,1)} %get-tuple-element.141.right.du, bf16[384,3584]{1,0:T(8,128)(2,1)} %get-tuple-element.142.kept, ...), custom_call_target="tpu_custom_call" | custom-call | flops 5637144576 | bytes 14680064 | tf_op jit(solution)/shard_map/pallas_call | solution.py:383
  793.5 17.3 %collective-permute-done.32.arrived = bf16[384,3584]{1,0:T(8,128)(2,1)} collective-permute-done((bf16[384,3584]{1,0:T(8,128)(2,1)}, bf16[384,3584]{1,0:T(8,128)(2,1)}, u32[]{:S(2)}, u32[]{:S(2)}) %collective-permute-start.32) | collective-permute-done | bytes 2752544 | tf_op jit(solution)/shard_map/ppermute | solution.py:618
  821.4 22.8 %fusion.8 = (bf16[2,896,1536]{2,1,0:T(8,128)(2,1)}, f32[2,896,1536]{2,1,0:T(8,128)}, f32[2,896,1536]{2,1,0:T(8,128)}) fusion(bf16[2,896,1536]{2,1,0:T(8,128)(2,1)} %refs_0_.11, f32[]{:T(128)} %bitcast.16, bf16[1,896,1536]{2,1,0:T(8,128)(2,1)} %bitcast.36, bf16[1,896,1536]{2,1,0:T(8,128)(2,1)} %bitcast.37, f32[2,896,1536]{2,1,0:T(8,128)} %param.21, ...), kind=kLoop, calls=%fused_computation.17 | loop fusion | flops 55050240 | bytes 60555268 | tf_op jit(solution)/shard_map/convert_element_type | solution.py:27
  844.3 37.6 %fusion.2 = (bf16[2,384,3584]{2,1,0:T(8,128)(2,1)}, f32[2,384,3584]{2,1,0:T(8,128)}, f32[2,384,3584]{2,1,0:T(8,128)}, bf16[2,384,3584]{2,1,0:T(8,128)(2,1)}, f32...) fusion(bf16[2,384,3584]{2,1,0:T(8,128)(2,1)} %refs_0_.10, f32[]{:T(128)} %bitcast.16, ...), kind=kLoop, calls=%fused_computation.11 | loop fusion | flops 110100480 | bytes 121110528 | tf_op jit(solution)/shard_map/convert_element_type | solution.py:27
  (76 shorter events, 130.1 us)
Async XLA Ops:
  0.6 129.3 %collective-permute-start.1 = (bf16[2,384,3584]{2,1,0:T(8,128)(2,1)}, bf16[2,384,3584]{2,1,0:T(8,128)(2,1)}, u32[]{:S(2)}, u32[]{:S(2)}) collective-permute-start(bf16[2,384,3584]{2,1,0:T(8,128)(2,1)} %refs_0_.10), channel_id=1, source_target_pairs={{0,1},{1,0},{2,3},{3,2},{4,5},{5,4},{6,7},{7,6}} | collective-permute-start | bytes 16515080 | tf_op jit(solution)/shard_map/ppermute | solution.py:554
  1.5 128.9 %collective-permute-start.4 = (bf16[2,384,3584]{2,1,0:T(8,128)(2,1)}, bf16[2,384,3584]{2,1,0:T(8,128)(2,1)}, u32[]{:S(2)}, u32[]{:S(2)}) collective-permute-start(bf16[2,384,3584]{2,1,0:T(8,128)(2,1)} %refs_4_.7), channel_id=1, source_target_pairs={{0,1},{1,0},{2,3},{3,2},{4,5},{5,4},{6,7},{7,6}} | collective-permute-start | bytes 16515080 | tf_op jit(solution)/shard_map/ppermute | solution.py:554
  10.5 57.0 %collective-permute-start.5 = (bf16[384,1792]{1,0:T(8,128)(2,1)S(1)}, bf16[384,1792]{1,0:T(8,128)(2,1)}, u32[]{:S(2)}, u32[]{:S(2)}) collective-permute-start(bf16[384,1792]{1,0:T(8,128)(2,1)S(1)} %get-tuple-element.171), channel_id=1, source_target_pairs={{0,2},{2,0},{1,3},{3,1},{4,6},{6,4},{5,7},{7,5}} | collective-permute-start | bytes 4128776 | tf_op jit(solution)/shard_map/ppermute | solution.py:562
  69.2 60.7 %collective-permute-start.6 = (bf16[384,1792]{1,0:T(8,128)(2,1)}, bf16[384,1792]{1,0:T(8,128)(2,1)}, u32[]{:S(2)}, u32[]{:S(2)}) collective-permute-start(bf16[384,1792]{1,0:T(8,128)(2,1)} %collective-permute-done.5.refs_6_), channel_id=1, source_target_pairs={{0,4},{4,0},{1,5},{5,1},{2,6},{6,2},{3,7},{7,3}} | collective-permute-start | bytes 4128776 | tf_op jit(solution)/shard_map/ppermute | solution.py:576
  92.4 142.3 %collective-permute-start.10 = (bf16[2,896,1536]{2,1,0:T(8,128)(2,1)}, bf16[2,896,1536]{2,1,0:T(8,128)(2,1)}, u32[]{:S(2)}, u32[]{:S(2)}) collective-permute-start(bf16[2,896,1536]{2,1,0:T(8,128)(2,1)} %refs_0_.11), channel_id=1, source_target_pairs={{0,1},{1,0},{2,3},{3,2},{4,5},{5,4},{6,7},{7,6}} | collective-permute-start | bytes 16515080 | tf_op jit(solution)/shard_map/ppermute | solution.py:554
  100.8 63.8 %collective-permute-start.11 = (bf16[448,1536]{1,0:T(8,128)(2,1)}, bf16[448,1536]{1,0:T(8,128)(2,1)}, u32[]{:S(2)}, u32[]{:S(2)}) collective-permute-start(bf16[448,1536]{1,0:T(8,128)(2,1)} %get-tuple-element.169), channel_id=1, source_target_pairs={{0,2},{2,0},{1,3},{3,1},{4,6},{6,4},{5,7},{7,5}} | collective-permute-start | bytes 4128776 | tf_op jit(solution)/shard_map/ppermute | solution.py:562
  129.9 38.7 %collective-permute-start.3 = (bf16[384,1792]{1,0:T(8,128)(2,1)}, bf16[384,1792]{1,0:T(8,128)(2,1)}, u32[]{:S(2)}, u32[]{:S(2)}) collective-permute-start(bf16[384,1792]{1,0:T(8,128)(2,1)} %collective-permute-done.2.refs_2_), channel_id=1, source_target_pairs={{0,1},{1,0},{2,3},{3,2},{4,5},{5,4},{6,7},{7,6}} | collective-permute-start | bytes 4128776 | tf_op jit(solution)/shard_map/ppermute | solution.py:577
  129.9 39.2 %collective-permute-start.7 = (bf16[384,1792]{1,0:T(8,128)(2,1)}, bf16[384,1792]{1,0:T(8,128)(2,1)}, u32[]{:S(2)}, u32[]{:S(2)}) collective-permute-start(bf16[384,1792]{1,0:T(8,128)(2,1)} %collective-permute-done.6.refs_6_), channel_id=1, source_target_pairs={{0,1},{1,0},{2,3},{3,2},{4,5},{5,4},{6,7},{7,6}} | collective-permute-start | bytes 4128776 | tf_op jit(solution)/shard_map/ppermute | solution.py:577
  166.4 105.4 %collective-permute-start.23 = (bf16[448,1536]{1,0:T(8,128)(2,1)}, bf16[448,1536]{1,0:T(8,128)(2,1)}, u32[]{:S(2)}, u32[]{:S(2)}) collective-permute-start(bf16[448,1536]{1,0:T(8,128)(2,1)} %get-tuple-element.168), channel_id=1, source_target_pairs={{0,2},{2,0},{1,3},{3,1},{4,6},{6,4},{5,7},{7,5}} | collective-permute-start | bytes 4128776 | tf_op jit(solution)/shard_map/ppermute | solution.py:562
  168.6 62.8 %collective-permute-start.15 = (bf16[384,1792]{1,0:T(8,128)(2,1)}, bf16[384,1792]{1,0:T(8,128)(2,1)}, u32[]{:S(2)}, u32[]{:S(2)}) collective-permute-start(bf16[384,1792]{1,0:T(8,128)(2,1)} %get-tuple-element.172), channel_id=1, source_target_pairs={{0,2},{2,0},{1,3},{3,1},{4,6},{6,4},{5,7},{7,5}} | collective-permute-start | bytes 4128776 | tf_op jit(solution)/shard_map/ppermute | solution.py:562
  169.1 64.0 %collective-permute-start.13 = (bf16[448,1536]{1,0:T(8,128)(2,1)}, bf16[448,1536]{1,0:T(8,128)(2,1)}, u32[]{:S(2)}, u32[]{:S(2)}) collective-permute-start(bf16[448,1536]{1,0:T(8,128)(2,1)} %collective-permute-done.11.refs_2_), channel_id=1, source_target_pairs={{0,1},{1,0},{2,3},{3,2},{4,5},{5,4},{6,7},{7,6}} | collective-permute-start | bytes 4128776 | tf_op jit(solution)/shard_map/ppermute | solution.py:570
  197.1 37.5 %collective-permute-start.14 = (bf16[448,1536]{1,0:T(8,128)(2,1)}, bf16[448,1536]{1,0:T(8,128)(2,1)}, u32[]{:S(2)}, u32[]{:S(2)}) collective-permute-start(bf16[448,1536]{1,0:T(8,128)(2,1)} %collective-permute-done.12.refs_3_), channel_id=1, source_target_pairs={{0,1},{1,0},{2,3},{3,2},{4,5},{5,4},{6,7},{7,6}} | collective-permute-start | bytes 4128776 | tf_op jit(solution)/shard_map/ppermute | solution.py:577
  231.4 39.4 %collective-permute-start.18 = (bf16[384,1792]{1,0:T(8,128)(2,1)}, bf16[384,1792]{1,0:T(8,128)(2,1)}, u32[]{:S(2)}, u32[]{:S(2)}) collective-permute-start(bf16[384,1792]{1,0:T(8,128)(2,1)} %get-tuple-element.170), channel_id=1, source_target_pairs={{0,2},{2,0},{1,3},{3,1},{4,6},{6,4},{5,7},{7,5}} | collective-permute-start | bytes 4128776 | tf_op jit(solution)/shard_map/ppermute | solution.py:562
  233.1 38.7 %collective-permute-start.16 = (bf16[384,1792]{1,0:T(8,128)(2,1)}, bf16[384,1792]{1,0:T(8,128)(2,1)}, u32[]{:S(2)}, u32[]{:S(2)}) collective-permute-start(bf16[384,1792]{1,0:T(8,128)(2,1)} %collective-permute-done.15.refs_2_), channel_id=1, source_target_pairs={{0,4},{4,0},{1,5},{5,1},{2,6},{6,2},{3,7},{7,3}} | collective-permute-start | bytes 4128776 | tf_op jit(solution)/shard_map/ppermute | solution.py:576
  271.8 138.2 %collective-permute-start.25 = (bf16[448,1536]{1,0:T(8,128)(2,1)}, bf16[448,1536]{1,0:T(8,128)(2,1)}, u32[]{:S(2)}, u32[]{:S(2)}) collective-permute-start(bf16[448,1536]{1,0:T(8,128)(2,1)} %collective-permute-done.23.refs_2_), channel_id=1, source_target_pairs={{0,1},{1,0},{2,3},{3,2},{4,5},{5,4},{6,7},{7,6}} | collective-permute-start | bytes 4128776 | tf_op jit(solution)/shard_map/ppermute | solution.py:570
  271.9 67.3 %collective-permute-start.17 = (bf16[384,1792]{1,0:T(8,128)(2,1)}, bf16[384,1792]{1,0:T(8,128)(2,1)}, u32[]{:S(2)}, u32[]{:S(2)}) collective-permute-start(bf16[384,1792]{1,0:T(8,128)(2,1)} %collective-permute-done.16.refs_2_), channel_id=1, source_target_pairs={{0,1},{1,0},{2,3},{3,2},{4,5},{5,4},{6,7},{7,6}} | collective-permute-start | bytes 4128776 | tf_op jit(solution)/shard_map/ppermute | solution.py:577
  303.2 36.0 %collective-permute-start.20 = (bf16[384,1792]{1,0:T(8,128)(2,1)}, bf16[384,1792]{1,0:T(8,128)(2,1)}, u32[]{:S(2)}, u32[]{:S(2)}) collective-permute-start(bf16[384,1792]{1,0:T(8,128)(2,1)} %collective-permute-done.19.refs_6_), channel_id=1, source_target_pairs={{0,1},{1,0},{2,3},{3,2},{4,5},{5,4},{6,7},{7,6}} | collective-permute-start | bytes 4128776 | tf_op jit(solution)/shard_map/ppermute | solution.py:577
  338.6 35.8 %collective-permute-start.24 = (bf16[448,1536]{1,0:T(8,128)(2,1)}, bf16[448,1536]{1,0:T(8,128)(2,1)}, u32[]{:S(2)}, u32[]{:S(2)}) collective-permute-start(bf16[448,1536]{1,0:T(8,128)(2,1)} %collective-permute-done.23.refs_2_), channel_id=1, source_target_pairs={{0,4},{4,0},{1,5},{5,1},{2,6},{6,2},{3,7},{7,3}} | collective-permute-start | bytes 4128776 | tf_op jit(solution)/shard_map/ppermute | solution.py:576
  409.7 350.6 %collective-permute-start.29 = (bf16[1536,896]{1,0:T(8,128)(2,1)}, bf16[1536,896]{1,0:T(8,128)(2,1)}, u32[]{:S(2)}, u32[]{:S(2)}) collective-permute-start(bf16[1536,896]{1,0:T(8,128)(2,1)} %get-tuple-element.105), channel_id=1, source_target_pairs={{0,2},{2,0},{1,3},{3,1},{4,6},{6,4},{5,7},{7,5}} | collective-permute-start | bytes 8257544 | tf_op jit(solution)/shard_map/ppermute | solution.py:618
  481.8 235.0 %collective-permute-start.27 = (bf16[384,3584]{1,0:T(8,128)(2,1)}, bf16[384,3584]{1,0:T(8,128)(2,1)}, u32[]{:S(2)}, u32[]{:S(2)}) collective-permute-start(bf16[384,3584]{1,0:T(8,128)(2,1)} %get-tuple-element.114), channel_id=1, source_target_pairs={{0,2},{2,0},{1,3},{3,1},{4,6},{6,4},{5,7},{7,5}} | collective-permute-start | bytes 8257544 | tf_op jit(solution)/shard_map/ppermute | solution.py:618
  510.3 235.9 %collective-permute-start.28 = (bf16[384,3584]{1,0:T(8,128)(2,1)}, bf16[384,3584]{1,0:T(8,128)(2,1)}, u32[]{:S(2)}, u32[]{:S(2)}) collective-permute-start(bf16[384,3584]{1,0:T(8,128)(2,1)} %get-tuple-element.116), channel_id=1, source_target_pairs={{0,2},{2,0},{1,3},{3,1},{4,6},{6,4},{5,7},{7,5}} | collective-permute-start | bytes 8257544 | tf_op jit(solution)/shard_map/ppermute | solution.py:618
  615.5 152.8 %collective-permute-start.30 = (bf16[1536,896]{1,0:T(8,128)(2,1)}, bf16[1536,896]{1,0:T(8,128)(2,1)}, u32[]{:S(2)}, u32[]{:S(2)}) collective-permute-start(bf16[1536,896]{1,0:T(8,128)(2,1)} %get-tuple-element.123), channel_id=1, source_target_pairs={{0,2},{2,0},{1,3},{3,1},{4,6},{6,4},{5,7},{7,5}} | collective-permute-start | bytes 8257544 | tf_op jit(solution)/shard_map/ppermute | solution.py:618
  689.5 86.6 %collective-permute-start.31 = (bf16[384,3584]{1,0:T(8,128)(2,1)}, bf16[384,3584]{1,0:T(8,128)(2,1)}, u32[]{:S(2)}, u32[]{:S(2)}) collective-permute-start(bf16[384,3584]{1,0:T(8,128)(2,1)} %get-tuple-element.133), channel_id=1, source_target_pairs={{0,2},{2,0},{1,3},{3,1},{4,6},{6,4},{5,7},{7,5}} | collective-permute-start | bytes 8257544 | tf_op jit(solution)/shard_map/ppermute | solution.py:618
  716.8 94.0 %collective-permute-start.32 = (bf16[384,3584]{1,0:T(8,128)(2,1)}, bf16[384,3584]{1,0:T(8,128)(2,1)}, u32[]{:S(2)}, u32[]{:S(2)}) collective-permute-start(bf16[384,3584]{1,0:T(8,128)(2,1)} %get-tuple-element.135), channel_id=1, source_target_pairs={{0,2},{2,0},{1,3},{3,1},{4,6},{6,4},{5,7},{7,5}} | collective-permute-start | bytes 8257544 | tf_op jit(solution)/shard_map/ppermute | solution.py:618
  (10 other events, 310.0 us)

commit v5 on v4

--- a/solution.py
+++ b/solution.py
@@ -33,6 +33,7 @@
 
 
 VMEM = 63 << 20
+FREE = 0
 
 
 def call(kernel, out_shape, grid, in_specs, out_specs, flops, moved, prefetch=None, scratch=()):
@@ -48,7 +49,7 @@
         out_shape=out_shape,
         grid_spec=gs,
         compiler_params=pltpu.CompilerParams(vmem_limit_bytes=VMEM),
-        cost_estimate=pl.CostEstimate(flops=flops, bytes_accessed=moved, transcendentals=0),
+        cost_estimate=pl.CostEstimate(flops=flops, bytes_accessed=moved, transcendentals=FREE),
     )
 
 
@@ -80,7 +81,7 @@
     out_t[...] = turned_of(new)
 
 
-def by_rows(kernel, kinds, *arrays, bm=256):
+def by_rows(kernel, kinds, *arrays, bm=512):
     m, n = arrays[0].shape
     straight, across = pl.BlockSpec((bm, n), lambda i: (i, 0)), pl.BlockSpec((n, bm), lambda i: (0, i))
     return call(
@@ -89,8 +90,10 @@
     )(*arrays)
 
 
-def gate_up_kernel(number, width, outputs, at, a, *refs):
-    sources, outs, (buf, sem) = (refs[:4], refs[4:8]), refs[-2 - outputs : -2], refs[-2:]
+def gate_up_kernel(number, width, outputs, at, a_far, *refs):
+    sources, outs, (buf, sem) = (refs[:4], refs[4:8]), refs[-4 - outputs : -4], refs[-4:-2]
+    a, a_sem = refs[-2:]
+    a_copy = pltpu.make_async_copy(a_far, a, a_sem)
     by_gate, by_up, hidden = outs[:3]
     t = pl.program_id(0)
     tile = hidden.shape[1]
@@ -111,6 +114,7 @@
 
     @pl.when(t == 0)
     def _():
+        a_copy.start()
         for one in copies(t):
             one.start()
 
@@ -118,6 +122,10 @@
     def _():
         for one in copies(t + 1):
             one.start()
+
+    @pl.when(t == 0)
+    def _():
+        a_copy.wait()
 
     for one in copies(t):
         one.wait()
@@ -147,13 +155,18 @@
         grid_spec=pltpu.PrefetchScalarGridSpec(
             num_scalar_prefetch=1,
             grid=(tiles,),
-            in_specs=[resident((m, k))] + [any_space] * (8 + len(before)),
+            in_specs=[any_space] * (9 + len(before)),
             out_specs=[out] * 3 + [w] * (2 if number else 0),
-            scratch_shapes=[pltpu.VMEM((2, 2, k, bn), BF16), pltpu.SemaphoreType.DMA((2, 2, 4))],
+            scratch_shapes=[
+                pltpu.VMEM((2, 2, k, bn), BF16),
+                pltpu.SemaphoreType.DMA((2, 2, 4)),
+                pltpu.VMEM((m, k), BF16),
+                pltpu.SemaphoreType.DMA,
+            ],
         ),
         input_output_aliases={10 + i: i for i in range(len(before))},
         compiler_params=pltpu.CompilerParams(vmem_limit_bytes=VMEM),
-        cost_estimate=pl.CostEstimate(flops=4 * m * width * k, bytes_accessed=10 * m * width + 4 * k * width, transcendentals=0),
+        cost_estimate=pl.CostEstimate(flops=4 * m * width * k, bytes_accessed=10 * m * width + 4 * k * width, transcendentals=FREE),
         name="gate_up",
     )(at, a, *gates, *ups, *before)
 
@@ -200,7 +213,7 @@
         put.wait()
 
 
-def down(number, hidden, x, pieces, bm=256):
+def down(number, hidden, x, pieces, bm=512):
     m, k = hidden.shape
     n, rows = pieces[0].shape[2], pieces[0].shape[1]
     out = pl.BlockSpec((bm, n), lambda i: (i, 0))
@@ -348,8 +361,8 @@
             pltpu.SemaphoreType.DMA((2, tiles)),
             pltpu.SemaphoreType.DMA((2, tiles)),
         ],
-        compiler_params=pltpu.CompilerParams(vmem_limit_bytes=VMEM, collective_id=0, has_side_effects=True),
-        cost_estimate=pl.CostEstimate(flops=3 * m * n * k // 2, bytes_accessed=2 * (m * k + k * n + m * n), transcendentals=0),
+        compiler_params=pltpu.CompilerParams(vmem_limit_bytes=VMEM, collective_id=FREE, has_side_effects=True),
+        cost_estimate=pl.CostEstimate(flops=3 * m * n * k // 2, bytes_accessed=2 * (m * k + k * n + m * n), transcendentals=FREE),
         name="term_rows",
     )(left, right)
 
@@ -422,24 +435,27 @@
         factor[...] = jnp.minimum(1.0, 0.5 * lax.rsqrt(squares / elements + 1e-30))
 
 
+ENDED = 896
+
+
 def ended(own, arrived, before, elements):
     m, n = own.shape
-    spec = pl.BlockSpec((m, TILE), lambda j: (0, j))
+    spec = pl.BlockSpec((m, ENDED), lambda j: (0, j))
     return pl.pallas_call(
         functools.partial(ended_kernel, elements),
         out_shape=[shaped((m, n)), shaped((8, 128), F32)],
-        grid=(n // TILE,),
+        grid=(n // ENDED,),
         in_specs=[spec, spec, pl.BlockSpec(memory_space=pltpu.SMEM)],
         out_specs=[spec, pl.BlockSpec((8, 128), lambda j: (0, 0))],
         scratch_shapes=[
-            pltpu.VMEM((8, TILE), F32),
+            pltpu.VMEM((8, ENDED), F32),
             pltpu.VMEM((8, 128), F32),
             pltpu.VMEM((3, 8, 128), F32),
             pltpu.SemaphoreType.DMA((3,)),
             pltpu.SemaphoreType.DMA((3,)),
         ],
         compiler_params=pltpu.CompilerParams(vmem_limit_bytes=VMEM, collective_id=2, has_side_effects=True),
-        cost_estimate=pl.CostEstimate(flops=4 * m * n, bytes_accessed=8 * m * n, transcendentals=0),
+        cost_estimate=pl.CostEstimate(flops=4 * m * n, bytes_accessed=8 * m * n, transcendentals=FREE),
         name="ended",
     )(own, arrived, before)
 
@@ -516,7 +532,7 @@
         out_specs=[pl.BlockSpec((m, wide), lambda j: (0, 0))] * 2,
         scratch_shapes=[pltpu.VMEM((m, n), BF16), pltpu.VMEM((2, m, wide), BF16), pltpu.SemaphoreType.DMA((4, 2)), pltpu.SemaphoreType.DMA((4, 2))],
         compiler_params=pltpu.CompilerParams(vmem_limit_bytes=VMEM, collective_id=1, has_side_effects=True),
-        cost_estimate=pl.CostEstimate(flops=2 * m * n * k, bytes_accessed=2 * (m * k + k * n + m * n), transcendentals=0),
+        cost_estimate=pl.CostEstimate(flops=2 * m * n * k, bytes_accessed=2 * (m * k + k * n + m * n), transcendentals=FREE),
         name="term_columns",
     )(left, right)
 
@@ -538,7 +554,7 @@
         in_specs=[spec, spec],
         out_specs=[pl.BlockSpec((bn, m), lambda j: (j, 0)), pl.BlockSpec(memory_space=pltpu.SMEM)],
         compiler_params=pltpu.CompilerParams(vmem_limit_bytes=VMEM),
-        cost_estimate=pl.CostEstimate(flops=4 * m * n, bytes_accessed=8 * m * n, transcendentals=0),
+        cost_estimate=pl.CostEstimate(flops=4 * m * n, bytes_accessed=8 * m * n, transcendentals=FREE),
         name="turned",
     )(own, arrived)
     return g, squares

time: 893 us -> 885 us (level)
  Pallas kernels: 613 us -> 604 us
where the time goes in v5:
time: 885 us; the launch traced here: 877 us
  Pallas kernels  604 us (68%)
  waiting for transfers between devices  172 us (19%)
  other arithmetic  60.4 us (7%)
  starting transfers between devices  23.7 us (3%)
  local copies, waits for them, and re-layouts  11.9 us (1%)
    pallas_call x4, Pallas kernels, gate_up(): pl.pallas_call(functools.partial(gate_up_kernel, number, width, 5 if numb...  137 us
    pallas_call x4, Pallas kernels, term_rows(): pl.pallas_call(term_rows_kernel, out_shape=[shaped((rows, n)), shaped((ro...  108 us
    ppermute x6, waiting for transfers between devices, second(): ry = lax.ppermute(rx, 'rep', OVER_Y)  98 us
    pallas_call x2, Pallas kernels, term_columns(): pl.pallas_call(term_columns_kernel, out_shape=[shaped((m, wide)), shaped(...  69.6 us
    convert_element_type x2, other arithmetic, adamw(): return ((w - 0.02 * step).astype(BF16), m, v)  60.4 us
    ppermute x6, waiting for transfers between devices, across(): return lax.ppermute(mine, 'dp', OVER_X)  57 us
    pallas_call x1, Pallas kernels, by_a(): call(by_a_kernel, shaped((m, n)), (m // bm, n // bn), [lhs, lhs, w, w], p...  55 us
    pallas_call x1, Pallas kernels, by_hidden(): call(by_hidden_kernel, [shaped((m, n))] * 2, (n // bn,), [resident((m, k)...  45 us
  transfers between devices with their start and end apart: 33, of which 7 were waited for; matrix products, arithmetic and copies ran while one was open for 1% of the time, Pallas kernels for 68%

profile of v5, /device:TPU:0, one launch (start us, length us, event | category | flops | bytes accessed | tf_op | source)
XLA Modules:
  0.0 877.0 jit_solution(14958262923556385795)
XLA Ops:
  10.5 28.1 %collective-permute-done.refs_2_ = bf16[384,1792]{1,0:T(8,128)(2,1)} collective-permute-done((bf16[384,1792]{1,0:T(8,128)(2,1)S(1)}, bf16[384,1792]{1,0:T(8,128)(2,1)}, u32[]{:S(2)}, u32[]{:S(2)}) %collective-permute-start) | collective-permute-done | bytes 1376288 | tf_op jit(solution)/shard_map/ppermute | solution.py:578
  38.6 28.8 %collective-permute-done.5.refs_6_ = bf16[384,1792]{1,0:T(8,128)(2,1)} collective-permute-done((bf16[384,1792]{1,0:T(8,128)(2,1)S(1)}, bf16[384,1792]{1,0:T(8,128)(2,1)}, u32[]{:S(2)}, u32[]{:S(2)}) %collective-permute-start.5) | collective-permute-done | bytes 1376288 | tf_op jit(solution)/shard_map/ppermute | solution.py:578
  102.6 27.3 %collective-permute-done.6.refs_6_ = bf16[384,1792]{1,0:T(8,128)(2,1)} collective-permute-done((bf16[384,1792]{1,0:T(8,128)(2,1)}, bf16[384,1792]{1,0:T(8,128)(2,1)}, u32[]{:S(2)}, u32[]{:S(2)}) %collective-permute-start.6) | collective-permute-done | bytes 1376288 | tf_op jit(solution)/shard_map/ppermute | solution.py:592
  130.4 33.8 %gate_up.4 = (f32[2048,3584]{1,0:T(8,128)}, f32[2048,3584]{1,0:T(8,128)}, bf16[2048,3584]{1,0:T(8,128)(2,1)}) custom-call(s32[5]{0:T(128)} %stack.60.at, bf16[2048,1536]{1,0:T(8,128)(2,1)} %get-tuple-element.89.a_far, bf16[2,384,3584]{2,1,0:T(8,128)(2,1)} %refs_0_.10, bf16[2,384,3584]{2,1,0:T(8,128)(2,1)} %collective-permute-done.1.refs_1_, ...), custom_call_target="tpu_custom_call" | custom-call | flops 22548578304 | bytes 47710208 | tf_op jit(solution)/shard_map/gate_up/pallas_call | solution.py:152
  168.6 28.0 %collective-permute-done.12.refs_3_ = bf16[448,1536]{1,0:T(8,128)(2,1)} collective-permute-done((bf16[448,1536]{1,0:T(8,128)(2,1)}, bf16[448,1536]{1,0:T(8,128)(2,1)}, u32[]{:S(2)}, u32[]{:S(2)}) %collective-permute-start.12) | collective-permute-done | bytes 1376288 | tf_op jit(solution)/shard_map/ppermute | solution.py:592
  196.6 33.8 %gate_up.5 = (f32[2048,3584]{1,0:T(8,128)}, f32[2048,3584]{1,0:T(8,128)}, bf16[2048,3584]{1,0:T(8,128)(2,1)}) custom-call(s32[5]{0:T(128)} %stack.62.at, bf16[2048,1536]{1,0:T(8,128)(2,1)} %get-tuple-element.89.a_far, bf16[2,384,3584]{2,1,0:T(8,128)(2,1)} %refs_0_.10, ...), custom_call_target="tpu_custom_call", output_to_operand_aliasing={{0}: (10, {}), {1}: (11, {}), {2}: (12, {})} | custom-call | flops 22548578304 | bytes 47710208 | tf_op jit(solution)/shard_map/gate_up/pallas_call | solution.py:152
  233.7 35.9 %shard_map.180 = (bf16[2048,1536]{1,0:T(8,128)(2,1)}, bf16[2048,1536]{1,0:T(8,128)(2,1)}, bf16[1536,2048]{1,0:T(8,128)(2,1)}, bf16[3584,1536]{1,0:T(8,128)(2,1)}) custom-call(bf16[2048,3584]{1,0:T(8,128)(2,1)} %get-tuple-element.122.hidden.right, bf16[2048,1536]{1,0:T(8,128)(2,1)} %bitcast.31, bf16[2,896,1536]{2,1,0:T(8,128)(2,1)} %refs_0_.11, ...), custom_call_target="tpu_custom_call" | custom-call | flops 22548578304 | bytes 36700160 | tf_op jit(solution)/shard_map/pallas_call | solution.py:221
  271.2 30.8 %collective-permute-done.19.refs_6_ = bf16[384,1792]{1,0:T(8,128)(2,1)} collective-permute-done((bf16[384,1792]{1,0:T(8,128)(2,1)}, bf16[384,1792]{1,0:T(8,128)(2,1)}, u32[]{:S(2)}, u32[]{:S(2)}) %collective-permute-start.19) | collective-permute-done | bytes 1376288 | tf_op jit(solution)/shard_map/ppermute | solution.py:592
  302.0 34.7 %gate_up.6 = (f32[2048,3584]{1,0:T(8,128)}, f32[2048,3584]{1,0:T(8,128)}, bf16[2048,3584]{1,0:T(8,128)(2,1)}, bf16[1536,3584]{1,0:T(8,128)(2,1)}, bf16[1536,3584]{1,0:T(8,128)(2,1)}) custom-call(s32[5]{0:T(128)} %stack.60.at, bf16[2048,1536]{1,0:T(8,128)(2,1)} %get-tuple-element.95.a_far, bf16[2,384,3584]{2,1,0:T(8,128)(2,1)} %refs_0_.10, ...), custom_call_target="tpu_custom_call" | custom-call | flops 22548578304 | bytes 47710208 | tf_op jit(solution)/shard_map/gate_up/pallas_call | solution.py:152
  337.2 34.6 %gate_up.7 = (f32[2048,3584]{1,0:T(8,128)}, f32[2048,3584]{1,0:T(8,128)}, bf16[2048,3584]{1,0:T(8,128)(2,1)}, bf16[1536,3584]{1,0:T(8,128)(2,1)}, bf16[1536,3584]{1,0:T(8,128)(2,1)}) custom-call(s32[5]{0:T(128)} %stack.62.at, ...), custom_call_target="tpu_custom_call", output_to_operand_aliasing={{0}: (10, {}), {1}: (11, {}), {2}: (12, {}), {3}: (13, {}),... | custom-call | flops 22548578304 | bytes 47710208 | tf_op jit(solution)/shard_map/gate_up/pallas_call | solution.py:152
  372.1 35.0 %term_columns.2 = (bf16[1536,896]{1,0:T(8,128)(2,1)}, f32[1536,896]{1,0:T(8,128)}) custom-call(bf16[1536,2048]{1,0:T(8,128)(2,1)} %shard_map.179.left, bf16[2048,3584]{1,0:T(8,128)(2,1)} %get-tuple-element.104.right), custom_call_target="tpu_custom_call" | custom-call | flops 22548578304 | bytes 31981568 | tf_op jit(solution)/shard_map/term_columns/pallas_call | solution.py:527
  407.5 44.5 %shard_map.181 = (bf16[2048,3584]{1,0:T(8,128)(2,1)}, bf16[2048,3584]{1,0:T(8,128)(2,1)}) custom-call(bf16[2048,1536]{1,0:T(8,128)(2,1)} %bitcast.28, f32[2048,3584]{1,0:T(8,128)} %get-tuple-element.107.gate, f32[2048,3584]{1,0:T(8,128)} %get-tuple-element.108.up, bf16[2,896,1536]{2,1,0:T(8,128)(2,1)} %refs_0_.11, ...), custom_call_target="tpu_custom_call" | custom-call | flops 22548578304 | bytes 88080384 | tf_op jit(solution)/shard_map/pallas_call | solution.py:270
  452.0 27.3 %term_rows.4 = (bf16[384,3584]{1,0:T(8,128)(2,1)}, bf16[384,3584]{1,0:T(8,128)(2,1)}) custom-call(bf16[1536,2048]{1,0:T(8,128)(2,1)} %get-tuple-element.111.left, bf16[2048,3584]{1,0:T(8,128)(2,1)} %get-tuple-element.138.right.dg), custom_call_target="tpu_custom_call" | custom-call | flops 16911433728 | bytes 31981568 | tf_op jit(solution)/shard_map/term_rows/pallas_call | solution.py:351
  481.0 26.8 %term_rows.5 = (bf16[384,3584]{1,0:T(8,128)(2,1)}, bf16[384,3584]{1,0:T(8,128)(2,1)}) custom-call(bf16[1536,2048]{1,0:T(8,128)(2,1)} %get-tuple-element.111.left, bf16[2048,3584]{1,0:T(8,128)(2,1)} %get-tuple-element.141.right.du), custom_call_target="tpu_custom_call" | custom-call | flops 16911433728 | bytes 31981568 | tf_op jit(solution)/shard_map/term_rows/pallas_call | solution.py:351
  508.1 55.0 %shard_map.182.by_a = bf16[2048,1536]{1,0:T(8,128)(2,1)} custom-call(bf16[2048,3584]{1,0:T(8,128)(2,1)} %get-tuple-element.138.right.dg, bf16[2048,3584]{1,0:T(8,128)(2,1)} %get-tuple-element.141.right.du, bf16[1536,3584]{1,0:T(8,128)(2,1)} %get-tuple-element.118.wg, bf16[1536,3584]{1,0:T(8,128)(2,1)} %get-tuple-element.119.wu), custom_call_target="tpu_custom_call" | custom-call | flops 45097156608 | bytes 73400320 | tf_op jit(solution)/shard_map/pallas_call | solution.py:288
  576.9 34.6 %term_columns.3 = (bf16[1536,896]{1,0:T(8,128)(2,1)}, f32[1536,896]{1,0:T(8,128)}) custom-call(bf16[1536,2048]{1,0:T(8,128)(2,1)} %get-tuple-element.121.left, bf16[2048,3584]{1,0:T(8,128)(2,1)} %get-tuple-element.122.hidden.right), custom_call_target="tpu_custom_call" | custom-call | flops 22548578304 | bytes 31981568 | tf_op jit(solution)/shard_map/term_columns/pallas_call | solution.py:527
  613.3 45.0 %shard_map.184 = (bf16[2048,3584]{1,0:T(8,128)(2,1)}, bf16[2048,3584]{1,0:T(8,128)(2,1)}) custom-call(bf16[2048,1536]{1,0:T(8,128)(2,1)} %get-tuple-element.124.dy, bf16[3584,1536]{1,0:T(8,128)(2,1)} %get-tuple-element.125.w, f32[2048,3584]{1,0:T(8,128)} %get-tuple-element.126.gate, f32[2048,3584]{1,0:T(8,128)} %get-tuple-element.127.up), custom_call_target="tpu_custom_call" | custom-call | flops 22548578304 | bytes 88080384 | tf_op jit(solution)/shard_map/pallas_call | solution.py:242
  658.3 27.3 %term_rows.6 = (bf16[384,3584]{1,0:T(8,128)(2,1)}, bf16[384,3584]{1,0:T(8,128)(2,1)}) custom-call(bf16[1536,2048]{1,0:T(8,128)(2,1)} %get-tuple-element.87.left, bf16[2048,3584]{1,0:T(8,128)(2,1)} %get-tuple-element.148.right), custom_call_target="tpu_custom_call" | custom-call | flops 16911433728 | bytes 31981568 | tf_op jit(solution)/shard_map/term_rows/pallas_call | solution.py:351
  686.0 26.8 %term_rows.7 = (bf16[384,3584]{1,0:T(8,128)(2,1)}, bf16[384,3584]{1,0:T(8,128)(2,1)}) custom-call(bf16[1536,2048]{1,0:T(8,128)(2,1)} %get-tuple-element.87.left, bf16[2048,3584]{1,0:T(8,128)(2,1)} %get-tuple-element.136.right), custom_call_target="tpu_custom_call" | custom-call | flops 16911433728 | bytes 31981568 | tf_op jit(solution)/shard_map/term_rows/pallas_call | solution.py:351
  742.3 14.1 %shard_map.187 = (bf16[384,3584]{1,0:T(8,128)(2,1)}, f32[1,1]{1,0:T(1,128)}) custom-call(s32[5]{0:T(128)} %stack.60.at, bf16[1536,2048]{1,0:T(8,128)(2,1)} %get-tuple-element.111.left, bf16[2048,3584]{1,0:T(8,128)(2,1)} %get-tuple-element.141.right.du, bf16[384,3584]{1,0:T(8,128)(2,1)} %get-tuple-element.142.kept, ...), custom_call_target="tpu_custom_call" | custom-call | flops 5637144576 | bytes 14680064 | tf_op jit(solution)/shard_map/pallas_call | solution.py:396
  772.2 14.1 %shard_map.188 = (bf16[384,3584]{1,0:T(8,128)(2,1)}, f32[1,1]{1,0:T(1,128)}) custom-call(s32[5]{0:T(128)} %stack.60.at, bf16[1536,2048]{1,0:T(8,128)(2,1)} %get-tuple-element.87.left, bf16[2048,3584]{1,0:T(8,128)(2,1)} %get-tuple-element.148.right, bf16[384,3584]{1,0:T(8,128)(2,1)} %get-tuple-element.149.kept, bf16[384,3584]{1,0:T(8,128)(2,1)} %collective-permute-done.31.arrived), custom_call_target="tpu_custom_call" | custom-call | flops 5637144576 | bytes 14680064 | tf_op jit(solution)/shard_map/pallas_call | solution.py:396
  789.6 17.3 %collective-permute-done.32.arrived = bf16[384,3584]{1,0:T(8,128)(2,1)} collective-permute-done((bf16[384,3584]{1,0:T(8,128)(2,1)}, bf16[384,3584]{1,0:T(8,128)(2,1)}, u32[]{:S(2)}, u32[]{:S(2)}) %collective-permute-start.32) | collective-permute-done | bytes 2752544 | tf_op jit(solution)/shard_map/ppermute | solution.py:634
  816.0 22.8 %fusion.8 = (bf16[2,896,1536]{2,1,0:T(8,128)(2,1)}, f32[2,896,1536]{2,1,0:T(8,128)}, f32[2,896,1536]{2,1,0:T(8,128)}) fusion(bf16[2,896,1536]{2,1,0:T(8,128)(2,1)} %refs_0_.11, f32[]{:T(128)} %bitcast.16, bf16[1,896,1536]{2,1,0:T(8,128)(2,1)} %bitcast.36, bf16[1,896,1536]{2,1,0:T(8,128)(2,1)} %bitcast.37, f32[2,896,1536]{2,1,0:T(8,128)} %param.21, ...), kind=kLoop, calls=%fused_computation.17 | loop fusion | flops 55050240 | bytes 60555268 | tf_op jit(solution)/shard_map/convert_element_type | solution.py:27
  838.9 37.6 %fusion.2 = (bf16[2,384,3584]{2,1,0:T(8,128)(2,1)}, f32[2,384,3584]{2,1,0:T(8,128)}, f32[2,384,3584]{2,1,0:T(8,128)}, bf16[2,384,3584]{2,1,0:T(8,128)(2,1)}, f32...) fusion(bf16[2,384,3584]{2,1,0:T(8,128)(2,1)} %refs_0_.10, f32[]{:T(128)} %bitcast.16, ...), kind=kLoop, calls=%fused_computation.11 | loop fusion | flops 110100480 | bytes 121110528 | tf_op jit(solution)/shard_map/convert_element_type | solution.py:27
  (76 shorter events, 128.3 us)
Async XLA Ops:
  0.6 129.3 %collective-permute-start.1 = (bf16[2,384,3584]{2,1,0:T(8,128)(2,1)}, bf16[2,384,3584]{2,1,0:T(8,128)(2,1)}, u32[]{:S(2)}, u32[]{:S(2)}) collective-permute-start(bf16[2,384,3584]{2,1,0:T(8,128)(2,1)} %refs_0_.10), channel_id=1, source_target_pairs={{0,1},{1,0},{2,3},{3,2},{4,5},{5,4},{6,7},{7,6}} | collective-permute-start | bytes 16515080 | tf_op jit(solution)/shard_map/ppermute | solution.py:570
  1.5 128.9 %collective-permute-start.4 = (bf16[2,384,3584]{2,1,0:T(8,128)(2,1)}, bf16[2,384,3584]{2,1,0:T(8,128)(2,1)}, u32[]{:S(2)}, u32[]{:S(2)}) collective-permute-start(bf16[2,384,3584]{2,1,0:T(8,128)(2,1)} %refs_4_.7), channel_id=1, source_target_pairs={{0,1},{1,0},{2,3},{3,2},{4,5},{5,4},{6,7},{7,6}} | collective-permute-start | bytes 16515080 | tf_op jit(solution)/shard_map/ppermute | solution.py:570
  10.5 57.0 %collective-permute-start.5 = (bf16[384,1792]{1,0:T(8,128)(2,1)S(1)}, bf16[384,1792]{1,0:T(8,128)(2,1)}, u32[]{:S(2)}, u32[]{:S(2)}) collective-permute-start(bf16[384,1792]{1,0:T(8,128)(2,1)S(1)} %get-tuple-element.171), channel_id=1, source_target_pairs={{0,2},{2,0},{1,3},{3,1},{4,6},{6,4},{5,7},{7,5}} | collective-permute-start | bytes 4128776 | tf_op jit(solution)/shard_map/ppermute | solution.py:578
  69.2 60.7 %collective-permute-start.6 = (bf16[384,1792]{1,0:T(8,128)(2,1)}, bf16[384,1792]{1,0:T(8,128)(2,1)}, u32[]{:S(2)}, u32[]{:S(2)}) collective-permute-start(bf16[384,1792]{1,0:T(8,128)(2,1)} %collective-permute-done.5.refs_6_), channel_id=1, source_target_pairs={{0,4},{4,0},{1,5},{5,1},{2,6},{6,2},{3,7},{7,3}} | collective-permute-start | bytes 4128776 | tf_op jit(solution)/shard_map/ppermute | solution.py:592
  89.0 144.6 %collective-permute-start.10 = (bf16[2,896,1536]{2,1,0:T(8,128)(2,1)}, bf16[2,896,1536]{2,1,0:T(8,128)(2,1)}, u32[]{:S(2)}, u32[]{:S(2)}) collective-permute-start(bf16[2,896,1536]{2,1,0:T(8,128)(2,1)} %refs_0_.11), channel_id=1, source_target_pairs={{0,1},{1,0},{2,3},{3,2},{4,5},{5,4},{6,7},{7,6}} | collective-permute-start | bytes 16515080 | tf_op jit(solution)/shard_map/ppermute | solution.py:570
  100.8 63.3 %collective-permute-start.11 = (bf16[448,1536]{1,0:T(8,128)(2,1)}, bf16[448,1536]{1,0:T(8,128)(2,1)}, u32[]{:S(2)}, u32[]{:S(2)}) collective-permute-start(bf16[448,1536]{1,0:T(8,128)(2,1)} %get-tuple-element.169), channel_id=1, source_target_pairs={{0,2},{2,0},{1,3},{3,1},{4,6},{6,4},{5,7},{7,5}} | collective-permute-start | bytes 4128776 | tf_op jit(solution)/shard_map/ppermute | solution.py:578
  129.9 38.2 %collective-permute-start.3 = (bf16[384,1792]{1,0:T(8,128)(2,1)}, bf16[384,1792]{1,0:T(8,128)(2,1)}, u32[]{:S(2)}, u32[]{:S(2)}) collective-permute-start(bf16[384,1792]{1,0:T(8,128)(2,1)} %collective-permute-done.2.refs_2_), channel_id=1, source_target_pairs={{0,1},{1,0},{2,3},{3,2},{4,5},{5,4},{6,7},{7,6}} | collective-permute-start | bytes 4128776 | tf_op jit(solution)/shard_map/ppermute | solution.py:593
  129.9 38.7 %collective-permute-start.7 = (bf16[384,1792]{1,0:T(8,128)(2,1)}, bf16[384,1792]{1,0:T(8,128)(2,1)}, u32[]{:S(2)}, u32[]{:S(2)}) collective-permute-start(bf16[384,1792]{1,0:T(8,128)(2,1)} %collective-permute-done.6.refs_6_), channel_id=1, source_target_pairs={{0,1},{1,0},{2,3},{3,2},{4,5},{5,4},{6,7},{7,6}} | collective-permute-start | bytes 4128776 | tf_op jit(solution)/shard_map/ppermute | solution.py:593
  166.0 104.7 %collective-permute-start.23 = (bf16[448,1536]{1,0:T(8,128)(2,1)}, bf16[448,1536]{1,0:T(8,128)(2,1)}, u32[]{:S(2)}, u32[]{:S(2)}) collective-permute-start(bf16[448,1536]{1,0:T(8,128)(2,1)} %get-tuple-element.168), channel_id=1, source_target_pairs={{0,2},{2,0},{1,3},{3,1},{4,6},{6,4},{5,7},{7,5}} | collective-permute-start | bytes 4128776 | tf_op jit(solution)/shard_map/ppermute | solution.py:578
  168.1 62.3 %collective-permute-start.15 = (bf16[384,1792]{1,0:T(8,128)(2,1)}, bf16[384,1792]{1,0:T(8,128)(2,1)}, u32[]{:S(2)}, u32[]{:S(2)}) collective-permute-start(bf16[384,1792]{1,0:T(8,128)(2,1)} %get-tuple-element.172), channel_id=1, source_target_pairs={{0,2},{2,0},{1,3},{3,1},{4,6},{6,4},{5,7},{7,5}} | collective-permute-start | bytes 4128776 | tf_op jit(solution)/shard_map/ppermute | solution.py:578
  168.6 63.5 %collective-permute-start.13 = (bf16[448,1536]{1,0:T(8,128)(2,1)}, bf16[448,1536]{1,0:T(8,128)(2,1)}, u32[]{:S(2)}, u32[]{:S(2)}) collective-permute-start(bf16[448,1536]{1,0:T(8,128)(2,1)} %collective-permute-done.11.refs_2_), channel_id=1, source_target_pairs={{0,1},{1,0},{2,3},{3,2},{4,5},{5,4},{6,7},{7,6}} | collective-permute-start | bytes 4128776 | tf_op jit(solution)/shard_map/ppermute | solution.py:586
  196.6 37.0 %collective-permute-start.14 = (bf16[448,1536]{1,0:T(8,128)(2,1)}, bf16[448,1536]{1,0:T(8,128)(2,1)}, u32[]{:S(2)}, u32[]{:S(2)}) collective-permute-start(bf16[448,1536]{1,0:T(8,128)(2,1)} %collective-permute-done.12.refs_3_), channel_id=1, source_target_pairs={{0,1},{1,0},{2,3},{3,2},{4,5},{5,4},{6,7},{7,6}} | collective-permute-start | bytes 4128776 | tf_op jit(solution)/shard_map/ppermute | solution.py:593
  230.4 39.2 %collective-permute-start.18 = (bf16[384,1792]{1,0:T(8,128)(2,1)}, bf16[384,1792]{1,0:T(8,128)(2,1)}, u32[]{:S(2)}, u32[]{:S(2)}) collective-permute-start(bf16[384,1792]{1,0:T(8,128)(2,1)} %get-tuple-element.170), channel_id=1, source_target_pairs={{0,2},{2,0},{1,3},{3,1},{4,6},{6,4},{5,7},{7,5}} | collective-permute-start | bytes 4128776 | tf_op jit(solution)/shard_map/ppermute | solution.py:578
  232.1 38.5 %collective-permute-start.16 = (bf16[384,1792]{1,0:T(8,128)(2,1)}, bf16[384,1792]{1,0:T(8,128)(2,1)}, u32[]{:S(2)}, u32[]{:S(2)}) collective-permute-start(bf16[384,1792]{1,0:T(8,128)(2,1)} %collective-permute-done.15.refs_2_), channel_id=1, source_target_pairs={{0,4},{4,0},{1,5},{5,1},{2,6},{6,2},{3,7},{7,3}} | collective-permute-start | bytes 4128776 | tf_op jit(solution)/shard_map/ppermute | solution.py:592
  270.7 136.8 %collective-permute-start.25 = (bf16[448,1536]{1,0:T(8,128)(2,1)}, bf16[448,1536]{1,0:T(8,128)(2,1)}, u32[]{:S(2)}, u32[]{:S(2)}) collective-permute-start(bf16[448,1536]{1,0:T(8,128)(2,1)} %collective-permute-done.23.refs_2_), channel_id=1, source_target_pairs={{0,1},{1,0},{2,3},{3,2},{4,5},{5,4},{6,7},{7,6}} | collective-permute-start | bytes 4128776 | tf_op jit(solution)/shard_map/ppermute | solution.py:586
  270.7 66.5 %collective-permute-start.17 = (bf16[384,1792]{1,0:T(8,128)(2,1)}, bf16[384,1792]{1,0:T(8,128)(2,1)}, u32[]{:S(2)}, u32[]{:S(2)}) collective-permute-start(bf16[384,1792]{1,0:T(8,128)(2,1)} %collective-permute-done.16.refs_2_), channel_id=1, source_target_pairs={{0,1},{1,0},{2,3},{3,2},{4,5},{5,4},{6,7},{7,6}} | collective-permute-start | bytes 4128776 | tf_op jit(solution)/shard_map/ppermute | solution.py:593
  302.0 35.2 %collective-permute-start.20 = (bf16[384,1792]{1,0:T(8,128)(2,1)}, bf16[384,1792]{1,0:T(8,128)(2,1)}, u32[]{:S(2)}, u32[]{:S(2)}) collective-permute-start(bf16[384,1792]{1,0:T(8,128)(2,1)} %collective-permute-done.19.refs_6_), channel_id=1, source_target_pairs={{0,1},{1,0},{2,3},{3,2},{4,5},{5,4},{6,7},{7,6}} | collective-permute-start | bytes 4128776 | tf_op jit(solution)/shard_map/ppermute | solution.py:593
  371.9 35.6 %collective-permute-start.26 = (bf16[448,1536]{1,0:T(8,128)(2,1)}, bf16[448,1536]{1,0:T(8,128)(2,1)}, u32[]{:S(2)}, u32[]{:S(2)}) collective-permute-start(bf16[448,1536]{1,0:T(8,128)(2,1)} %collective-permute-done.24.refs_3_), channel_id=1, source_target_pairs={{0,1},{1,0},{2,3},{3,2},{4,5},{5,4},{6,7},{7,6}} | collective-permute-start | bytes 4128776 | tf_op jit(solution)/shard_map/ppermute | solution.py:593
  407.1 349.3 %collective-permute-start.29 = (bf16[1536,896]{1,0:T(8,128)(2,1)}, bf16[1536,896]{1,0:T(8,128)(2,1)}, u32[]{:S(2)}, u32[]{:S(2)}) collective-permute-start(bf16[1536,896]{1,0:T(8,128)(2,1)} %get-tuple-element.105), channel_id=1, source_target_pairs={{0,2},{2,0},{1,3},{3,1},{4,6},{6,4},{5,7},{7,5}} | collective-permute-start | bytes 8257544 | tf_op jit(solution)/shard_map/ppermute | solution.py:634
  479.3 233.6 %collective-permute-start.27 = (bf16[384,3584]{1,0:T(8,128)(2,1)}, bf16[384,3584]{1,0:T(8,128)(2,1)}, u32[]{:S(2)}, u32[]{:S(2)}) collective-permute-start(bf16[384,3584]{1,0:T(8,128)(2,1)} %get-tuple-element.114), channel_id=1, source_target_pairs={{0,2},{2,0},{1,3},{3,1},{4,6},{6,4},{5,7},{7,5}} | collective-permute-start | bytes 8257544 | tf_op jit(solution)/shard_map/ppermute | solution.py:634
  507.8 234.5 %collective-permute-start.28 = (bf16[384,3584]{1,0:T(8,128)(2,1)}, bf16[384,3584]{1,0:T(8,128)(2,1)}, u32[]{:S(2)}, u32[]{:S(2)}) collective-permute-start(bf16[384,3584]{1,0:T(8,128)(2,1)} %get-tuple-element.116), channel_id=1, source_target_pairs={{0,2},{2,0},{1,3},{3,1},{4,6},{6,4},{5,7},{7,5}} | collective-permute-start | bytes 8257544 | tf_op jit(solution)/shard_map/ppermute | solution.py:634
  611.5 152.8 %collective-permute-start.30 = (bf16[1536,896]{1,0:T(8,128)(2,1)}, bf16[1536,896]{1,0:T(8,128)(2,1)}, u32[]{:S(2)}, u32[]{:S(2)}) collective-permute-start(bf16[1536,896]{1,0:T(8,128)(2,1)} %get-tuple-element.123), channel_id=1, source_target_pairs={{0,2},{2,0},{1,3},{3,1},{4,6},{6,4},{5,7},{7,5}} | collective-permute-start | bytes 8257544 | tf_op jit(solution)/shard_map/ppermute | solution.py:634
  685.6 86.6 %collective-permute-start.31 = (bf16[384,3584]{1,0:T(8,128)(2,1)}, bf16[384,3584]{1,0:T(8,128)(2,1)}, u32[]{:S(2)}, u32[]{:S(2)}) collective-permute-start(bf16[384,3584]{1,0:T(8,128)(2,1)} %get-tuple-element.133), channel_id=1, source_target_pairs={{0,2},{2,0},{1,3},{3,1},{4,6},{6,4},{5,7},{7,5}} | collective-permute-start | bytes 8257544 | tf_op jit(solution)/shard_map/ppermute | solution.py:634
  712.9 94.0 %collective-permute-start.32 = (bf16[384,3584]{1,0:T(8,128)(2,1)}, bf16[384,3584]{1,0:T(8,128)(2,1)}, u32[]{:S(2)}, u32[]{:S(2)}) collective-permute-start(bf16[384,3584]{1,0:T(8,128)(2,1)} %get-tuple-element.135), channel_id=1, source_target_pairs={{0,2},{2,0},{1,3},{3,1},{4,6},{6,4},{5,7},{7,5}} | collective-permute-start | bytes 8257544 | tf_op jit(solution)/shard_map/ppermute | solution.py:634
  (10 other events, 306.2 us)
